TPU v7x, 32 devices: a whole 2x2x4 slice. The times are simulated.
32 devices in a mesh: batch: 8 (over y, x, core), tensor: 4 (over z).
Axes of the slice: x: 2, y: 2, z: 4, core: 2. Of those that a mesh axis runs over, the one named last changes fastest.
Arguments:
- hidden_in: bfloat16 [32, 512, 768], P(('batch', 'tensor')), may hold values from -6 to 6
- segment_ids: int32 [32, 512], P('batch'), may hold values from 0 to 7, never falling along the last dimension, each value on 1 to 128 neighbouring positions
- query_weight: bfloat16 [768, 768], P(None, 'tensor'), may hold values from -0.21875 to 0.21875
- query_bias: float32 [768], P('tensor'), may hold values from -3 to 3
- key_weight: bfloat16 [768, 768], P(None, 'tensor'), may hold values from -0.21875 to 0.21875
- value_weight: bfloat16 [768, 768], P(None, 'tensor'), may hold values from -0.21875 to 0.21875
- value_bias: float32 [768], P('tensor'), may hold values from -3 to 3
- out_weight: bfloat16 [768, 768], P('tensor'), may hold values from -1.25 to 1.25
- out_bias: float32 [768], replicated, may hold values from -3 to 3
- attn_gain: float32 [768], replicated, may hold values from 0.5 to 1.5
- attn_shift: float32 [768], replicated, may hold values from -3 to 3
- up_weight: bfloat16 [768, 3072], P(None, 'tensor'), may hold values from -0.21875 to 0.21875
- up_bias: float32 [3072], P('tensor'), may hold values from -3 to 3
- down_weight: bfloat16 [3072, 768], P('tensor'), may hold values from -0.109375 to 0.109375
- down_bias: float32 [768], replicated, may hold values from -3 to 3
- ffn_gain: float32 [768], replicated, may hold values from 0.5 to 1.5
- ffn_shift: float32 [768], replicated, may hold values from -3 to 3
- cotangent: bfloat16 [32, 512, 768], P(('batch', 'tensor')), may hold values from -6 to 6
Outputs:
- layer_out: bfloat16 [32, 512, 768], P(('batch', 'tensor'))
- pooled: float32 [32, 8, 768], P(('batch', 'tensor'))
- grad_input: float32 [32, 512, 768], P(('batch', 'tensor'))
- grad_query_weight: float32 [768, 768], P(None, 'tensor')
- grad_query_bias: float32 [768], P('tensor')
- grad_key_weight: float32 [768, 768], P(None, 'tensor')
- grad_value_weight: float32 [768, 768], P(None, 'tensor')
- grad_value_bias: float32 [768], P('tensor')
- grad_out_weight: float32 [768, 768], P('tensor')
- grad_out_bias: float32 [768], P('tensor')
- grad_attn_gain: float32 [768], P('tensor')
- grad_attn_shift: float32 [768], P('tensor')
- grad_up_weight: float32 [768, 3072], P(None, 'tensor')
- grad_up_bias: float32 [3072], P('tensor')
- grad_down_weight: float32 [3072, 768], P('tensor')
- grad_down_bias: float32 [768], P('tensor')
- grad_ffn_gain: float32 [768], P('tensor')
- grad_ffn_shift: float32 [768], P('tensor')
Inputs may be any that keep to these rules, and one draw needn't show every extreme that they name: `segment_ids`: in each row the text numbers never fall, every text 0 to 7 occurs, each has 1 to 128 positions, and some text has exactly 128.
All inputs are finite; a program needn't handle non-finite values.
Results may differ from a plain program's by a relative error of at most 0.015.
Values may be sent and summed in bfloat16 or wider, within the bound.
A program may use at most 128 MiB of HBM per device.

v0:
```python
import math

import jax
import jax.numpy as jnp
from jax import lax
from jax.sharding import PartitionSpec as P

HEAD_DIM = 64
TEXTS = 8


def product(left, right):
    return jnp.dot(left, right, preferred_element_type=jnp.float32)


def through_rows(left, right):
    return lax.dot_general(
        left, right, (((0,), (0,)), ((), ())), preferred_element_type=jnp.float32
    )


def against_cols(left, right):
    return lax.dot_general(
        left, right, (((1,), (1,)), ((), ())), preferred_element_type=jnp.float32
    )


def normalize(resid, gain, shift):
    center = resid - jnp.mean(resid, axis=-1, keepdims=True)
    spread = jnp.mean(center * center, axis=-1, keepdims=True)
    return center * lax.rsqrt(spread + 1e-12) * gain + shift


def gelu_exact(value):
    return jax.nn.gelu(value, approximate=False)


def per_device(
    hidden_in,
    segment_ids,
    query_weight,
    query_bias,
    key_weight,
    value_weight,
    value_bias,
    out_weight,
    out_bias,
    attn_gain,
    attn_shift,
    up_weight,
    up_bias,
    down_weight,
    down_bias,
    ffn_gain,
    ffn_shift,
    cotangent,
):
    local_rows, length, model_width = hidden_in.shape
    inner_width = query_weight.shape[1]
    heads_here = inner_width // HEAD_DIM
    score_scale = 1.0 / math.sqrt(HEAD_DIM)
    gathered = lax.all_gather(hidden_in, "tensor", axis=0, tiled=True)
    all_rows = gathered.shape[0]
    tokens = all_rows * length
    flat_in = gathered.reshape(tokens, model_width)
    query = (product(flat_in, query_weight) + query_bias).astype(jnp.bfloat16)
    keyset = product(flat_in, key_weight).astype(jnp.bfloat16)
    valueset = (product(flat_in, value_weight) + value_bias).astype(jnp.bfloat16)

    def by_heads(tensor):
        return tensor.reshape(all_rows, length, heads_here, HEAD_DIM)

    query_heads, key_heads, value_heads = (by_heads(query), by_heads(keyset), by_heads(valueset))

    def scored(query_row, key_row, segment_row):
        scores = (
            jnp.einsum("qhd,khd->hqk", query_row, key_row, preferred_element_type=jnp.float32)
            * score_scale
        )
        same_text = segment_row[:, None] == segment_row[None, :]
        return jnp.where(same_text[None], scores, -1000000000.0)

    def attend(items):
        query_row, key_row, value_row, segment_row = items
        scores = scored(query_row, key_row, segment_row)
        row_peak = jnp.max(scores, axis=-1, keepdims=True)
        exponent = jnp.exp(scores - row_peak)
        row_total = jnp.sum(exponent, axis=-1, keepdims=True)
        probability = (exponent / row_total).astype(jnp.bfloat16)
        context_row = jnp.einsum(
            "hqk,khd->qhd", probability, value_row, preferred_element_type=jnp.float32
        )
        return (context_row.astype(jnp.bfloat16), row_peak + jnp.log(row_total))

    context, log_totals = lax.map(attend, (query_heads, key_heads, value_heads, segment_ids))
    context = context.reshape(all_rows, length, inner_width)
    input_float = hidden_in.astype(jnp.float32)
    partial_out = product(context.reshape(tokens, inner_width), out_weight).reshape(
        all_rows, length, model_width
    )
    attn = lax.psum_scatter(partial_out, "tensor", scatter_dimension=0, tiled=True)
    hidden1, norm1_pull = jax.vjp(normalize, attn + out_bias + input_float, attn_gain, attn_shift)
    hidden1_low = hidden1.astype(jnp.bfloat16)
    hidden1_all = lax.all_gather(hidden1_low, "tensor", axis=0, tiled=True).reshape(
        tokens, model_width
    )
    preact = product(hidden1_all, up_weight) + up_bias
    activated, gelu_pull = jax.vjp(gelu_exact, preact)
    activated_low = activated.astype(jnp.bfloat16)
    partial_ffn = product(activated_low, down_weight).reshape(all_rows, length, model_width)
    ffn = lax.psum_scatter(partial_ffn, "tensor", scatter_dimension=0, tiled=True)
    final, norm2_pull = jax.vjp(normalize, ffn + down_bias + hidden1, ffn_gain, ffn_shift)
    first_row = lax.axis_index("tensor") * local_rows
    segment_here = lax.dynamic_slice_in_dim(segment_ids, first_row, local_rows, 0)
    labels = jnp.arange(TEXTS, dtype=jnp.int32)
    member = (segment_here[:, None, :] == labels[None, :, None]).astype(jnp.float32)
    counts = jnp.sum(member, axis=-1)
    pooled = (
        jnp.einsum("rts,rsd->rtd", member, final, precision=lax.Precision.HIGHEST)
        / counts[:, :, None]
    )
    dresid2, ffn_gain_part, ffn_shift_part = norm2_pull(cotangent.astype(jnp.float32))
    down_bias_part = jnp.sum(dresid2, axis=(0, 1))
    dffn_low = dresid2.astype(jnp.bfloat16)
    dffn_all = lax.all_gather(dffn_low, "tensor", axis=0, tiled=True).reshape(tokens, model_width)
    grad_down = through_rows(activated_low, dffn_all)
    dactivated = against_cols(dffn_all, down_weight)
    dpreact = gelu_pull(dactivated)[0].astype(jnp.bfloat16)
    grad_up_bias = jnp.sum(dpreact.astype(jnp.float32), axis=0)
    grad_up = through_rows(hidden1_all, dpreact)
    dhidden_part = against_cols(dpreact, up_weight).reshape(all_rows, length, model_width)
    dhidden1 = lax.psum_scatter(dhidden_part, "tensor", scatter_dimension=0, tiled=True) + dresid2
    dresid1, attn_gain_part, attn_shift_part = norm1_pull(dhidden1)
    out_bias_part = jnp.sum(dresid1, axis=(0, 1))
    dattn_low = dresid1.astype(jnp.bfloat16)
    dattn_all = lax.all_gather(dattn_low, "tensor", axis=0, tiled=True).reshape(tokens, model_width)
    grad_out = through_rows(context.reshape(tokens, inner_width), dattn_all)
    dcontext = against_cols(dattn_all, out_weight).astype(jnp.bfloat16)
    dcontext_heads = by_heads(dcontext)

    def attend_back(items):
        query_row, key_row, value_row, segment_row, log_row, dctx_row = items
        scores = scored(query_row, key_row, segment_row)
        probability = jnp.exp(scores - log_row)
        dvalue_row = jnp.einsum(
            "hqk,qhd->khd",
            probability.astype(jnp.bfloat16),
            dctx_row,
            preferred_element_type=jnp.float32,
        ).astype(jnp.bfloat16)
        dprobs = jnp.einsum("qhd,khd->hqk", dctx_row, value_row, preferred_element_type=jnp.float32)
        dscores = (
            probability * (dprobs - jnp.sum(dprobs * probability, axis=-1, keepdims=True))
        ).astype(jnp.bfloat16)
        dquery_row = (
            jnp.einsum("hqk,khd->qhd", dscores, key_row, preferred_element_type=jnp.float32)
            * score_scale
        ).astype(jnp.bfloat16)
        dkey_row = (
            jnp.einsum("hqk,qhd->khd", dscores, query_row, preferred_element_type=jnp.float32)
            * score_scale
        ).astype(jnp.bfloat16)
        return (dquery_row, dkey_row, dvalue_row)

    dquery, dkey, dvalue = lax.map(
        attend_back, (query_heads, key_heads, value_heads, segment_ids, log_totals, dcontext_heads)
    )
    dquery = dquery.reshape(tokens, inner_width)
    dkey = dkey.reshape(tokens, inner_width)
    dvalue = dvalue.reshape(tokens, inner_width)
    grad_query = through_rows(flat_in, dquery)
    grad_query_bias = jnp.sum(dquery.astype(jnp.float32), axis=0)
    grad_key = through_rows(flat_in, dkey)
    grad_value = through_rows(flat_in, dvalue)
    grad_value_bias = jnp.sum(dvalue.astype(jnp.float32), axis=0)
    dinput_part = (
        against_cols(dquery, query_weight)
        + against_cols(dkey, key_weight)
        + against_cols(dvalue, value_weight)
    ).reshape(all_rows, length, model_width)
    vector_terms = jnp.stack(
        [
            out_bias_part,
            attn_gain_part,
            attn_shift_part,
            down_bias_part,
            ffn_gain_part,
            ffn_shift_part,
        ]
    )
    dinput, vector_sums = (
        lax.psum_scatter(
            dinput_part.astype(jnp.bfloat16), "tensor", scatter_dimension=0, tiled=True
        ).astype(jnp.float32),
        lax.psum_scatter(
            vector_terms.astype(jnp.bfloat16), "tensor", scatter_dimension=1, tiled=True
        ).astype(jnp.float32),
    )
    totals = lax.psum(
        (
            grad_query,
            grad_query_bias,
            grad_key,
            grad_value,
            grad_value_bias,
            grad_out,
            grad_up,
            grad_up_bias,
            grad_down,
            vector_sums,
        ),
        "batch",
    )
    vectors = totals[9]
    return (
        final.astype(jnp.bfloat16),
        pooled,
        dinput + dresid1,
        totals[0],
        totals[1],
        totals[2],
        totals[3],
        totals[4],
        totals[5],
        vectors[0],
        vectors[1],
        vectors[2],
        totals[6],
        totals[7],
        totals[8],
        vectors[3],
        vectors[4],
        vectors[5],
    )


def solution(mesh):
    in_specs = (
        P(("batch", "tensor"), None, None),
        P("batch", None),
        P(None, "tensor"),
        P("tensor"),
        P(None, "tensor"),
        P(None, "tensor"),
        P("tensor"),
        P("tensor", None),
        P(),
        P(),
        P(),
        P(None, "tensor"),
        P("tensor"),
        P("tensor", None),
        P(),
        P(),
        P(),
        P(("batch", "tensor"), None, None),
    )
    out_specs = (
        P(("batch", "tensor"), None, None),
        P(("batch", "tensor"), None, None),
        P(("batch", "tensor"), None, None),
        P(None, "tensor"),
        P("tensor"),
        P(None, "tensor"),
        P(None, "tensor"),
        P("tensor"),
        P("tensor", None),
        P("tensor"),
        P("tensor"),
        P("tensor"),
        P(None, "tensor"),
        P("tensor"),
        P("tensor", None),
        P("tensor"),
        P("tensor"),
        P("tensor"),
    )
    return jax.shard_map(
        per_device, mesh=mesh, in_specs=in_specs, out_specs=out_specs, check_vma=False
    )
```

profile of v0, /device:TPU:0, one launch (start us, length us, event | category | flops | bytes accessed | tf_op | source)
XLA Modules:
  0.0 927.0 jit_solution(11372551995541683853)
XLA Ops:
  8.0 67.8 %all-gather.5.cloned.1.call-done = bf16[4,512,768]{2,1,0:T(8,128)(2,1)} async-done(((bf16[1,512,768]{2,1,0:T(8,128)(2,1)}), bf16[4,512,768]{2,1,0:T(8,128)(2,1)}) %all-gather.5.cloned.1.call-update) | async-done | bytes 3145744 | tf_op jit(solution)/shard_map/all_gather | solution.py:62
  75.8 3.2 fusion.60
  80.6 3.1 fusion.61
  84.6 3.1 convolution_convert_fusion.1
  88.5 17.4 %while.26 = (s32[]{:T(128)}, bf16[4,512,3,64]{1,3,2,0:T(8,128)(2,1)S(1)}, f32[4,3,512,1]{2,1,3,0:T(4,128)}, bf16[4,512,3,64]{1,3,2,0:T(8,128)(2,1)}, s32[4,512]{...) while((s32[]{:T(128)}, ...), condition=%wide.region_3.4_spmd, body=%wide.region_0.3_spmd.sunk | while | flops 211122688 | bytes 11336281 | solution.py:95
  90.8 2.0 fusion.154
  95.2 2.0 fusion.154
  99.5 2.0 fusion.154
  103.9 2.0 fusion.154
  105.9 4.9 fusion.81
  110.9 109.5 %reduce-scatter.8.cloned.1.call-done = f32[1,512,768]{2,1,0:T(8,128)} async-done(((f32[4,512,768]{2,1,0:T(8,128)}), f32[1,512,768]{2,1,0:T(8,128)}) %reduce-scatter.8.cloned.1.call-update) | async-done | bytes 1572880 | tf_op jit(solution)/shard_map/reduce_scatter | solution.py:101
  220.4 1.9 fusion.90
  223.8 1.9 fusion.68
  226.0 63.9 %all-gather.7.cloned.1.call-done = bf16[4,512,768]{2,1,0:T(8,128)(2,1)} async-done(((bf16[1,512,768]{2,1,0:T(8,128)(2,1)}), bf16[4,512,768]{2,1,0:T(8,128)(2,1)}) %all-gather.7.cloned.1.call-update) | async-done | bytes 3145744 | tf_op jit(solution)/shard_map/all_gather | solution.py:104
  289.8 18.4 %multiply_convert_fusion.1 = (bf16[2048,768]{1,0:T(8,128)(2,1)S(1)}, f32[2048,768]{1,0:T(8,128)}, f32[2048,768]{1,0:T(8,128)}) fusion(f32[768]{0:T(1024)} %param.34, bf16[2048,768]{1,0:T(8,128)(2,1)} %bitcast.240, bf16[768,768]{1,0:T(8,128)(2,1)S(1)} %copy-done), kind=kOutput, calls=%fused_computation.67 | convolution fusion | flops 2519728128 | bytes 20057088 | tf_op jit(solution)/shard_map/dot_general | solution.py:13
  308.3 4.5 fusion.92
  312.8 109.5 %reduce-scatter.10.cloned.1.call-done = f32[1,512,768]{2,1,0:T(8,128)} async-done(((f32[4,512,768]{2,1,0:T(8,128)}), f32[1,512,768]{2,1,0:T(8,128)}) %reduce-scatter.10.cloned.1.call-update) | async-done | bytes 1572880 | tf_op jit(solution)/shard_map/reduce_scatter | solution.py:111
  422.4 2.1 fusion.88
  426.1 1.6 fusion.87
  428.9 1.7 add_reduce_fusion.1
  430.8 63.8 %all-gather.9.cloned.1.call-done = bf16[4,512,768]{2,1,0:T(8,128)(2,1)} async-done(((bf16[1,512,768]{2,1,0:T(8,128)(2,1)}), bf16[4,512,768]{2,1,0:T(8,128)(2,1)}) %all-gather.9.cloned.1.call-update) | async-done | bytes 3145744 | tf_op jit(solution)/shard_map/all_gather | solution.py:125
  494.7 11.0 %convert_reduce_fusion = (f32[768]{0:T(1024)}, bf16[2048,768]{1,0:T(8,128)(2,1)S(1)}) fusion(f32[2048,768]{1,0:T(8,128)} %get-tuple-element.242, f32[2048,768]{1,0:T(8,128)} %get-tuple-element.260, f32[768]{0:T(1024)} %param.34, bf16[2048,768]{1,0:T(8,128)(2,1)} %bitcast.242, bf16[768,768]{1,0:T(8,128)(2,1)} %param.35), kind=kOutput, calls=%fused_computation.64 | convolution fusion | flops 2442657024 | bytes 20060160 | tf_op jit(solution)/shard_map/dot_general | solution.py:23
  505.7 4.5 fusion.93
  510.3 109.5 %reduce-scatter.12.cloned.1.call-done = f32[1,512,768]{2,1,0:T(8,128)} async-done(((f32[4,512,768]{2,1,0:T(8,128)}), f32[1,512,768]{2,1,0:T(8,128)}) %reduce-scatter.12.cloned.1.call-update) | async-done | bytes 1572880 | tf_op jit(solution)/shard_map/reduce_scatter | solution.py:132
  619.8 2.7 multiply_reduce_fusion.1
  627.0 62.6 %all-gather.11.cloned.1.call-done = bf16[4,512,768]{2,1,0:T(8,128)(2,1)} async-done(((bf16[1,512,768]{2,1,0:T(8,128)(2,1)}), bf16[4,512,768]{2,1,0:T(8,128)(2,1)}) %all-gather.11.cloned.1.call-update) | async-done | bytes 3145744 | tf_op jit(solution)/shard_map/all_gather | solution.py:136
  689.6 3.1 convolution_convert_fusion
  695.4 29.1 %while.27 = (s32[]{:T(128)}, bf16[4,512,3,64]{1,3,2,0:T(8,128)(2,1)S(1)}, bf16[4,512,3,64]{1,3,2,0:T(8,128)(2,1)}, bf16[4,512,3,64]{1,3,2,0:T(8,128)(2,1)}, bf16...) while((s32[]{:T(128)}, ...), condition=%wide.region_18.19_spmd, body=%wide.region_16.18_spmd.sunk | while | flops 511146496 | bytes 26127476 | solution.py:165
  697.3 1.6 multiply_reduce_fusion.6
  704.6 1.6 multiply_reduce_fusion.6
  711.8 1.6 multiply_reduce_fusion.6
  719.1 1.6 multiply_reduce_fusion.6
  724.5 2.1 copy.90
  730.6 2.8 add_convert_fusion
  734.0 1.9 copy.91
  736.1 6.2 fusion.98
  742.3 4.2 fusion.97
  746.5 1.7 convolution_bitcast_fusion
  748.1 1.7 convolution_bitcast_fusion.1
  749.8 1.7 convolution_bitcast_fusion.2
  751.9 1.6 fusion.96
  759.0 25.1 %all-reduce = (f32[192]{0:T(256)}, f32[192]{0:T(256)}, f32[6,192]{1,0:T(8,128)S(1)}, f32[768]{0:T(1024)}) all-reduce(f32[192]{0:T(256)S(1)} %reduce_sum.226, f32[192]{0:T(256)S(1)} %reduce_sum.228, bf16[6,192]{1,0:T(8,128)(2,1)S(1)} %copy.97, f32[768]{0:T(1024)S(1)} %copy-done.43), channel_id=1, replica_groups=mesh['batch'=8,'tensor'=4] {'batch'}, use_global_device_ids=true, to_apply=%region_22.23 | all-reduce | flops 2304 | bytes 16128 | tf_op jit(solution)/shard_map/psum | solution.py:199
  784.8 7.9 reduce-scatter.14.cloned.1.call-done
  792.7 3.0 convert_add_fusion
  795.7 114.8 %all-reduce.4.cloned.1.call-done = (f32[768,192]{0,1:T(8,128)}, f32[768,192]{0,1:T(8,128)}, f32[768,192]{0,1:T(8,128)}, f32[192,768]{1,0:T(8,128)}, f32[768,768]{1,0:T(8,128)}, /*index=5*/f32[768,768]{1,0:T(8,128)}) async-done(((f32[768,192]{0,1:T(8,128)}, f32[768,192]{0,1:T(8,128)}, f32[768,192]{0,1:T(8,128)}, f32[192,768]{1,0:T(8,128)}, f32[768,768]{1,0:T(8,128)}, /*index=5*/f32[768,768]{1,0:T(8,128)}), ...) | async-done | bytes 7077904 | tf_op jit(solution)/shard_map/psum | solution.py:199
  910.5 2.1 copy.135
  912.5 1.9 copy.136
  914.5 1.9 copy.137
  (231 shorter events, 62.8 us)
Async XLA Ops:
  7.2 282.6 %copy-start = (bf16[768,768]{1,0:T(8,128)(2,1)S(1)}, bf16[768,768]{1,0:T(8,128)(2,1)}, u32[]{:S(2)}) copy-start(bf16[768,768]{1,0:T(8,128)(2,1)} %param.33) | copy-start | bytes 3538948
  7.2 68.6 %all-gather.5.cloned.1.call-start = ((), (), s32[]{:S(2)}) async-start(), calls=%async_computation.5 | async-start | bytes 3932160 | tf_op jit(solution)/shard_map/all_gather | solution.py:62
  7.9 212.5 %reduce-scatter.8.cloned.1.call-start = ((), (), s32[]{:S(2)}) async-start(), calls=%async_computation.6 | async-start | bytes 7864320 | tf_op jit(solution)/shard_map/reduce_scatter | solution.py:101
  79.0 1.6 copy-start.20
  79.0 1.6 copy-start.48
  105.9 4.9 copy-start.7
  105.9 4.9 copy-start.11
  110.8 109.6 %copy-start.44 = (f32[768]{0:T(1024)S(1)}, f32[768]{0:T(1024)}, u32[]{:S(2)}) copy-start(f32[768]{0:T(1024)} %param.30) | copy-start | bytes 9220
  110.8 113.0 %copy-start.25 = (f32[768]{0:T(1024)S(1)}, f32[768]{0:T(1024)}, u32[]{:S(2)}) copy-start(f32[768]{0:T(1024)} %param.31) | copy-start | bytes 9220
  110.8 179.0 %all-gather.7.cloned.1.call-start = ((), (), s32[]{:S(2)}) async-start(), calls=%async_computation.7 | async-start | bytes 3932160 | tf_op jit(solution)/shard_map/all_gather | solution.py:104
  225.7 196.6 %reduce-scatter.10.cloned.1.call-start = ((), (), s32[]{:S(2)}) async-start(), calls=%async_computation.8 | async-start | bytes 7864320 | tf_op jit(solution)/shard_map/reduce_scatter | solution.py:111
  289.8 18.4 %copy-start.47 = (bf16[768,768]{1,0:T(8,128)(2,1)S(1)}, bf16[768,768]{1,0:T(8,128)(2,1)}, u32[]{:S(2)}) copy-start(bf16[768,768]{1,0:T(8,128)(2,1)} %param.35) | copy-start | bytes 3538948
  308.3 4.5 copy-start.49
  312.8 181.9 %all-gather.9.cloned.1.call-start = ((), (), s32[]{:S(2)}) async-start(), calls=%async_computation.9 | async-start | bytes 3932160 | tf_op jit(solution)/shard_map/all_gather | solution.py:125
  422.4 2.4 copy-start.12
  422.4 2.4 copy-start.37
  424.4 3.3 copy-start.3
  424.4 1.7 copy-start.41
  424.5 3.2 copy-start.29
  424.8 2.9 copy-start.31
  427.7 2.8 copy-start.33
  430.6 189.3 %reduce-scatter.12.cloned.1.call-start = ((), (), s32[]{:S(2)}) async-start(), calls=%async_computation.10 | async-start | bytes 7864320 | tf_op jit(solution)/shard_map/reduce_scatter | solution.py:132
  505.7 4.5 copy-start.50
  510.2 109.6 %copy-start.28 = (f32[512]{0:T(512)S(1)}, f32[512]{0:T(512)}, u32[]{:S(2)}) copy-start(f32[512]{0:T(512)} %copy-done.27) | copy-start | bytes 6148
  510.2 109.6 %copy-start.34 = (f32[512]{0:T(512)S(1)}, f32[512]{0:T(512)}, u32[]{:S(2)}) copy-start(f32[512]{0:T(512)} %copy-done.33) | copy-start | bytes 6148
  510.3 112.3 %copy-start.36 = (f32[512]{0:T(512)S(1)}, f32[512]{0:T(512)}, u32[]{:S(2)}) copy-start(f32[512]{0:T(512)} %copy-done.35) | copy-start | bytes 6148
  510.3 179.3 %all-gather.11.cloned.1.call-start = ((), (), s32[]{:S(2)}) async-start(), calls=%async_computation.11 | async-start | bytes 3932160 | tf_op jit(solution)/shard_map/all_gather | solution.py:136
  622.6 3.0 copy-start.13
  623.2 2.5 copy-start.40
  623.2 2.5 copy-start.39
  623.2 66.3 %copy-start.19 = (bf16[192,768]{1,0:T(8,128)(2,1)S(1)}, bf16[192,768]{1,0:T(8,128)(2,1)}, u32[]{:S(2)}) copy-start(bf16[192,768]{1,0:T(8,128)(2,1)} %param.29) | copy-start | bytes 884740
  625.5 131.0 %reduce-scatter.16.cloned.1.call-start = ((), (), s32[]{:S(2)}) async-start(), calls=%async_computation.13 | async-start | bytes 245760
  626.7 166.0 %reduce-scatter.14.cloned.1.call-start = ((), (), s32[]{:S(2)}) async-start(), calls=%async_computation.12 | async-start | bytes 3932160 | tf_op jit(solution)/shard_map/reduce_scatter | solution.py:192
  692.6 2.8 copy-start.8
  724.5 2.1 copy-start.9
  724.5 2.3 copy-start.15
  726.7 1.7 copy-start.21
  733.5 177.0 %all-reduce.4.cloned.1.call-start = ((), (), s32[]{:S(2)}) async-start(), calls=%async_computation.14 | async-start | bytes 14155776 | tf_op jit(solution)/shard_map/psum | solution.py:199
  734.0 2.1 copy-start.46
  736.1 6.2 copy-start.45
  736.1 6.2 copy-start.51
  742.3 4.2 copy-start.2
  749.8 2.2 copy-start.14
  753.6 5.4 copy-start.43
  910.5 5.9 copy-start.18
  910.5 6.7 copy-start.17
  916.4 2.2 copy-start.16
  917.2 2.8 copy-start.1
  (14 other events, 15.7 us)
Sparse Core Ops, SparseCore 0:
  9.6 66.1 all-gather.4
  110.9 109.4 reduce-scatter.7
  225.9 63.9 all-gather.6
  312.9 109.4 reduce-scatter.9
  430.7 63.9 all-gather.8
  510.4 109.4 reduce-scatter.11
  625.6 63.9 all-gather.10
  691.8 18.2 reduce-scatter.15
  733.6 59.0 reduce-scatter.13
  797.7 112.6 all-reduce.3
where the time goes:
time: 935 us; the launch traced here: 927 us
  waiting for transfers between devices  710 us (76%)
  matrix products  112 us (12%)
  local copies, waits for them, and re-layouts  32.4 us (3%)
  other arithmetic  30.5 us (3%)
  blocking collectives  25.1 us (3%)
  between operations  15 us (2%)
    psum x1, waiting for transfers between devices, per_device(): lax.psum((grad_query, grad_query_bias, grad_key, grad_value, grad_value_b...  115 us
    reduce_scatter x1, waiting for transfers between devices, per_device(): lax.psum_scatter(partial_ffn, 'tensor', scatter_dimension=0, tiled=True)  110 us
    reduce_scatter x1, waiting for transfers between devices, per_device(): lax.psum_scatter(dhidden_part, 'tensor', scatter_dimension=0, tiled=True)  110 us
    reduce_scatter x1, waiting for transfers between devices, per_device(): lax.psum_scatter(partial_out, 'tensor', scatter_dimension=0, tiled=True)  110 us
    all_gather x1, waiting for transfers between devices, per_device(): gathered = lax.all_gather(hidden_in, 'tensor', axis=0, tiled=True)  67.8 us
    all_gather x1, waiting for transfers between devices, per_device(): lax.all_gather(hidden1_low, 'tensor', axis=0, tiled=True)  63.9 us
    all_gather x1, waiting for transfers between devices, per_device(): lax.all_gather(dffn_low, 'tensor', axis=0, tiled=True)  63.8 us
    all_gather x1, waiting for transfers between devices, per_device(): lax.all_gather(dattn_low, 'tensor', axis=0, tiled=True)  62.6 us
  transfers between devices with their start and end apart: 10, of which 9 were waited for; matrix products, arithmetic and copies ran while one was open for 8% of the time, Pallas kernels for 0%

commit v1 on v0

v1 whole, which is shorter than its diff:
```python
import functools
import math

import jax
import jax.numpy as jnp
from jax import lax
from jax.experimental import pallas as pl
from jax.experimental.pallas import tpu as pltpu
from jax.sharding import PartitionSpec as P

HEAD_DIM = 64
TEXTS = 8
PLANE = 8
CHIPS = 4
MESH = pl.DeviceIdType.MESH
F32 = jnp.float32
BF16 = jnp.bfloat16


class Place:
    def __init__(self, n_t):
        bi = lax.axis_index("batch")
        self.t = lax.axis_index("tensor")
        self.n_t = n_t
        self.r = lax.rem(bi, PLANE)
        self.base = bi - self.r
        self.c = lax.rem(self.r, 2)
        self.q = self.r // 2

    def z(self, step):
        return {"batch": self.base + self.r, "tensor": lax.rem(self.t + step, self.n_t)}

    def chip(self, j):
        other = self.xor_q(j)
        return {"batch": self.base + other * 2 + self.c, "tensor": self.t}

    def xor_q(self, j):
        x, y = lax.rem(self.q, 2), self.q // 2
        if j & 1:
            x = 1 - x
        if j & 2:
            y = 1 - y
        return y * 2 + x

    def sibling(self):
        return {"batch": self.base + self.q * 2 + 1 - self.c, "tensor": self.t}

    def greet(self):
        barrier = pltpu.get_barrier_semaphore()
        peers = [self.z(s) for s in range(1, self.n_t)]
        peers += [self.chip(j) for j in range(1, CHIPS)] + [self.sibling()]
        for peer in peers:
            pl.semaphore_signal(barrier, inc=1, device_id=peer, device_id_type=MESH)
        pl.semaphore_wait(barrier, len(peers))


def remote(src, dst, send, recv, dev):
    return pltpu.make_async_remote_copy(
        src_ref=src, dst_ref=dst, send_sem=send, recv_sem=recv, device_id=dev, device_id_type=MESH
    )


def gather_kernel(n_t, wl, w, zs, zr, xs, xr, ss, sr, ls):
    me = Place(n_t)
    groups, rows = wl.shape[0], wl.shape[1]
    ch = rows // PLANE
    half = rows // 2
    mine = pl.ds(pl.multiple_of((me.c * CHIPS + me.q) * ch, ch), ch)
    my_half = pl.ds(pl.multiple_of(me.c * half, half), half)
    me.greet()

    def zcopy(g, s):
        return remote(wl.at[g, mine], w.at[g, me.t, mine], zs.at[g, s], zr.at[g, s], me.z(s + 1))

    def came(s):
        return lax.rem(me.t + n_t - 1 - s, n_t)

    def xcopy(g, s, j):
        place = w.at[g, came(s), mine]
        return remote(place, place, xs.at[g, s, j], xr.at[g, s, j], me.chip(j + 1))

    def scopy(g, s):
        place = w.at[g, came(s), my_half]
        return remote(place, place, ss.at[g, s], sr.at[g, s], me.sibling())

    for g in range(groups):
        for s in range(n_t - 1):
            zcopy(g, s).start()
    for g in range(groups):
        pltpu.make_async_copy(wl.at[g], w.at[g, me.t], ls.at[g]).start()
    for g in range(groups):
        for s in range(n_t - 1):
            zcopy(g, s).wait_recv()
            for j in range(CHIPS - 1):
                xcopy(g, s, j).start()
    for g in range(groups):
        for s in range(n_t - 1):
            for j in range(CHIPS - 1):
                xcopy(g, s, j).wait_recv()
            scopy(g, s).start()
    for g in range(groups):
        for s in range(n_t - 1):
            scopy(g, s).wait_recv()
    for g in range(groups):
        pltpu.make_async_copy(wl.at[g], w.at[g, me.t], ls.at[g]).wait()
        for s in range(n_t - 1):
            zcopy(g, s).wait_send()
            scopy(g, s).wait_send()
            for j in range(CHIPS - 1):
                xcopy(g, s, j).wait_send()


def gather_weights(wl, n_t):
    groups, rows, cols = wl.shape
    dma = pltpu.SemaphoreType.DMA
    return pl.pallas_call(
        functools.partial(gather_kernel, n_t),
        out_shape=jax.ShapeDtypeStruct((groups, n_t, rows, cols), wl.dtype),
        in_specs=[pl.BlockSpec(memory_space=pltpu.VMEM)],
        out_specs=pl.BlockSpec(memory_space=pltpu.VMEM),
        scratch_shapes=[
            dma((groups, n_t - 1)),
            dma((groups, n_t - 1)),
            dma((groups, n_t - 1, CHIPS - 1)),
            dma((groups, n_t - 1, CHIPS - 1)),
            dma((groups, n_t - 1)),
            dma((groups, n_t - 1)),
            dma((groups,)),
        ],
        compiler_params=pltpu.CompilerParams(
            collective_id=1, has_side_effects=True, vmem_limit_bytes=60 << 20
        ),
    )(wl)


def reduce_kernel(
    n_t, gin, vin, fout, vout, g_ref, a_ref, b_ref, d_ref, va, vb, vd, vsum,
    ls, as_, ar, bs, br, ds_, dr, fs, fr, ss, sr, vs, vr,
):
    me = Place(n_t)
    groups, rows = gin.shape[0], gin.shape[2]
    ch = rows // PLANE
    half = rows // 2
    mine = pl.ds(pl.multiple_of((me.c * CHIPS + me.q) * ch, ch), ch)
    my_half = pl.ds(pl.multiple_of(me.c * half, half), half)
    other_half = pl.ds(pl.multiple_of((1 - me.c) * half, half), half)
    me.greet()
    units = [(g, s) for g in range(groups) for s in range(n_t)]

    def tu(s):
        return lax.rem(me.t + 1 + s, n_t)

    def r1(g, s):
        return remote(
            gin.at[g, tu(s), other_half], a_ref.at[g, s], as_.at[g, s], ar.at[g, s], me.sibling()
        )

    def r2(g, s, j):
        target = pl.ds(pl.multiple_of((me.c * CHIPS + me.xor_q(j + 1)) * ch, ch), ch)
        return remote(
            g_ref.at[g, s, pl.ds(pl.multiple_of(me.xor_q(j + 1) * ch, ch), ch)],
            b_ref.at[g, s, j], bs.at[g, s, j], br.at[g, s, j], me.chip(j + 1),
        )

    own_q = pl.ds(pl.multiple_of(me.q * ch, ch), ch)

    def r3(g, s):
        return remote(
            g_ref.at[g, s, own_q], d_ref.at[g, s], ds_.at[g, s], dr.at[g, s], me.z(s + 1)
        )

    def r4(g, j):
        place = fout.at[g, mine]
        return remote(place, place, fs.at[g, j], fr.at[g, j], me.chip(j + 1))

    def r5(g):
        place = fout.at[g, my_half]
        return remote(place, place, ss.at[g], sr.at[g], me.sibling())

    v1 = remote(vin, va, vs.at[0], vr.at[0], me.sibling())
    v1.start()
    for g, s in units:
        r1(g, s).start()
    v1.wait_recv()
    vsum[...] = vin[...] + va[...]
    v2 = [
        remote(vsum, vb.at[j], vs.at[1 + j], vr.at[1 + j], me.chip(j + 1)) for j in range(CHIPS - 1)
    ]
    for c in v2:
        c.start()

    for g, s in units:
        r1(g, s).wait_recv()

        @pl.loop(0, CHIPS)
        def _(k):
            part = pl.ds(pl.multiple_of(k * ch, ch), ch)
            src = pl.ds(pl.multiple_of(me.c * half + k * ch, ch), ch)
            g_ref[g, s, part] = (
                gin[g, tu(s), src].astype(F32) + a_ref[g, s, part].astype(F32)
            ).astype(BF16)

        for j in range(CHIPS - 1):
            r2(g, s, j).start()
    for c in v2:
        c.wait()
    va[...] = vsum[...] + vb[0] + vb[1] + vb[2]
    v3 = [
        remote(va.at[tu(s)], vd.at[s], vs.at[4 + s], vr.at[4 + s], me.z(s + 1))
        for s in range(n_t - 1)
    ]
    for c in v3:
        c.start()
    for g, s in units:
        for j in range(CHIPS - 1):
            r2(g, s, j).wait_recv()
        total = g_ref[g, s, own_q].astype(F32)
        for j in range(CHIPS - 1):
            total = total + b_ref[g, s, j].astype(F32)
        g_ref[g, s, own_q] = total.astype(BF16)
        if s < n_t - 1:
            r3(g, s).start()
    for c in v3:
        c.wait()
    vout[...] = va[me.t] + vd[0] + vd[1] + vd[2]
    for g in range(groups):
        for s in range(n_t - 1):
            r3(g, s).wait_recv()
        total = g_ref[g, n_t - 1, own_q].astype(F32)
        for s in range(n_t - 1):
            total = total + d_ref[g, s].astype(F32)
        fout[g, mine] = total.astype(BF16)
        for j in range(CHIPS - 1):
            r4(g, j).start()
    for g in range(groups):
        for j in range(CHIPS - 1):
            r4(g, j).wait_recv()
        r5(g).start()
    for g in range(groups):
        r5(g).wait_recv()
    v1.wait_send()
    for g, s in units:
        r1(g, s).wait_send()
        for j in range(CHIPS - 1):
            r2(g, s, j).wait_send()
        if s < n_t - 1:
            r3(g, s).wait_send()
    for g in range(groups):
        for j in range(CHIPS - 1):
            r4(g, j).wait_send()
        r5(g).wait_send()


def reduce_grads(gin, vin, n_t):
    groups, _, rows, cols = gin.shape
    dma = pltpu.SemaphoreType.DMA
    vmem = pltpu.VMEM
    ch, half = rows // PLANE, rows // 2
    vshape = vin.shape
    return pl.pallas_call(
        functools.partial(reduce_kernel, n_t),
        out_shape=(
            jax.ShapeDtypeStruct((groups, rows, cols), BF16),
            jax.ShapeDtypeStruct(vshape[1:], F32),
        ),
        in_specs=[pl.BlockSpec(memory_space=vmem)] * 2,
        out_specs=[pl.BlockSpec(memory_space=vmem)] * 2,
        scratch_shapes=[
            vmem((groups, n_t, half, cols), BF16),
            vmem((groups, n_t, half, cols), BF16),
            vmem((groups, n_t, CHIPS - 1, ch, cols), BF16),
            vmem((groups, n_t - 1, ch, cols), BF16),
            vmem(vshape, F32),
            vmem((CHIPS - 1,) + vshape, F32),
            vmem((n_t - 1,) + vshape[1:], F32),
            vmem(vshape, F32),
            dma((1,)),
            dma((groups, n_t)),
            dma((groups, n_t)),
            dma((groups, n_t, CHIPS - 1)),
            dma((groups, n_t, CHIPS - 1)),
            dma((groups, n_t - 1)),
            dma((groups, n_t - 1)),
            dma((groups, CHIPS - 1)),
            dma((groups, CHIPS - 1)),
            dma((groups,)),
            dma((groups,)),
            dma((4 + n_t,)),
            dma((4 + n_t,)),
        ],
        compiler_params=pltpu.CompilerParams(
            collective_id=2, has_side_effects=True, vmem_limit_bytes=62 << 20
        ),
    )(gin, vin)


def product(left, right):
    return jnp.dot(left, right, preferred_element_type=F32)


def through_rows(left, right):
    return lax.dot_general(left, right, (((0,), (0,)), ((), ())), preferred_element_type=F32)


def against_cols(left, right):
    return lax.dot_general(left, right, (((1,), (1,)), ((), ())), preferred_element_type=F32)


def normalize(resid, gain, shift):
    center = resid - jnp.mean(resid, axis=-1, keepdims=True)
    spread = jnp.mean(center * center, axis=-1, keepdims=True)
    return center * lax.rsqrt(spread + 1e-12) * gain + shift


def gelu_exact(value):
    return jax.nn.gelu(value, approximate=False)


def per_device(
    n_t, n_b,
    hidden_in, segment_ids, query_weight, query_bias, key_weight, value_weight, value_bias,
    out_weight, out_bias, attn_gain, attn_shift, up_weight, up_bias, down_weight, down_bias,
    ffn_gain, ffn_shift, cotangent,
):
    x = hidden_in[0]
    inner = query_weight.shape[1]
    heads = inner // HEAD_DIM
    scale = 1.0 / math.sqrt(HEAD_DIM)
    t = lax.axis_index("tensor")
    qkvo = jnp.concatenate([query_weight, key_weight, value_weight, out_weight.T], axis=1)
    w = gather_weights(jnp.stack([qkvo, up_weight, down_weight]), n_t)
    biases = lax.all_gather(
        jnp.concatenate([query_bias, value_bias, up_bias]), "tensor", axis=0, tiled=False
    )
    bq, bv, bu = biases[:, :inner], biases[:, inner : 2 * inner], biases[:, 2 * inner :]
    seg = lax.dynamic_slice_in_dim(segment_ids, t, 1, 0)[0]
    same = seg[:, None] == seg[None, :]

    def heads_of(v):
        return v.reshape(v.shape[0], n_t * heads, HEAD_DIM)

    def cat(f):
        return jnp.concatenate([f(i) for i in range(n_t)], axis=1)

    q = cat(lambda i: product(x, w[0, i, :, :inner]) + bq[i]).astype(BF16)
    k = cat(lambda i: product(x, w[0, i, :, inner : 2 * inner])).astype(BF16)
    v = cat(lambda i: product(x, w[0, i, :, 2 * inner : 3 * inner]) + bv[i]).astype(BF16)
    qh, kh, vh = heads_of(q), heads_of(k), heads_of(v)
    scores = jnp.einsum("qhd,khd->hqk", qh, kh, preferred_element_type=F32) * scale
    scores = jnp.where(same[None], scores, -1000000000.0)
    ex = jnp.exp(scores - jnp.max(scores, axis=-1, keepdims=True))
    prob = ex / jnp.sum(ex, axis=-1, keepdims=True)
    plow = prob.astype(BF16)
    ctx = jnp.einsum("hqk,khd->qhd", plow, vh, preferred_element_type=F32).astype(BF16)
    ctx = ctx.reshape(x.shape)
    xf = x.astype(F32)
    wot = jnp.concatenate([w[0, i, :, 3 * inner :] for i in range(n_t)], axis=1)
    attn = against_cols(ctx, wot)
    hidden1, pull1 = jax.vjp(normalize, attn + out_bias + xf, attn_gain, attn_shift)
    h1 = hidden1.astype(BF16)
    ffn = 0.0
    acts, pulls = [], []
    for i in range(n_t):
        pre = product(h1, w[1, i]) + bu[i]
        act, pull = jax.vjp(gelu_exact, pre)
        acts.append(act.astype(BF16))
        pulls.append(pull)
        ffn = ffn + product(acts[-1], w[2, i])
    final, pull2 = jax.vjp(normalize, ffn + down_bias + hidden1, ffn_gain, ffn_shift)
    labels = jnp.arange(TEXTS, dtype=jnp.int32)
    member = (seg[None, :] == labels[:, None]).astype(F32)
    pooled = (
        jnp.dot(member, final, precision=lax.Precision.HIGHEST)
        / jnp.sum(member, axis=-1)[:, None]
    )
    dres2, ffn_gain_part, ffn_shift_part = pull2(cotangent[0].astype(F32))
    dffn = dres2.astype(BF16)
    gdown, gup, gub = [], [], []
    dh = dres2
    for i in range(n_t):
        gdown.append(through_rows(acts[i], dffn).astype(BF16))
        dpre = pulls[i](against_cols(dffn, w[2, i]))[0].astype(BF16)
        gub.append(jnp.sum(dpre.astype(F32), axis=0))
        gup.append(through_rows(h1, dpre).astype(BF16))
        dh = dh + against_cols(dpre, w[1, i])
    dres1, attn_gain_part, attn_shift_part = pull1(dh)
    dattn = dres1.astype(BF16)
    gout = through_rows(dattn, ctx).astype(BF16)
    dctx = product(dattn, wot).astype(BF16)
    dctxh = heads_of(dctx)
    dv = jnp.einsum("hqk,qhd->khd", plow, dctxh, preferred_element_type=F32).astype(BF16)
    dprob = jnp.einsum("qhd,khd->hqk", dctxh, vh, preferred_element_type=F32)
    ds = (prob * (dprob - jnp.sum(dprob * prob, axis=-1, keepdims=True))).astype(BF16)
    dq = (jnp.einsum("hqk,khd->qhd", ds, kh, preferred_element_type=F32) * scale).astype(BF16)
    dk = (jnp.einsum("hqk,qhd->khd", ds, qh, preferred_element_type=F32) * scale).astype(BF16)
    dq, dk, dv = (z.reshape(x.shape) for z in (dq, dk, dv))
    grads = [through_rows(x, z).astype(BF16) for z in (dq, dk, dv)] + [gout]
    cols = lambda z, i: z[..., i * inner : (i + 1) * inner]
    gqkvo = [jnp.concatenate([cols(z, i) for z in grads], axis=1) for i in range(n_t)]
    dx = dres1
    for i in range(n_t):
        dqkv = jnp.concatenate([cols(dq, i), cols(dk, i), cols(dv, i)], axis=1)
        dx = dx + against_cols(dqkv, w[0, i, :, : 3 * inner])
    vecs = [
        jnp.sum(dres1, axis=0), attn_gain_part, attn_shift_part,
        jnp.sum(dres2, axis=0), ffn_gain_part, ffn_shift_part,
        jnp.sum(dq.astype(F32), axis=0), jnp.sum(dv.astype(F32), axis=0),
    ]
    vrow = [jnp.concatenate([cols(z, i) for z in vecs] + [gub[i]]) for i in range(n_t)]
    used = vrow[0].shape[0]
    lanes = 384
    vin = jnp.pad(jnp.stack(vrow), ((0, 0), (0, 8 * lanes - used))).reshape(n_t, 8, lanes)
    gin = jnp.stack([jnp.stack(gdown), jnp.stack(gup), jnp.stack(gqkvo)])
    fout, vout = reduce_grads(gin, vin, n_t)
    if n_b > PLANE:
        apart = [[i + PLANE * j for j in range(n_b // PLANE)] for i in range(PLANE)]
        fout, vout = lax.psum((fout.astype(F32), vout), "batch", axis_index_groups=apart)
    fout = fout.astype(F32)
    vec = vout.reshape(-1)
    vc = lambda i: vec[i * inner : (i + 1) * inner]
    return (
        final.astype(BF16)[None],
        pooled[None],
        dx[None],
        fout[2, :, :inner],
        vc(6),
        fout[2, :, inner : 2 * inner],
        fout[2, :, 2 * inner : 3 * inner],
        vc(7),
        fout[2, :, 3 * inner :].T,
        vc(0),
        vc(1),
        vc(2),
        fout[1],
        vec[8 * inner : 8 * inner + up_bias.shape[0]],
        fout[0],
        vc(3),
        vc(4),
        vc(5),
    )


def solution(mesh):
    rows, tens = P(("batch", "tensor"), None, None), P("tensor")
    col, row = P(None, "tensor"), P("tensor", None)
    in_specs = (
        rows, P("batch", None), col, tens, col, col, tens, row, P(), P(), P(), col, tens, row,
        P(), P(), P(), rows,
    )
    out_specs = (
        rows, rows, rows, col, tens, col, col, tens, row, tens, tens, tens, col, tens, row, tens,
        tens, tens,
    )
    body = functools.partial(per_device, mesh.shape["tensor"], mesh.shape["batch"])
    return jax.shard_map(
        body, mesh=mesh, in_specs=in_specs, out_specs=out_specs, check_vma=False
    )
```

time: 935 us -> 427 us (0.46)
  waiting for transfers between devices: 710 us -> 0 us
  Pallas kernels: 0 us -> 195 us
  matrix products: 112 us -> 148 us
  between operations: 15 us -> 1.93 us
  blocking collectives: 25.1 us -> 14.2 us
    reduce_scatter x4 -> x0, waiting for transfers between devices: 337 us -> none  [the longest x1 110 us: per_device(): lax.psum_scatter(partial_ffn, 'tensor', scatter_dimension=0, tiled=True)]
    all_gather x4 -> x0, waiting for transfers between devices: 258 us -> none  [the longest x1 67.8 us: per_device(): gathered = lax.all_gather(hidden_in, 'tensor', axis=0, tiled=True)]
    pallas_call x0 -> x2, Pallas kernels: none -> 195 us  [the longest x1 116 us: reduce_grads(): pl.pallas_call(functools.partial(reduce_kernel, n_t), out_shape=(jax.Shap...]
    psum x1 -> x0, waiting for transfers between devices: 115 us -> none  [per_device(): lax.psum((grad_query, grad_query_bias, grad_key, grad_value, grad_value_b...]
    dot_general x35 -> x27, matrix products: 71.5 us -> 107 us  [the longest x21 82.6 us: product(): return jnp.dot(left, right, preferred_element_type=F32)]
    psum x1 -> x0, blocking collectives: 25.1 us -> none  [per_device(): lax.psum((grad_query, grad_query_bias, grad_key, grad_value, grad_value_b...]
    all_gather x0 -> x1, blocking collectives: none -> 14.2 us  [per_device(): lax.all_gather(jnp.concatenate([query_bias, value_bias, up_bias]), 'tenso...]
    another operation x0 -> x8, other arithmetic: none -> 14.1 us  [the longest x5 11.6 us: per_device(): gin = jnp.stack([jnp.stack(gdown), jnp.stack(gup), jnp.stack(gqkvo)])]
  transfers between devices with their start and end apart: 10 -> 0, of which waited for: 9 -> 0; matrix products, arithmetic and copies ran while one was open for 8% -> 0% of each run, Pallas kernels for 0% -> 0%
where the time goes in v1:
time: 427 us; the launch traced here: 421 us
  Pallas kernels  195 us (46%)
  matrix products  148 us (35%)
  local copies, waits for them, and re-layouts  33.5 us (8%)
  other arithmetic  28.1 us (7%)
  blocking collectives  14.2 us (3%)
    pallas_call x1, Pallas kernels, reduce_grads(): pl.pallas_call(functools.partial(reduce_kernel, n_t), out_shape=(jax.Shap...  116 us
    dot_general x21, matrix products, product(): return jnp.dot(left, right, preferred_element_type=F32)  82.6 us
    pallas_call x1, Pallas kernels, gather_weights(): pl.pallas_call(functools.partial(gather_kernel, n_t), out_shape=jax.Shape...  79 us
    dot_general x13, matrix products, against_cols(): lax.dot_general(left, right, (((1,), (1,)), ((), ())), preferred_element_...  22.5 us
    unnamed x159, local copies, waits for them, and re-layouts  19 us
    all_gather x1, blocking collectives, per_device(): lax.all_gather(jnp.concatenate([query_bias, value_bias, up_bias]), 'tenso...  14.2 us
    another operation x5, other arithmetic, per_device(): gin = jnp.stack([jnp.stack(gdown), jnp.stack(gup), jnp.stack(gqkvo)])  11.6 us
    dot_general x12, matrix products, through_rows(): lax.dot_general(left, right, (((0,), (0,)), ((), ())), preferred_element_...  9.98 us

profile of v1, /device:TPU:0, one launch (start us, length us, event | category | flops | bytes accessed | tf_op | source)
XLA Modules:
  0.0 421.0 jit_solution(8473077786853996908)
XLA Ops:
  4.9 1.9 pad_maximum_fusion.1.wl
  6.8 79.0 %shard_map.313 = bf16[3,4,768,768]{3,2,1,0:T(8,128)(2,1)} custom-call(bf16[3,768,768]{2,1,0:T(8,128)(2,1)} %pad_maximum_fusion.1.wl), custom_call_target="tpu_custom_call" | custom-call | tf_op jit(solution)/shard_map/pallas_call | solution.py:116
  86.0 14.2 %all-gather.1 = f32[4,1,1152]{2,1,0:T(1,128)S(1)} all-gather(f32[1,1,1152]{2,1,0:T(1,128)S(1)} %reshape.224), channel_id=2, replica_groups=mesh['batch'=8,'tensor'=4] {'tensor'}, dimensions={0}, use_global_device_ids=true | all-gather | bytes 23040 | tf_op jit(solution)/shard_map/all_gather | solution.py:332
  100.3 2.1 fusion.98
  102.4 2.1 fusion.97
  104.5 2.1 fusion.96
  106.6 2.1 fusion.95
  109.0 1.7 convolution_convert_fusion.13
  110.7 1.7 convolution_convert_fusion.14
  112.4 1.7 convolution_convert_fusion.15
  114.2 1.8 convolution_convert_fusion.16
  116.0 1.5 fusion.102
  117.5 1.5 fusion.101
  119.0 1.5 fusion.100
  120.5 1.5 fusion.99
  122.1 8.5 %fusion.234 = (f32[12,512]{1,0:T(8,128)S(1)}, f32[12,512,512]{1,2,0:T(8,128)}) fusion(pred[512,512]{0,1:T(8,128)(4,1)S(1)} %broadcast_compare_fusion, bf16[512,3,64]{0,2,1:T(8,128)(2,1)S(1)} %bitcast.362, bf16[512,3,64]{0,2,1:T(8,128)(2,1)S(1)} %bitcast.364, bf16[512,3,64]{0,2,1:T(8,128)(2,1)S(1)} %bitcast.366, bf16[512,3,64]{0,2,1:T(8,128)(2,1)S(1)} %bitcast.368, ...), kind=kOutput, calls=%fused_computation.367 | convolution fusion | flops 417595904 | bytes 14442496 | tf_op jit(solution)/shard_map/sub | solution.py:351
  130.6 6.2 %fusion.50 = bf16[12,64,512]{2,1,0:T(8,128)(2,1)S(1)} fusion(bf16[512,3,64]{0,2,1:T(8,128)(2,1)} %bitcast.398, bf16[512,3,64]{0,2,1:T(8,128)(2,1)} %bitcast.400, bf16[512,3,64]{0,2,1:T(8,128)(2,1)} %bitcast.402, bf16[512,3,64]{0,2,1:T(8,128)(2,1)} %bitcast.404, f32[12,512,512]{1,2,0:T(8,128)} %get-tuple-element.201, f32[12,512]{1,0:T(8,128)S(1)} %get-tuple-element.200), kind=kOutput, calls=%fused_computation.145 | convolution fusion | flops 410517504 | bytes 14180352 | tf_op jit(solution)/shard_map/hqk,khd->qhd/dot_general | solution.py:354
  136.8 2.4 slice_bitcast_fusion.9
  139.2 1.3 fusion.235
  141.6 11.7 %multiply_convert_fusion.3 = (bf16[512,768]{1,0:T(8,128)(2,1)S(1)}, f32[512,768]{1,0:T(8,128)S(1)}, f32[512,768]{1,0:T(8,128)S(1)}) fusion(f32[768]{0:T(1024)S(1)} %get-tuple-element.99, bf16[512,768]{1,0:T(8,128)(2,1)S(1)} %fusion.58, bf16[3,4,768,768]{3,2,1,0:T(8,128)(2,1)} %shard_map.313), kind=kOutput, calls=%fused_computation.58 | convolution fusion | flops 629932032 | bytes 5901312 | tf_op jit(solution)/shard_map/dot_general | solution.py:298
  153.4 23.2 %multiply_convert_fusion.4 = (bf16[512,768]{1,0:T(8,128)(2,1)S(1)}, f32[512,768]{1,0:T(8,128)S(1)}, f32[512,768]{1,0:T(8,128)S(1)}) fusion(f32[768]{0:T(1024)S(1)} %get-tuple-element.100, bf16[512,768]{1,0:T(8,128)(2,1)S(1)} %fusion.58, bf16[3,4,768,768]{3,2,1,0:T(8,128)(2,1)S(1)} %bitcast.347), kind=kOutput, calls=%fused_computation.71 | convolution fusion | flops 629932032 | bytes 5902336 | tf_op jit(solution)/shard_map/dot_general | solution.py:298
  177.6 10.2 %multiply_convert_fusion.6 = (bf16[512,768]{1,0:T(8,128)(2,1)S(1)}, f32[512,768]{1,0:T(8,128)S(1)}, f32[512,768]{1,0:T(8,128)S(1)}) fusion(f32[768]{0:T(1024)S(1)} %get-tuple-element.102, bf16[512,768]{1,0:T(8,128)(2,1)S(1)} %fusion.58, bf16[3,4,768,768]{3,2,1,0:T(8,128)(2,1)S(1)} %bitcast.347), kind=kOutput, calls=%fused_computation.97 | convolution fusion | flops 629932032 | bytes 5902336 | tf_op jit(solution)/shard_map/dot_general | solution.py:298
  188.6 10.2 %multiply_convert_fusion.5 = (bf16[512,768]{1,0:T(8,128)(2,1)S(1)}, f32[512,768]{1,0:T(8,128)S(1)}, f32[512,768]{1,0:T(8,128)S(1)}) fusion(f32[768]{0:T(1024)S(1)} %get-tuple-element.101, bf16[512,768]{1,0:T(8,128)(2,1)S(1)} %fusion.58, bf16[3,4,768,768]{3,2,1,0:T(8,128)(2,1)S(1)} %bitcast.347), kind=kOutput, calls=%fused_computation.84 | convolution fusion | flops 629932032 | bytes 5902336 | tf_op jit(solution)/shard_map/dot_general | solution.py:298
  199.8 1.3 fusion.236
  203.0 1.6 fusion.212
  204.7 1.5 fusion.104
  207.0 1.8 convert_reduce_fusion.1
  208.8 1.8 convert_reduce_fusion.2
  211.5 1.8 convert_reduce_fusion.3
  214.2 1.8 convert_reduce_fusion.4
  217.7 2.0 multiply_reduce_fusion.1
  220.3 2.2 convolution_convert_fusion.12
  222.5 2.3 copy.93
  224.8 7.6 %convert_reduce_fusion.5 = (f32[12,64]{1,0:T(8,128)}, bf16[12,64,512]{2,1,0:T(8,128)(2,1)S(1)}) fusion(bf16[512,12,64]{0,2,1:T(8,128)(2,1)} %bitcast.357, f32[12,512,512]{1,2,0:T(8,128)} %get-tuple-element.201, f32[12,512]{1,0:T(8,128)} %copy-done.31), kind=kOutput, calls=%fused_computation.43 | convolution fusion | flops 410123520 | bytes 14183424 | tf_op jit(solution)/shard_map/hqk,qhd->khd/dot_general | solution.py:391
  234.1 5.7 %multiply_reduce_fusion = (f32[12,512]{1,0:T(8,128)S(1)}, f32[12,512,512]{1,2,0:T(8,128)}) fusion(f32[12,512,512]{1,2,0:T(8,128)S(1)} %bitcast.349, f32[12,512]{1,0:T(8,128)S(1)} %copy-done.32, bf16[512,12,64]{0,2,1:T(8,128)(2,1)S(1)} %bitcast.358, bf16[512,3,64]{0,2,1:T(8,128)(2,1)S(1)} %bitcast.399, bf16[512,3,64]{0,2,1:T(8,128)(2,1)S(1)} %bitcast.401, ...), kind=kOutput, calls=%fused_computation.3 | convolution fusion | flops 413263872 | bytes 26787840 | tf_op jit(solution)/shard_map/qhd,khd->hqk/dot_general | solution.py:392
  239.8 6.0 %multiply_convert_fusion = bf16[12,512,512]{1,2,0:T(8,128)(2,1)S(1)} fusion(f32[12,512,512]{1,2,0:T(8,128)} %get-tuple-element.212, f32[12,512]{1,0:T(8,128)S(1)} %get-tuple-element.211, f32[12,512,512]{1,2,0:T(8,128)S(1)} %bitcast.349, f32[12,512]{1,0:T(8,128)S(1)} %copy-done.32), kind=kLoop, calls=%fused_computation.2 | loop fusion | flops 12582912 | bytes 31506432 | tf_op jit(solution)/shard_map/convert_element_type | solution.py:393
  247.1 2.0 multiply_convert_fusion.1
  249.3 2.0 fusion.123
  251.4 2.0 fusion.125
  253.4 2.0 fusion.127
  255.5 3.5 add_bitcast_fusion
  264.0 1.6 maximum_bitcast_fusion.6
  265.5 1.6 maximum_bitcast_fusion.4
  278.7 6.4 %pad_maximum_fusion.gin = bf16[3,4,768,768]{3,2,1,0:T(8,128)(2,1)} fusion(bf16[1,4,768,768]{3,2,1,0:T(8,128)(2,1)S(1)} %maximum_bitcast_fusion.2, bf16[1,4,768,768]{3,2,1,0:T(8,128)(2,1)S(1)} %get-tuple-element.237, bf16[1,4,768,768]{3,2,1,0:T(8,128)(2,1)S(1)} %get-tuple-element.236), kind=kLoop, calls=%fused_computation.1 | loop fusion | flops 14155776 | bytes 28311552 | tf_op jit(solution)/shard_map/stack | solution.py:413
  288.0 116.4 %shard_map.314 = (bf16[3,768,768]{2,1,0:T(8,128)(2,1)}, f32[8,384]{1,0:T(8,128)}) custom-call(bf16[3,4,768,768]{3,2,1,0:T(8,128)(2,1)} %pad_maximum_fusion.gin, f32[4,8,384]{2,1,0:T(8,128)} %bitcast.378), custom_call_target="tpu_custom_call" | custom-call | tf_op jit(solution)/shard_map/pallas_call | solution.py:260
  404.4 2.6 convert_element_type.205
  407.0 2.9 copy-done.2
  415.3 4.9 %slice_bitcast_fusion = (f32[768,768]{1,0:T(8,128)}, f32[768,768]{1,0:T(8,128)}) fusion(f32[3,768,768]{2,1,0:T(8,128)} %copy-done.2), kind=kLoop, calls=%fused_computation.25 | loop fusion | bytes 9437184 | tf_op jit(solution)/shard_map/squeeze | solution.py:436
  (245 shorter events, 43.5 us)
Async XLA Ops:
  0.7 108.1 %copy-start = (s32[4,512]{1,0:T(4,128)S(1)}, s32[4,512]{1,0:T(4,128)}, u32[]{:S(2)}) copy-start(s32[4,512]{1,0:T(4,128)} %param.19) | copy-start | bytes 24580
  0.7 2.4 copy-start.16
  0.7 2.5 copy-start.17
  3.4 1.5 copy-start.6
  6.8 79.1 %copy-start.41 = (f32[768]{0:T(1024)S(1)}, f32[768]{0:T(1024)}, u32[]{:S(2)}) copy-start(f32[768]{0:T(1024)} %param.30) | copy-start | bytes 9220
  6.8 79.1 %copy-start.46 = (f32[192]{0:T(256)S(1)}, f32[192]{0:T(256)}, u32[]{:S(2)}) copy-start(f32[192]{0:T(256)} %param.21) | copy-start | bytes 2308
  6.8 79.1 %copy-start.47 = (f32[192]{0:T(256)S(1)}, f32[192]{0:T(256)}, u32[]{:S(2)}) copy-start(f32[192]{0:T(256)} %param.24) | copy-start | bytes 2308
  6.8 93.5 %copy-start.3 = (bf16[1,512,768]{2,1,0:T(8,128)(2,1)S(1)}, bf16[1,512,768]{2,1,0:T(8,128)(2,1)}, u32[]{:S(2)}) copy-start(bf16[1,512,768]{2,1,0:T(8,128)(2,1)} %param.18) | copy-start | bytes 2359300
  114.2 7.9 %copy-start.18 = (bf16[192,512]{1,0:T(8,128)(2,1)}, bf16[192,512]{1,0:T(8,128)(2,1)S(1)}, u32[]{:S(2)}) copy-start(bf16[192,512]{1,0:T(8,128)(2,1)S(1)} %convolution_convert_fusion.15) | copy-start | bytes 589828
  116.0 6.1 %copy-start.20 = (bf16[192,512]{1,0:T(8,128)(2,1)}, bf16[192,512]{1,0:T(8,128)(2,1)S(1)}, u32[]{:S(2)}) copy-start(bf16[192,512]{1,0:T(8,128)(2,1)S(1)} %convolution_convert_fusion.16) | copy-start | bytes 589828
  117.5 4.6 %copy-start.22 = (bf16[192,512]{1,0:T(8,128)(2,1)}, bf16[192,512]{1,0:T(8,128)(2,1)S(1)}, u32[]{:S(2)}) copy-start(bf16[192,512]{1,0:T(8,128)(2,1)S(1)} %fusion.102) | copy-start | bytes 589828
  119.0 11.6 %copy-start.24 = (bf16[192,512]{1,0:T(8,128)(2,1)}, bf16[192,512]{1,0:T(8,128)(2,1)S(1)}, u32[]{:S(2)}) copy-start(bf16[192,512]{1,0:T(8,128)(2,1)S(1)} %fusion.101) | copy-start | bytes 589828
  120.5 10.1 %copy-start.26 = (bf16[192,512]{1,0:T(8,128)(2,1)}, bf16[192,512]{1,0:T(8,128)(2,1)S(1)}, u32[]{:S(2)}) copy-start(bf16[192,512]{1,0:T(8,128)(2,1)S(1)} %fusion.100) | copy-start | bytes 589828
  122.0 8.6 %copy-start.28 = (bf16[192,512]{1,0:T(8,128)(2,1)}, bf16[192,512]{1,0:T(8,128)(2,1)S(1)}, u32[]{:S(2)}) copy-start(bf16[192,512]{1,0:T(8,128)(2,1)S(1)} %fusion.99) | copy-start | bytes 589828
  130.6 6.2 %copy-start.31 = (f32[12,512]{1,0:T(8,128)}, f32[12,512]{1,0:T(8,128)S(1)}, u32[]{:S(2)}) copy-start(f32[12,512]{1,0:T(8,128)S(1)} %get-tuple-element.200) | copy-start | bytes 73732
  136.8 2.4 copy-start.49
  136.8 2.4 copy-start.48
  141.3 12.1 %slice-start = ((s8[14155776]{0:T(1024)(128)(4,1)}), s8[4194304]{0:T(1024)(128)(4,1)S(1)}, s32[]{:S(2)}) async-start(s8[14155776]{0:T(1024)(128)(4,1)} %bitcast.346), calls=%async_computation | async-start | bytes 8388608
  141.6 47.1 %copy-start.8 = (bf16[512,768]{1,0:T(8,128)(2,1)}, bf16[512,768]{1,0:T(8,128)(2,1)S(1)}, u32[]{:S(2)}) copy-start(bf16[512,768]{1,0:T(8,128)(2,1)S(1)} %fusion.58) | copy-start | bytes 2359300
  141.6 11.8 %slice-start.1 = ((s8[14155776]{0:T(1024)(128)(4,1)}), s8[4194304]{0:T(1024)(128)(4,1)S(1)}, s32[]{:S(2)}) async-start(s8[14155776]{0:T(1024)(128)(4,1)} %bitcast.346), calls=%async_computation.1 | async-start | bytes 8388608
  141.6 11.8 %slice-start.2 = ((s8[14155776]{0:T(1024)(128)(4,1)}), s8[4194304]{0:T(1024)(128)(4,1)S(1)}, s32[]{:S(2)}) async-start(s8[14155776]{0:T(1024)(128)(4,1)} %bitcast.346), calls=%async_computation.2 | async-start | bytes 8388608
  141.6 11.8 %slice-start.3 = ((s8[14155776]{0:T(1024)(128)(4,1)}), s8[1572864]{0:T(1024)(128)(4,1)S(1)}, s32[]{:S(2)}) async-start(s8[14155776]{0:T(1024)(128)(4,1)} %bitcast.346), calls=%async_computation.3 | async-start | bytes 3145728
  153.3 46.3 %copy-start.12 = (bf16[512,768]{1,0:T(8,128)(2,1)}, bf16[512,768]{1,0:T(8,128)(2,1)S(1)}, u32[]{:S(2)}) copy-start(bf16[512,768]{1,0:T(8,128)(2,1)S(1)} %get-tuple-element.107) | copy-start | bytes 2359300
  201.4 1.6 copy-start.40
  207.0 7.2 %copy-start.10 = (bf16[512,768]{1,0:T(8,128)(2,1)}, bf16[512,768]{1,0:T(8,128)(2,1)S(1)}, u32[]{:S(2)}) copy-start(bf16[512,768]{1,0:T(8,128)(2,1)S(1)} %get-tuple-element.127) | copy-start | bytes 2359300
  208.8 8.9 %copy-start.14 = (bf16[512,768]{1,0:T(8,128)(2,1)}, bf16[512,768]{1,0:T(8,128)(2,1)S(1)}, u32[]{:S(2)}) copy-start(bf16[512,768]{1,0:T(8,128)(2,1)S(1)} %get-tuple-element.218) | copy-start | bytes 2359300
  224.8 7.7 %slice-start.4 = ((s8[12582912]{0:T(1024)(128)(4,1)}), s8[4194304]{0:T(1024)(128)(4,1)S(1)}, s32[]{:S(2)}) async-start(s8[12582912]{0:T(1024)(128)(4,1)} %bitcast.348), calls=%async_computation.4 | async-start | bytes 8388608
  224.8 7.7 %slice-start.5 = ((s8[12582912]{0:T(1024)(128)(4,1)}), s8[4194304]{0:T(1024)(128)(4,1)S(1)}, s32[]{:S(2)}) async-start(s8[12582912]{0:T(1024)(128)(4,1)} %bitcast.348), calls=%async_computation.5 | async-start | bytes 8388608
  224.8 8.5 %slice-start.6 = ((s8[12582912]{0:T(1024)(128)(4,1)}), s8[4194304]{0:T(1024)(128)(4,1)S(1)}, s32[]{:S(2)}) async-start(s8[12582912]{0:T(1024)(128)(4,1)} %bitcast.348), calls=%async_computation.6 | async-start | bytes 8388608
  224.8 8.5 %copy-start.54 = (bf16[192,512]{1,0:T(8,128)(2,1)S(1)}, bf16[192,512]{1,0:T(8,128)(2,1)}, u32[]{:S(2)}) copy-start(bf16[192,512]{1,0:T(8,128)(2,1)} %fusion.95) | copy-start | bytes 589828
  232.4 1.5 copy-start.7
  232.4 1.5 copy-start.32
  232.4 1.5 copy-start.51
  232.4 1.6 copy-start.52
  232.4 1.7 copy-start.53
  239.8 6.0 %copy-start.19 = (bf16[192,512]{1,0:T(8,128)(2,1)S(1)}, bf16[192,512]{1,0:T(8,128)(2,1)}, u32[]{:S(2)}) copy-start(bf16[192,512]{1,0:T(8,128)(2,1)} %copy-done.18) | copy-start | bytes 589828
  239.8 6.0 %copy-start.21 = (bf16[192,512]{1,0:T(8,128)(2,1)S(1)}, bf16[192,512]{1,0:T(8,128)(2,1)}, u32[]{:S(2)}) copy-start(bf16[192,512]{1,0:T(8,128)(2,1)} %copy-done.20) | copy-start | bytes 589828
  245.8 1.3 copy-start.23
  245.8 1.3 copy-start.25
  255.5 3.5 copy-start.50
  267.1 1.4 copy-start.13
  271.9 1.4 copy-start.15
  285.1 1.5 copy-start.44
  285.1 1.7 copy-start.43
  285.1 2.1 copy-start.42
  407.0 2.9 copy-start.2
  409.9 1.6 copy-start.34
  415.3 5.5 %copy-start.1 = (s32[4,512]{1,0:T(4,128)S(1)}, s32[4,512]{1,0:T(4,128)}, u32[]{:S(2)}) copy-start(s32[4,512]{1,0:T(4,128)} %param.19) | copy-start | bytes 24580
  (26 other events, 26.7 us)

commit v2 on v0

v2 whole, which is shorter than its diff:
```python
import functools
import math

import jax
import jax.numpy as jnp
from jax import lax
from jax.experimental import pallas as pl
from jax.experimental.pallas import tpu as pltpu
from jax.sharding import PartitionSpec as P

HEAD_DIM = 64
TEXTS = 8
TEXT_MOST = 128
PLANE = 8
CHIPS = 4
LANES = 128
TILE = 256
MESH = pl.DeviceIdType.MESH
F32 = jnp.float32
BF16 = jnp.bfloat16
QKVO, UP, DOWN = 0, 1, 2
ERFC_STEP = 0.43
ERFC_POLY = (
    0.24251981500369507,
    0.24429385145717694,
    0.2054723295686731,
    0.24508130662046312,
    -0.0823056340674522,
    0.3798888788682746,
    -0.3080966384375393,
    0.07314607841870144,
)


class Place:
    def __init__(self, n_t):
        bi = lax.axis_index("batch")
        self.t = lax.axis_index("tensor")
        self.n_t = n_t
        self.r = lax.rem(bi, PLANE)
        self.base = bi - self.r
        self.c = lax.rem(self.r, 2)
        self.q = self.r // 2
        self.x = lax.rem(self.q, 2)
        self.y = self.q // 2

    def z(self, step):
        return {"batch": self.base + self.r, "tensor": lax.rem(self.t + step, self.n_t)}

    def other(self, axis):
        if isinstance(axis, int) and axis == 2:
            return (1 - self.y) * 2 + 1 - self.x
        over_x = self.y * 2 + 1 - self.x
        over_y = (1 - self.y) * 2 + self.x
        return over_x * (1 - axis) + over_y * axis

    def chip(self, axis):
        return {"batch": self.base + self.other(axis) * 2 + self.c, "tensor": self.t}

    def sibling(self):
        return {"batch": self.base + self.q * 2 + 1 - self.c, "tensor": self.t}

    def greet(self):
        barrier = pltpu.get_barrier_semaphore()
        peers = [self.z(s) for s in range(1, self.n_t)]
        peers += [self.chip(j) for j in range(3)] + [self.sibling()]
        for peer in peers:
            pl.semaphore_signal(barrier, inc=1, device_id=peer, device_id_type=MESH)
        pl.semaphore_wait(barrier, len(peers))


def remote(src, dst, send, recv, dev):
    return pltpu.make_async_remote_copy(
        src_ref=src, dst_ref=dst, send_sem=send, recv_sem=recv, device_id=dev, device_id_type=MESH
    )


def span(start, size):
    return pl.ds(start if isinstance(start, int) else pl.multiple_of(start, size), size)


def nn(left, right):
    return jnp.dot(left, right, preferred_element_type=F32)


def nt(left, right):
    return lax.dot_general(left, right, (((1,), (1,)), ((), ())), preferred_element_type=F32)


def tn(left, right):
    return lax.dot_general(left, right, (((0,), (0,)), ((), ())), preferred_element_type=F32)


def gelu_both(x):
    t = 1.0 / (1.0 + (ERFC_STEP * math.sqrt(0.5)) * jnp.abs(x))
    poly = jnp.full_like(x, ERFC_POLY[-1])
    for c in ERFC_POLY[-2::-1]:
        poly = poly * t + c
    bell = jnp.exp(x * x * -0.5)
    tail = 0.5 * (poly * t) * bell
    cdf = jnp.where(x > 0, 1.0 - tail, tail)
    return x * cdf, cdf + x * (bell * (1.0 / math.sqrt(2.0 * math.pi)))


def layer_kernel(
    n_t,
    wl, x, dy, segc, segr, vecs, bloc,
    layer_out, pooled, acc, fout, vout,
    w, g, a, b, d, qkv, ctx, dctx, prob, act, dg, h1, dlow, work, tr, dsc, n1, near, bias, rstd,
    sums, vsum, va, vb, vd,
    ls, zs, zr, xs, xr, rs, rr, ss, sr, cs, cr,
    r1s, r1r, r2s, r2r, r3s, r3r, r4s, r4r, r5s, r5r, vs, vr,
):
    me = Place(n_t)
    length, width = x.shape
    rows = w.shape[2]
    heads = 3
    ch, half = rows // PLANE, rows // 2
    mine = span((me.c * CHIPS + me.q) * ch, ch)
    my_half = span(me.c * half, half)
    blocks = length // LANES
    far = n_t - 1

    def came(s):
        return lax.rem(me.t + far - s, n_t)

    def goes(s):
        return lax.rem(me.t + 1 + s, n_t)

    def local(k):
        return pltpu.make_async_copy(wl.at[k], w.at[k, me.t], ls.at[k])

    def zcopy(k, s):
        place = w.at[k, me.t, mine]
        return remote(place, place, zs.at[k, s], zr.at[k, s], me.z(s + 1))

    def xcopy(k, s, j):
        place = w.at[k, came(s), mine]
        return remote(place, place, xs.at[k, s, j], xr.at[k, s, j], me.chip(j))

    def relay(k, s, j):
        start = (me.c * CHIPS + me.other(j)) * ch + j * (ch // 2)
        place = w.at[k, came(s), span(start, ch // 2)]
        return remote(place, place, rs.at[k, s, j], rr.at[k, s, j], me.chip(1 - j))

    def scopy(k, s):
        place = w.at[k, came(s), my_half]
        return remote(place, place, ss.at[k, s], sr.at[k, s], me.sibling())

    def bcopy(s):
        return remote(bloc, near.at[me.t], cs.at[s], cr.at[s], me.z(s + 1))

    def on_z(k, s):
        zcopy(k, s).wait_recv()
        for j in range(2):
            xcopy(k, s, j).start()

    def on_xy(k, s):
        for j in range(2):
            xcopy(k, s, j).wait_recv()
            relay(k, s, j).start()

    def on_relay(k, s):
        for j in range(2):
            relay(k, s, j).wait_recv()
        scopy(k, s).start()

    def slot(k):
        return 1 if k == 1 else 0

    def inbox(k):
        return act if k == 2 else a.at[k]

    def r1(k, s):
        return remote(
            g.at[slot(k), s, span((1 - me.c) * half, half)],
            inbox(k).at[s, span(0, half)], r1s.at[k, s], r1r.at[k, s], me.sibling(),
        )

    def quarter(q):
        return span(me.c * half + q * ch, ch)

    def turn(s):
        return lax.rem(jnp.int32(s), 2)

    def r2(k, s, j):
        first = turn(s)
        if j == 0:
            return remote(
                g.at[slot(k), s, quarter(me.other(first))], b.at[slot(k), s, 0],
                r2s.at[k, s, 0], r2r.at[k, s, 0], me.chip(first),
            )
        if j == 1:
            return remote(
                g.at[slot(k), s, quarter(me.other(2))], b.at[slot(k), s, 1],
                r2s.at[k, s, 1], r2r.at[k, s, 1], me.chip(first),
            )
        return remote(
            g.at[slot(k), s, quarter(me.other(1 - first))], b.at[slot(k), s, 2],
            r2s.at[k, s, 2], r2r.at[k, s, 2], me.chip(1 - first),
        )

    def r3(k, s):
        return remote(b.at[slot(k), s, 0], d.at[k, s], r3s.at[k, s], r3r.at[k, s], me.z(s + 1))

    def r4(k, j):
        place = fout.at[k, mine]
        return remote(place, place, r4s.at[k, j], r4r.at[k, j], me.chip(j))

    def r5(k):
        place = fout.at[k, my_half]
        return remote(place, place, r5s.at[k], r5r.at[k], me.sibling())

    def on_r1(k, s):
        r1(k, s).wait_recv()

        @pl.loop(0, half // 64)
        def _(m):
            src = span(me.c * half + m * 64, 64)
            got = inbox(k)[s, span(m * 64, 64)].astype(F32)
            g[slot(k), s, src] = (g[slot(k), s, src].astype(F32) + got).astype(BF16)

        r2(k, s, 0).start()
        r2(k, s, 1).start()

    def on_r2(k, s):
        first = turn(s)
        r2(k, s, 0).wait_recv()
        r2(k, s, 1).wait_recv()
        away = quarter(me.other(1 - first))
        keep = quarter(me.q)
        g[slot(k), s, away] = (
            g[slot(k), s, away].astype(F32) + b[slot(k), s, 1].astype(F32)
        ).astype(BF16)
        r2(k, s, 2).start()
        g[slot(k), s, keep] = (
            g[slot(k), s, keep].astype(F32) + b[slot(k), s, 0].astype(F32)
        ).astype(BF16)

    def on_r2b(k, s, last):
        r2(k, s, 2).wait_recv()
        b[slot(k), s, 0] = (
            g[slot(k), s, quarter(me.q)].astype(F32) + b[slot(k), s, 2].astype(F32)
        ).astype(BF16)
        if last is None:

            @pl.when(s < far)
            def _():
                r3(k, s).start()

        elif not last:
            r3(k, s).start()

    def on_r3(k):
        total = b[slot(k), far, 0].astype(F32)
        for s in range(far):
            r3(k, s).wait_recv()
            total = total + d[k, s].astype(F32)
        for s in range(far):
            r3(k, s).wait_send()
        fout[k, mine] = total.astype(BF16)
        for j in range(3):
            r4(k, j).start()

    def on_r4(k):
        for j in range(3):
            r4(k, j).wait_recv()
        r5(k).start()

    low_lanes = lax.broadcasted_iota(jnp.int32, (1, LANES), 1) < HEAD_DIM
    low = jnp.where(low_lanes, 1.0, 0.0).astype(BF16)
    high = jnp.where(low_lanes, 0.0, 1.0).astype(BF16)
    low32 = jnp.where(low_lanes, 1.0, 0.0)
    high32 = jnp.where(low_lanes, 0.0, 1.0)

    def band(i):
        lo = max(0, i * LANES - TEXT_MOST)
        return lo, min(length, (i + 1) * LANES + TEXT_MOST)

    def project(tt):
        @pl.loop(0, length // TILE)
        def _(m):
            r = span(m * TILE, TILE)
            xm = x[r, :]
            for lo, hi in ((0, 256), (256, 512), (512, 640)):
                piece = nn(xm, w[QKVO, tt, :, lo:hi])
                qkv[tt, r, lo:hi] = (
                    (piece + near[tt, 1:2, lo:hi]) * near[tt, 2:3, lo:hi]
                ).astype(BF16)

    def attend(tt):
        for i in range(blocks):
            lo, hi = band(i)
            r = slice(i * LANES, (i + 1) * LANES)
            heads_in = (
                (qkv[tt, r, 0:128] * low, 128, 256),
                (qkv[tt, r, 0:128] * high, 128, 256),
                (qkv[tt, r, 384:512] * low, 512, 384),
            )
            outs = []
            for h, (q, kc, vc) in enumerate(heads_in):
                s = nt(q, qkv[tt, lo:hi, kc : kc + LANES]) + bias[r, 0 : hi - lo]
                e = jnp.exp(s - jnp.max(s, axis=-1, keepdims=True))
                p = (e * (1.0 / jnp.sum(e, axis=-1, keepdims=True))).astype(BF16)
                prob[tt, h, r, 0 : hi - lo] = p
                outs.append(nn(p, qkv[tt, lo:hi, vc : vc + LANES]))
            ctx[tt, r, 0:128] = (outs[2] * high32).astype(BF16)
            ctx[tt, r, 128:256] = (outs[0] * low32 + outs[1] * high32).astype(BF16)

    def attend_back(tt):
        for group in range(2):
            if group == 0:
                qc, kc, vc, dc = 0, 128, 256, 128
                hs = ((0, low, low, low32), (1, high, high, high32))
            else:
                qc, kc, vc, dc = 384, 512, 384, 0
                hs = ((2, low, high, low32),)
            dq = [None] * blocks
            for i in range(blocks):
                lo, hi = band(i)
                r = slice(i * LANES, (i + 1) * LANES)
                for n, (h, qm, vm, out_mask) in enumerate(hs):
                    dp = nt(dctx[r, dc : dc + LANES] * vm, qkv[tt, lo:hi, vc : vc + LANES])
                    p = prob[tt, h, r, 0 : hi - lo].astype(F32)
                    pd = p * dp
                    ds = (pd - p * jnp.sum(pd, axis=-1, keepdims=True)).astype(BF16)
                    dsc[n, r, 0 : hi - lo] = ds
                    part = nn(ds, qkv[tt, lo:hi, kc : kc + LANES]) * (
                        out_mask * (1.0 / math.sqrt(HEAD_DIM))
                    )
                    dq[i] = part if dq[i] is None else dq[i] + part
                if group == 0:
                    work[r, 0:128] = dq[i].astype(BF16)
            for j in range(blocks):
                rj = slice(j * LANES, (j + 1) * LANES)
                dk = dv = None
                for i in range(blocks):
                    lo, hi = band(i)
                    if not lo <= j * LANES < hi:
                        continue
                    r = slice(i * LANES, (i + 1) * LANES)
                    at = slice(j * LANES - lo, (j + 1) * LANES - lo)
                    for n, (h, qm, vm, _) in enumerate(hs):
                        more = tn(dsc[n, r, at], qkv[tt, r, qc : qc + LANES] * qm)
                        dk = more if dk is None else dk + more
                        more = tn(prob[tt, h, r, at], dctx[r, dc : dc + LANES] * vm)
                        dv = more if dv is None else dv + more
                if group == 0:
                    work[rj, 128:256] = dk.astype(BF16)
                    work[rj, 256:384] = dv.astype(BF16)
                else:
                    work[rj, 384:512] = (dq[j] + dv).astype(BF16)
                    work[rj, 512:640] = dk.astype(BF16)

    def add_sum(k, tile):
        n = tile.shape[0] // 8
        sums[k] += jnp.sum(tile.reshape(n, 8, tile.shape[1]), axis=0)

    def transpose_to(src):
        @pl.loop(0, rows // TILE)
        def _(m):
            cols = span(m * TILE, TILE)
            tr[cols, :] = src[:, cols].T

    for k in range(3):
        local(k).start()
    dy_in = pltpu.make_async_copy(dy, work, ls.at[3])
    dy_in.start()
    me.greet()
    for s in range(far):
        bcopy(s).start()
    for k in range(3):
        local(k).wait()
        for s in range(far):
            zcopy(k, s).start()
    near[me.t] = bloc[...]
    sums[...] = jnp.zeros_like(sums)
    for i in range(blocks):
        lo, hi = band(i)
        r = slice(i * LANES, (i + 1) * LANES)
        bias[r, 0 : hi - lo] = jnp.where(segc[r, :] == segr[0:1, lo:hi], 0.0, -1000000000.0)
    project(me.t)
    for s in range(far):
        on_z(QKVO, s)
    for s in range(far):
        bcopy(s).wait_recv()
    on_xy(QKVO, 0)
    attend(me.t)
    on_xy(QKVO, 1)
    on_relay(QKVO, 0)
    on_xy(QKVO, 2)

    @pl.loop(0, far)
    def _(s):
        tt = came(s)
        on_z(UP, s)
        scopy(QKVO, s).wait_recv()
        project(tt)

        @pl.when(s < far - 1)
        def _():
            on_relay(QKVO, s + 1)

        attend(tt)

        @pl.when(s > 0)
        def _():
            on_xy(UP, s - 1)

    on_xy(UP, far - 1)
    for s in range(far):
        on_z(DOWN, s)

    @pl.loop(0, length // TILE)
    def _(m):
        r = span(m * TILE, TILE)
        for n in range(width // TILE):
            c = slice(n * TILE, (n + 1) * TILE)
            out = x[r, c].astype(F32) + vecs[0:1, c]
            for t in range(n_t):
                out = out + nt(ctx[t, r, :], w[QKVO, t, c, 512:768])
            acc[r, c] = out

    on_relay(UP, 0)

    @pl.loop(0, length // 32)
    def _(m):
        r = span(m * 32, 32)
        center = acc[r, :]
        center = center - jnp.mean(center, axis=-1, keepdims=True)
        inv = lax.rsqrt(jnp.mean(center * center, axis=-1, keepdims=True) + 1e-12)
        rstd[r, :] = inv
        center = center * inv
        n1[r, :] = center
        h1[r, :] = (center * vecs[1:2, :] + vecs[2:3, :]).astype(BF16)

    def rise(tt):
        @pl.loop(0, length // TILE)
        def _(m):
            r = span(m * TILE, TILE)
            hm = h1[r, :]
            for n in range(rows // TILE):
                c = slice(n * TILE, (n + 1) * TILE)
                up, slope = gelu_both(nn(hm, w[UP, tt, :, c]) + near[tt, 0:1, c])
                act[tt, r, c] = up.astype(BF16)
                dg[tt, r, c] = slope.astype(BF16)

    def fall(tt, first):
        @pl.loop(0, length // TILE)
        def _(m):
            r = span(m * TILE, TILE)
            am = act[tt, r, :]
            for n in range(width // TILE):
                c = slice(n * TILE, (n + 1) * TILE)
                out = nn(am, w[DOWN, tt, :, c])
                acc[r, c] = out if first else acc[r, c] + out

    rise(me.t)
    on_relay(UP, 1)

    @pl.loop(0, far)
    def _(s):
        scopy(UP, s).wait_recv()
        on_xy(DOWN, s)
        rise(came(s))

        @pl.when(s == 0)
        def _():
            on_relay(UP, far - 1)

    on_relay(DOWN, 0)
    fall(me.t, True)

    @pl.loop(0, far)
    def _(s):
        @pl.when(s < far - 1)
        def _():
            on_relay(DOWN, s + 1)

        scopy(DOWN, s).wait_recv()
        fall(came(s), False)

    dy_in.wait()

    @pl.loop(0, length // 32)
    def _(m):
        r = span(m * 32, 32)
        center = acc[r, :] + vecs[3:4, :] + (n1[r, :] * vecs[1:2, :] + vecs[2:3, :])
        center = center - jnp.mean(center, axis=-1, keepdims=True)
        inv = lax.rsqrt(jnp.mean(center * center, axis=-1, keepdims=True) + 1e-12)
        n2 = center * inv
        final = n2 * vecs[4:5, :] + vecs[5:6, :]
        out = final.astype(BF16)
        g[1, 0, r, :] = out
        g[1, 1, r, :] = (final - out.astype(F32)).astype(BF16)
        dyt = work[r, :].astype(F32)
        dn = dyt * vecs[4:5, :]
        dyn = dyt * n2
        add_sum(1, dyn)
        add_sum(2, dyt)
        dr = inv * (
            dn
            - jnp.mean(dn, axis=-1, keepdims=True)
            - n2 * jnp.mean(dn * n2, axis=-1, keepdims=True)
        )
        add_sum(0, dr)
        acc[r, :] = dr
        dlow[r, :] = dr.astype(BF16)

    to_out = pltpu.make_async_copy(g.at[1, 0, span(0, length)], layer_out, ls.at[4])
    to_out.start()
    labels = lax.broadcasted_iota(jnp.int32, (TEXTS, length), 0)
    member = jnp.where(segr[0:1, :] == labels, 1.0, 0.0)
    counts = jnp.sum(member, axis=-1, keepdims=True)
    member = member.astype(BF16)
    pooled[...] = (nn(member, g[1, 0, 0:length, :]) + nn(member, g[1, 1, 0:length, :])) / counts

    ones = jnp.ones((8, length), BF16)

    def grad_to(k, s, left_t, right):
        @pl.loop(0, rows // TILE)
        def _(m):
            r = span(m * TILE, TILE)
            lt = left_t(r)
            for n in range(width // TILE):
                c = slice(n * TILE, (n + 1) * TILE)
                g[k, s, r, c] = nn(lt, right[:, c]).astype(BF16)

    @pl.loop(0, n_t)
    def _(s):
        tt = goes(s)
        grad_to(0, s, lambda r: act[tt, :, r].T, dlow)
        r1(0, s).start()

    to_out.wait()
    transpose_to(h1)

    @pl.loop(0, n_t)
    def _(s):
        tt = goes(s)
        on_r1(0, s)

        @pl.loop(0, length // TILE)
        def _(m):
            r = span(m * TILE, TILE)
            dm = dlow[r, :]
            for n in range(rows // TILE):
                c = slice(n * TILE, (n + 1) * TILE)
                work[r, c] = (nt(dm, w[DOWN, tt, c, :]) * dg[tt, r, c].astype(F32)).astype(BF16)

        @pl.when(s > 0)
        def _():
            on_r2(0, s - 1)

        grad_to(1, s, lambda r: tr[r, :], work)
        r1(1, s).start()

        @pl.loop(0, length // TILE)
        def _(m):
            r = span(m * TILE, TILE)
            dm = work[r, :]
            for n in range(width // TILE):
                c = slice(n * TILE, (n + 1) * TILE)
                acc[r, c] += nt(dm, w[UP, tt, c, :])

        vsum[pl.ds(8 + tt, 1), :] = nn(ones, work[...])[0:1, :]

    on_r2(0, far)

    @pl.loop(0, length // 32)
    def _(m):
        r = span(m * 32, 32)
        dh, nt1 = acc[r, :], n1[r, :]
        add_sum(4, dh * nt1)
        add_sum(5, dh)
        dn = dh * vecs[1:2, :]
        dr = rstd[r, :] * (
            dn
            - jnp.mean(dn, axis=-1, keepdims=True)
            - nt1 * jnp.mean(dn * nt1, axis=-1, keepdims=True)
        )
        add_sum(3, dr)
        acc[r, :] = dr
        dlow[r, :] = dr.astype(BF16)

    for s in range(n_t):
        on_r2b(0, s, s == far)
    transpose_to(dlow)
    for k, row in ((3, 0), (4, 1), (5, 2), (0, 3), (1, 4), (2, 5)):
        vsum[row : row + 1, :] = jnp.sum(sums[k], axis=0, keepdims=True)
    vsum[6:8, :] = jnp.zeros((2, width), F32)
    work[:, 640:768] = jnp.zeros((length, LANES), BF16)

    @pl.loop(0, n_t)
    def _(s):
        tt = goes(s)
        on_r1(1, s)

        @pl.loop(0, length // TILE)
        def _(m):
            r = span(m * TILE, TILE)
            out = nn(dlow[r, :], w[QKVO, tt, :, 512:768])
            dctx[r, 0:128] = (out[:, 0:128] * high32).astype(BF16)
            dctx[r, 128:256] = out[:, 128:256].astype(BF16)

        @pl.when(s == 1)
        def _():
            on_r3(0)

        @pl.when(s == 2)
        def _():
            on_r4(0)

        attend_back(tt)

        @pl.when(s > 0)
        def _():
            on_r2(1, s - 1)

        r1(0, s).wait_send()
        for j in range(3):
            r2(0, s, j).wait_send()

        @pl.loop(0, rows // TILE)
        def _(m):
            r = span(m * TILE, TILE)
            lt = x[:, r].T
            g[0, s, r, 0:256] = nn(lt, work[:, 0:256]).astype(BF16)
            g[0, s, r, 256:512] = nn(lt, work[:, 256:512]).astype(BF16)
            g[0, s, r, 512:768] = (nn(lt, work[:, 512:768]) + nn(tr[r, :], ctx[tt])).astype(BF16)

        r1(2, s).start()

        @pl.loop(0, length // TILE)
        def _(m):
            r = span(m * TILE, TILE)
            dm = work[r, 0:640]
            for n in range(width // TILE):
                c = slice(n * TILE, (n + 1) * TILE)
                acc[r, c] += nt(dm, w[QKVO, tt, c, 0:640])

        vsum[pl.ds(12 + tt, 1), :] = nn(ones, work[...])[0:1, :]

    v1 = remote(vsum, va, vs.at[0], vr.at[0], me.sibling())
    v1.start()
    on_r2(1, far)
    for s in range(n_t):
        on_r1(2, s)
    v1.wait()
    vsum[...] = vsum[...] + va[...]
    v2 = [remote(vsum, vb.at[j], vs.at[1 + j], vr.at[1 + j], me.chip(j)) for j in range(3)]
    for c in v2:
        c.start()
    for s in range(n_t):
        on_r2b(1, s, s == far)
    for s in range(n_t):
        on_r2(2, s)
    for c in v2:
        c.wait()
    va[...] = vsum[...] + vb[0] + vb[1] + vb[2]
    v3 = [remote(va, vd.at[s], vs.at[4 + s], vr.at[4 + s], me.z(s + 1)) for s in range(far)]
    for c in v3:
        c.start()
    on_r3(1)
    for s in range(n_t):
        on_r2b(2, s, s == far)
    on_r4(1)
    on_r3(2)
    for c in v3:
        c.wait()
    total = va[...]
    for s in range(far):
        total = total + vd[s]
    vout[...] = total
    on_r4(2)
    for k in range(3):
        r5(k).wait_recv()

    for s in range(far):
        bcopy(s).wait_send()
    for k in range(3):
        for s in range(far):
            zcopy(k, s).wait_send()
            scopy(k, s).wait_send()
            for j in range(2):
                xcopy(k, s, j).wait_send()
                relay(k, s, j).wait_send()
        for s in range(n_t):
            if k > 0:
                r1(k, s).wait_send()
                for j in range(3):
                    r2(k, s, j).wait_send()
        for j in range(3):
            r4(k, j).wait_send()
        r5(k).wait_send()


def run_layer(wl, x, dy, segc, segr, vecs, bloc, n_t):
    groups, rows, cols = wl.shape
    length, width = x.shape
    ch, half, far = rows // PLANE, rows // 2, n_t - 1
    dma, vmem = pltpu.SemaphoreType.DMA, pltpu.VMEM
    here, there = pl.BlockSpec(memory_space=vmem), pl.BlockSpec(memory_space=pl.ANY)
    shape = jax.ShapeDtypeStruct
    pair = lambda *dims: [dma(dims), dma(dims)]
    return pl.pallas_call(
        functools.partial(layer_kernel, n_t),
        out_shape=(
            shape((length, width), BF16),
            shape((TEXTS, width), F32),
            shape((length, width), F32),
            shape((groups, rows, cols), BF16),
            shape((16, width), F32),
        ),
        in_specs=[there, here, there, here, here, here, here],
        out_specs=[there, here, here, here, here],
        scratch_shapes=[
            vmem((groups, n_t, rows, cols), BF16),
            vmem((2, n_t, rows, cols), BF16),
            vmem((2, n_t, half, cols), BF16),
            vmem((2, n_t, 3, ch, cols), BF16),
            vmem((groups, far, ch, cols), BF16),
            vmem((n_t, length, 640), BF16),
            vmem((n_t, length, 256), BF16),
            vmem((length, 256), BF16),
            vmem((n_t, 3, length, 384), BF16),
            vmem((n_t, length, rows), BF16),
            vmem((n_t, length, rows), BF16),
            vmem((length, width), BF16),
            vmem((length, width), BF16),
            vmem((length, width), BF16),
            vmem((width, length), BF16),
            vmem((2, length, 384), BF16),
            vmem((length, width), F32),
            vmem((n_t, 8, width), F32),
            vmem((length, 384), F32),
            vmem((length, 1), F32),
            vmem((6, 8, width), F32),
            vmem((16, width), F32),
            vmem((16, width), F32),
            vmem((3, 16, width), F32),
            vmem((far, 16, width), F32),
            dma((5,)),
            *pair(groups, far),
            *pair(groups, far, 2),
            *pair(groups, far, 2),
            *pair(groups, far),
            *pair(far),
            *pair(groups, n_t),
            *pair(groups, n_t, 3),
            *pair(groups, far),
            *pair(groups, 3),
            *pair(groups),
            *pair(4 + far),
        ],
        compiler_params=pltpu.CompilerParams(
            collective_id=1, has_side_effects=True, vmem_limit_bytes=67043328
        ),
    )(wl, x, dy, segc, segr, vecs, bloc)


def per_device(
    n_t, n_b,
    hidden_in, segment_ids, query_weight, query_bias, key_weight, value_weight, value_bias,
    out_weight, out_bias, attn_gain, attn_shift, up_weight, up_bias, down_weight, down_bias,
    ffn_gain, ffn_shift, cotangent,
):
    x = hidden_in[0]
    width, inner = query_weight.shape
    two = 2 * HEAD_DIM
    t = lax.axis_index("tensor")
    wo = out_weight.T
    qkvo = jnp.concatenate(
        [
            query_weight[:, :two], key_weight[:, :two], value_weight[:, :two],
            query_weight[:, two:], value_weight[:, two:], key_weight[:, two:],
            wo[:, two:], wo[:, :two],
        ],
        axis=1,
    )
    wl = jnp.stack([qkvo, up_weight, down_weight])
    none = jnp.zeros((two,), F32)
    scale = 1.0 / math.sqrt(HEAD_DIM)
    bias_row = jnp.concatenate(
        [query_bias[:two], none, value_bias[:two], query_bias[two:], value_bias[two:], none, none]
    )
    full = jnp.ones((HEAD_DIM,), F32)
    down = full * scale
    scale_row = jnp.concatenate([down, down] + [full] * 4 + [down] + [full] * 5)
    bloc = jnp.concatenate(
        [jnp.stack([up_bias, bias_row, scale_row]), jnp.zeros((5, width), F32)], axis=0
    )
    vecs = jnp.stack(
        [out_bias, attn_gain, attn_shift, down_bias, ffn_gain, ffn_shift, out_bias, out_bias]
    )
    seg = lax.dynamic_slice_in_dim(segment_ids, t, 1, 0)[0]
    segr = jnp.broadcast_to(seg[None, :], (8, seg.shape[0]))
    final, pooled, dx, fout, vout = run_layer(
        wl, x, cotangent[0], seg[:, None], segr, vecs, bloc, n_t
    )
    if n_b > PLANE:
        apart = [[i + PLANE * j for j in range(n_b // PLANE)] for i in range(PLANE)]
        fout, vout = lax.psum((fout.astype(F32), vout), "batch", axis_index_groups=apart)
    gq = fout[2].astype(F32)
    here = lax.dynamic_slice_in_dim(vout, t * inner, inner, 1)
    dub = lax.dynamic_slice_in_dim(vout, 8 + t, 1, 0)[0]
    dqb = lax.dynamic_slice_in_dim(vout, 12 + t, 1, 0)[0]
    h = HEAD_DIM
    return (
        final[None],
        pooled[None],
        dx[None],
        jnp.concatenate([gq[:, :two], gq[:, 6 * h : 7 * h]], axis=1),
        jnp.concatenate([dqb[:two], dqb[6 * h : 7 * h]]),
        jnp.concatenate([gq[:, two : 2 * two], gq[:, 8 * h : 9 * h]], axis=1),
        jnp.concatenate([gq[:, 2 * two : 3 * two], gq[:, 7 * h : 8 * h]], axis=1),
        jnp.concatenate([dqb[2 * two : 3 * two], dqb[7 * h : 8 * h]]),
        jnp.concatenate([gq[:, 10 * h :], gq[:, 9 * h : 10 * h]], axis=1).T,
        here[0],
        here[1],
        here[2],
        fout[1].astype(F32),
        dub,
        fout[0].astype(F32),
        here[3],
        here[4],
        here[5],
    )


def solution(mesh):
    rows, tens = P(("batch", "tensor"), None, None), P("tensor")
    col, row = P(None, "tensor"), P("tensor", None)
    in_specs = (
        rows, P("batch", None), col, tens, col, col, tens, row, P(), P(), P(), col, tens, row,
        P(), P(), P(), rows,
    )
    out_specs = (
        rows, rows, rows, col, tens, col, col, tens, row, tens, tens, tens, col, tens, row, tens,
        tens, tens,
    )
    body = functools.partial(per_device, mesh.shape["tensor"], mesh.shape["batch"])
    return jax.shard_map(
        body, mesh=mesh, in_specs=in_specs, out_specs=out_specs, check_vma=False
    )
```

time: 935 us -> 240 us (0.26)
  waiting for transfers between devices: 710 us -> 0 us
  Pallas kernels: 0 us -> 192 us
  matrix products: 112 us -> 0 us
  blocking collectives: 25.1 us -> 0 us
  other arithmetic: 30.5 us -> 8.72 us
  between operations: 15 us -> 0.79 us
    reduce_scatter x4 -> x0, waiting for transfers between devices: 337 us -> none  [the longest x1 110 us: per_device(): lax.psum_scatter(partial_ffn, 'tensor', scatter_dimension=0, tiled=True)]
    all_gather x4 -> x0, waiting for transfers between devices: 258 us -> none  [the longest x1 67.8 us: per_device(): gathered = lax.all_gather(hidden_in, 'tensor', axis=0, tiled=True)]
    pallas_call x0 -> x1, Pallas kernels: none -> 192 us  [run_layer(): pl.pallas_call(functools.partial(layer_kernel, n_t), out_shape=(shape((le...]
    psum x1 -> x0, waiting for transfers between devices: 115 us -> none  [per_device(): lax.psum((grad_query, grad_query_bias, grad_key, grad_value, grad_value_b...]
    dot_general x47 -> x0, matrix products: 112 us -> none  [the longest x6 37.1 us: product(): return jnp.dot(left, right, preferred_element_type=jnp.float32)]
    psum x1 -> x0, blocking collectives: 25.1 us -> none  [per_device(): lax.psum((grad_query, grad_query_bias, grad_key, grad_value, grad_value_b...]
    reduce_sum x17 -> x0, other arithmetic: 18.1 us -> none  [the longest x4 6.23 us: normalize(): center = resid - jnp.mean(resid, axis=-1, keepdims=True)]
    slice x1 -> x19, local copies, waits for them, and re-layouts: 0.59 us -> 11.4 us  [the longest x1 1.58 us: per_device(): here[5]]
  transfers between devices with their start and end apart: 10 -> 0, of which waited for: 9 -> 0; matrix products, arithmetic and copies ran while one was open for 8% -> 0% of each run, Pallas kernels for 0% -> 0%
where the time goes in v2:
time: 240 us; the launch traced here: 238 us
  Pallas kernels  192 us (80%)
  local copies, waits for them, and re-layouts  36.8 us (15%)
  other arithmetic  8.72 us (4%)
    pallas_call x1, Pallas kernels, run_layer(): pl.pallas_call(functools.partial(layer_kernel, n_t), out_shape=(shape((le...  192 us
    unnamed x24, local copies, waits for them, and re-layouts  13.2 us

profile of v2, /device:TPU:0, one launch (start us, length us, event | category | flops | bytes accessed | tf_op | source)
XLA Modules:
  0.0 238.2 jit_solution(5423715811316971543)
XLA Ops:
  0.7 0.7 slice.121
  1.4 0.7 slice.119
  2.1 0.7 slice.122
  2.8 0.7 slice.120
  3.7 0.7 fusion.4
  4.4 0.7 constant_dynamic-slice_fusion.2
  5.1 0.7 stack.45
  5.7 0.7 stack.46
  6.4 0.7 stack.47
  7.1 0.7 stack.52
  7.8 0.7 stack.48
  8.5 0.7 stack.49
  9.2 0.7 stack.50
  9.9 0.6 stack.51.vecs
  10.5 0.6 broadcast_in_dim.23.segr
  11.1 1.4 maximum_maximum_fusion.bloc
  12.5 0.9 slice.114
  13.4 0.8 copy.62
  14.2 0.9 slice.116
  15.1 0.8 copy.64
  15.9 0.9 slice.115
  16.8 0.8 copy.63
  17.6 0.9 slice.111
  18.6 0.8 copy.59
  19.4 0.8 copy.60
  20.2 0.8 copy.61
  21.0 0.9 copy.54.segc
  21.9 0.2 copy.53
  22.1 0.7 slice.149
  22.8 0.7 slice.148
  23.4 2.4 %concatenate.30 = bf16[768,768]{1,0:T(8,128)(2,1)S(1)} concatenate(bf16[768,128]{1,0:T(8,128)(2,1)} %copy.59, bf16[768,128]{1,0:T(8,128)(2,1)} %copy.60, bf16[768,128]{1,0:T(8,128)(2,1)} %copy.61, bf16[768,64]{1,0:T(8,128)(2,1)} %copy.62, bf16[768,64]{1,0:T(8,128)(2,1)} %copy.63, bf16[768,64]{1,0:T(8,128)(2,1)} %copy.64, bf16[768,64]{1,0:T(8,128)(2,1)} %slice.148, ...), dimensions={1} | concatenate | bytes 2359296 | tf_op jit(solution)/shard_map/concatenate | solution.py:773
  25.9 2.0 pad_maximum_fusion.wl
  27.8 191.9 %shard_map.313 = (bf16[512,768]{1,0:T(8,128)(2,1)}, f32[8,768]{1,0:T(8,128)}, f32[512,768]{1,0:T(8,128)}, bf16[3,768,768]{2,1,0:T(8,128)(2,1)}, f32[16,768]{1,0:T(8,128)}) custom-call(bf16[3,768,768]{2,1,0:T(8,128)(2,1)} %pad_maximum_fusion.wl, bf16[512,768]{1,0:T(8,128)(2,1)} %bitcast.44, bf16[512,768]{1,0:T(8,128)(2,1)} %bitcast.45, s32[512,1]{1,0:T(8,128)} %copy.54.segc, ...), custom_call_target="tpu_custom_call" | custom-call | tf_op jit(solution)/shard_map/pallas_call | solution.py:706
  219.8 0.8 dynamic-slice_bitcast_fusion
  220.6 0.8 dynamic-slice_bitcast_fusion.1
  221.4 0.6 pad_maximum_fusion.4
  222.0 1.6 fusion.3
  223.6 1.3 dynamic-slice_reduce_fusion
  224.9 4.6 %bitcast_convert_fusion = (f32[768,768]{1,0:T(8,128)}, f32[768,768]{1,0:T(8,128)}, f32[768,768]{1,0:T(8,128)S(1)}) fusion(bf16[3,768,768]{2,1,0:T(8,128)(2,1)} %get-tuple-element.26), kind=kLoop, calls=%fused_computation.1 | loop fusion | flops 1769472 | bytes 10616832 | tf_op jit(solution)/shard_map/convert_element_type | solution.py:824
  229.5 0.3 fusion.2
  229.9 0.1 pad_maximum_fusion.3
  230.0 1.1 copy.57
  231.1 1.1 copy.58
  232.3 1.1 copy.55
  233.3 1.1 copy.56
  234.4 2.1 copy.68
  236.5 0.6 copy.69
  237.1 1.1 copy.70
  (22 shorter events, 0.4 us)
Async XLA Ops:
  0.7 19.6 %slice-start.1 = ((bf16[768,192]{0,1:T(8,128)(2,1)}), bf16[768,128]{0,1:T(8,128)(2,1)S(1)}, s32[]{:S(2)}) async-start(bf16[768,192]{0,1:T(8,128)(2,1)} %param.23), calls=%async_computation.1 | async-start | bytes 393216 | tf_op jit(solution)/shard_map/slice | solution.py:775
  0.7 18.7 %slice-start = ((bf16[768,192]{0,1:T(8,128)(2,1)}), bf16[768,128]{0,1:T(8,128)(2,1)S(1)}, s32[]{:S(2)}) async-start(bf16[768,192]{0,1:T(8,128)(2,1)} %param.22), calls=%async_computation | async-start | bytes 393216 | tf_op jit(solution)/shard_map/slice | solution.py:775
  0.7 21.2 %copy-start.3 = (bf16[192,768]{1,0:T(8,128)(2,1)S(1)}, bf16[192,768]{1,0:T(8,128)(2,1)}, u32[]{:S(2)}) copy-start(bf16[192,768]{1,0:T(8,128)(2,1)} %param.25) | copy-start | bytes 884740
  20.2 5.6 %copy-start.1 = (bf16[768,768]{1,0:T(8,128)(2,1)S(1)}, bf16[768,768]{1,0:T(8,128)(2,1)}, u32[]{:S(2)}) copy-start(bf16[768,768]{1,0:T(8,128)(2,1)} %param.31) | copy-start | bytes 3538948
  20.2 5.6 %copy-start.2 = (bf16[768,768]{1,0:T(8,128)(2,1)S(1)}, bf16[768,768]{1,0:T(8,128)(2,1)}, u32[]{:S(2)}) copy-start(bf16[768,768]{1,0:T(8,128)(2,1)} %param.29) | copy-start | bytes 3538948
  232.2 4.2 %copy-start.4 = (f32[8,768]{1,0:T(8,128)S(1)}, f32[8,768]{1,0:T(8,128)}, u32[]{:S(2)}) copy-start(f32[8,768]{1,0:T(8,128)} %get-tuple-element.24) | copy-start | bytes 73732
  232.3 4.8 %copy-start = (f32[512,768]{1,0:T(8,128)S(1)}, f32[512,768]{1,0:T(8,128)}, u32[]{:S(2)}) copy-start(f32[512,768]{1,0:T(8,128)} %get-tuple-element.25) | copy-start | bytes 4718596

commit v3 on v2

--- a/solution.py
+++ b/solution.py
@@ -48,11 +48,9 @@
         return {"batch": self.base + self.r, "tensor": lax.rem(self.t + step, self.n_t)}
 
     def other(self, axis):
-        if isinstance(axis, int) and axis == 2:
-            return (1 - self.y) * 2 + 1 - self.x
-        over_x = self.y * 2 + 1 - self.x
-        over_y = (1 - self.y) * 2 + self.x
-        return over_x * (1 - axis) + over_y * axis
+        y = self.y if axis == 0 else 1 - self.y
+        x = self.x if axis == 1 else 1 - self.x
+        return y * 2 + x
 
     def chip(self, axis):
         return {"batch": self.base + self.other(axis) * 2 + self.c, "tensor": self.t}
@@ -104,10 +102,10 @@
 
 def layer_kernel(
     n_t,
-    wl, x, dy, segc, segr, vecs, bloc,
+    wq, wk, wv, wo, wup, wdown, x, dy, seg, vecs,
     layer_out, pooled, acc, fout, vout,
-    w, g, a, b, d, qkv, ctx, dctx, prob, act, dg, h1, dlow, work, tr, dsc, n1, near, bias, rstd,
-    sums, vsum, va, vb, vd,
+    w, g, a, b, d, qkv, ctx, dctx, prob, act, dg, h1, dlow, work, tr, dsc, n1, near, bloc, bias,
+    memb, rstd, sums, vsum, va, vb, vd,
     ls, zs, zr, xs, xr, rs, rr, ss, sr, cs, cr,
     r1s, r1r, r2s, r2r, r3s, r3r, r4s, r4r, r5s, r5r, vs, vr,
 ):
@@ -127,8 +125,20 @@
     def goes(s):
         return lax.rem(me.t + 1 + s, n_t)
 
+    pieces = (
+        (wq, 0, 128, 0), (wk, 0, 128, 128), (wv, 0, 128, 256), (wq, 128, 64, 384),
+        (wv, 128, 64, 448), (wk, 128, 64, 512), (wo, 128, 64, 576), (wo, 0, 128, 640),
+    )
+
     def local(k):
-        return pltpu.make_async_copy(wl.at[k], w.at[k, me.t], ls.at[k])
+        if k > 0:
+            return [pltpu.make_async_copy((wup, wdown)[k - 1], w.at[k, me.t], ls.at[7 + k])]
+        return [
+            pltpu.make_async_copy(
+                src.at[pl.ds(at, size)], w.at[0, me.t, pl.ds(to, size)], ls.at[n]
+            )
+            for n, (src, at, size, to) in enumerate(pieces)
+        ]
 
     def zcopy(k, s):
         place = w.at[k, me.t, mine]
@@ -180,24 +190,16 @@
     def quarter(q):
         return span(me.c * half + q * ch, ch)
 
-    def turn(s):
-        return lax.rem(jnp.int32(s), 2)
-
-    def r2(k, s, j):
-        first = turn(s)
-        if j == 0:
-            return remote(
-                g.at[slot(k), s, quarter(me.other(first))], b.at[slot(k), s, 0],
-                r2s.at[k, s, 0], r2r.at[k, s, 0], me.chip(first),
-            )
-        if j == 1:
-            return remote(
-                g.at[slot(k), s, quarter(me.other(2))], b.at[slot(k), s, 1],
-                r2s.at[k, s, 1], r2r.at[k, s, 1], me.chip(first),
-            )
+    cut = ch // 2
+
+    def sub(q, h):
+        return span(me.c * half + q * ch + h * cut, cut)
+
+    def r2(k, s, h, j):
+        source = (me.other(h), me.other(2), me.other(1 - h))[j]
         return remote(
-            g.at[slot(k), s, quarter(me.other(1 - first))], b.at[slot(k), s, 2],
-            r2s.at[k, s, 2], r2r.at[k, s, 2], me.chip(1 - first),
+            g.at[slot(k), s, sub(source, h)], b.at[slot(k), s, j, span(h * cut, cut)],
+            r2s.at[k, s, h, j], r2r.at[k, s, h, j], me.chip(1 - h if j == 2 else h),
         )
 
     def r3(k, s):
@@ -214,34 +216,28 @@
     def on_r1(k, s):
         r1(k, s).wait_recv()
 
-        @pl.loop(0, half // 64)
-        def _(m):
-            src = span(me.c * half + m * 64, 64)
-            got = inbox(k)[s, span(m * 64, 64)].astype(F32)
-            g[slot(k), s, src] = (g[slot(k), s, src].astype(F32) + got).astype(BF16)
-
-        r2(k, s, 0).start()
-        r2(k, s, 1).start()
+        @pl.loop(0, CHIPS)
+        def _(m):
+            src = span(me.c * half + m * ch, ch)
+            g[slot(k), s, src] += inbox(k)[s, span(m * ch, ch)]
+
+        for h in range(2):
+            for j in range(2):
+                r2(k, s, h, j).start()
 
     def on_r2(k, s):
-        first = turn(s)
-        r2(k, s, 0).wait_recv()
-        r2(k, s, 1).wait_recv()
-        away = quarter(me.other(1 - first))
-        keep = quarter(me.q)
-        g[slot(k), s, away] = (
-            g[slot(k), s, away].astype(F32) + b[slot(k), s, 1].astype(F32)
-        ).astype(BF16)
-        r2(k, s, 2).start()
-        g[slot(k), s, keep] = (
-            g[slot(k), s, keep].astype(F32) + b[slot(k), s, 0].astype(F32)
-        ).astype(BF16)
+        for h in range(2):
+            rows_h = span(h * cut, cut)
+            r2(k, s, h, 1).wait_recv()
+            g[slot(k), s, sub(me.other(1 - h), h)] += b[slot(k), s, 1, rows_h]
+            r2(k, s, h, 2).start()
+            r2(k, s, h, 0).wait_recv()
+            g[slot(k), s, sub(me.q, h)] += b[slot(k), s, 0, rows_h]
 
     def on_r2b(k, s, last):
-        r2(k, s, 2).wait_recv()
-        b[slot(k), s, 0] = (
-            g[slot(k), s, quarter(me.q)].astype(F32) + b[slot(k), s, 2].astype(F32)
-        ).astype(BF16)
+        for h in range(2):
+            r2(k, s, h, 2).wait_recv()
+        b[slot(k), s, 0] = g[slot(k), s, quarter(me.q)] + b[slot(k), s, 2]
         if last is None:
 
             @pl.when(s < far)
@@ -283,13 +279,13 @@
             r = span(m * TILE, TILE)
             xm = x[r, :]
             for lo, hi in ((0, 256), (256, 512), (512, 640)):
-                piece = nn(xm, w[QKVO, tt, :, lo:hi])
+                piece = nt(xm, w[QKVO, tt, lo:hi, :])
                 qkv[tt, r, lo:hi] = (
-                    (piece + near[tt, 1:2, lo:hi]) * near[tt, 2:3, lo:hi]
+                    (piece + near[tt, 1:2, lo:hi]) * scales[:, lo:hi]
                 ).astype(BF16)
 
-    def attend(tt):
-        for i in range(blocks):
+    def attend(tt, some=None):
+        for i in some or range(blocks):
             lo, hi = band(i)
             r = slice(i * LANES, (i + 1) * LANES)
             heads_in = (
@@ -356,6 +352,12 @@
         n = tile.shape[0] // 8
         sums[k] += jnp.sum(tile.reshape(n, 8, tile.shape[1]), axis=0)
 
+    def by_tiles(body):
+        @pl.loop(0, length // 64)
+        def _(m):
+            for part in range(4):
+                body(span(m * 64 + part * 16, 16))
+
     def transpose_to(src):
         @pl.loop(0, rows // TILE)
         def _(m):
@@ -363,37 +365,54 @@
             tr[cols, :] = src[:, cols].T
 
     for k in range(3):
-        local(k).start()
-    dy_in = pltpu.make_async_copy(dy, work, ls.at[3])
+        for copy in local(k):
+            copy.start()
+    dy_in = pltpu.make_async_copy(dy, work, ls.at[10])
     dy_in.start()
+    own = vecs[7:8, :]
+    mid, end = own[:, 128:256], own[:, 256:384]
+    turned = jnp.where(low_lanes, pltpu.roll(mid, HEAD_DIM, 1), pltpu.roll(end, HEAD_DIM, 1))
+    bloc[...] = jnp.zeros_like(bloc)
+    bloc[0:1, :] = vecs[6:7, :]
+    bloc[1:2, 0:128] = own[:, 0:128]
+    bloc[1:2, 256:384] = turned
+    bloc[1:2, 384:512] = jnp.where(low_lanes, mid, end)
+    near[me.t] = bloc[...]
     me.greet()
-    for s in range(far):
-        bcopy(s).start()
     for k in range(3):
-        local(k).wait()
+        for copy in local(k):
+            copy.wait()
         for s in range(far):
             zcopy(k, s).start()
-    near[me.t] = bloc[...]
+        if k == 0:
+            for s in range(far):
+                bcopy(s).start()
+    lane = lax.broadcasted_iota(jnp.int32, (1, 640), 1)
+    is_query = (lane < 128) | ((lane >= 384) & (lane < 448))
+    scales = jnp.where(is_query, 1.0 / math.sqrt(HEAD_DIM), 1.0)
     sums[...] = jnp.zeros_like(sums)
+    labels = lax.broadcasted_iota(jnp.int32, (TEXTS, length), 0)
+    memb[...] = jnp.where(seg[pl.ds(me.t, 1), :] == labels, 1.0, 0.0)
     for i in range(blocks):
         lo, hi = band(i)
         r = slice(i * LANES, (i + 1) * LANES)
-        bias[r, 0 : hi - lo] = jnp.where(segc[r, :] == segr[0:1, lo:hi], 0.0, -1000000000.0)
+        bias[r, 0 : hi - lo] = (tn(memb[:, r], memb[:, lo:hi]) - 1.0) * 1000000000.0
     project(me.t)
-    for s in range(far):
-        on_z(QKVO, s)
+    on_z(QKVO, 0)
+    attend(me.t, (0, 1))
+    on_z(QKVO, 1)
+    on_xy(QKVO, 0)
+    attend(me.t, (2, 3))
+    on_z(QKVO, 2)
+    on_xy(QKVO, 1)
+    on_relay(QKVO, 0)
     for s in range(far):
         bcopy(s).wait_recv()
-    on_xy(QKVO, 0)
-    attend(me.t)
-    on_xy(QKVO, 1)
-    on_relay(QKVO, 0)
     on_xy(QKVO, 2)
 
     @pl.loop(0, far)
     def _(s):
         tt = came(s)
-        on_z(UP, s)
         scopy(QKVO, s).wait_recv()
         project(tt)
 
@@ -402,14 +421,11 @@
             on_relay(QKVO, s + 1)
 
         attend(tt)
+        on_z(UP, s)
 
         @pl.when(s > 0)
         def _():
             on_xy(UP, s - 1)
-
-    on_xy(UP, far - 1)
-    for s in range(far):
-        on_z(DOWN, s)
 
     @pl.loop(0, length // TILE)
     def _(m):
@@ -418,14 +434,13 @@
             c = slice(n * TILE, (n + 1) * TILE)
             out = x[r, c].astype(F32) + vecs[0:1, c]
             for t in range(n_t):
-                out = out + nt(ctx[t, r, :], w[QKVO, t, c, 512:768])
+                out = out + nn(ctx[t, r, :], w[QKVO, t, 512:768, c])
             acc[r, c] = out
 
     on_relay(UP, 0)
 
-    @pl.loop(0, length // 32)
-    def _(m):
-        r = span(m * 32, 32)
+    @by_tiles
+    def _(r):
         center = acc[r, :]
         center = center - jnp.mean(center, axis=-1, keepdims=True)
         inv = lax.rsqrt(jnp.mean(center * center, axis=-1, keepdims=True) + 1e-12)
@@ -455,18 +470,23 @@
                 out = nn(am, w[DOWN, tt, :, c])
                 acc[r, c] = out if first else acc[r, c] + out
 
+    on_z(DOWN, 0)
     rise(me.t)
+    on_xy(UP, 2)
     on_relay(UP, 1)
+    on_z(DOWN, 1)
 
     @pl.loop(0, far)
     def _(s):
         scopy(UP, s).wait_recv()
+        rise(came(s))
+
+        @pl.when(s == 0)
+        def _():
+            on_relay(UP, far - 1)
+            on_z(DOWN, far - 1)
+
         on_xy(DOWN, s)
-        rise(came(s))
-
-        @pl.when(s == 0)
-        def _():
-            on_relay(UP, far - 1)
 
     on_relay(DOWN, 0)
     fall(me.t, True)
@@ -482,16 +502,15 @@
 
     dy_in.wait()
 
-    @pl.loop(0, length // 32)
-    def _(m):
-        r = span(m * 32, 32)
+    @by_tiles
+    def _(r):
         center = acc[r, :] + vecs[3:4, :] + (n1[r, :] * vecs[1:2, :] + vecs[2:3, :])
         center = center - jnp.mean(center, axis=-1, keepdims=True)
         inv = lax.rsqrt(jnp.mean(center * center, axis=-1, keepdims=True) + 1e-12)
         n2 = center * inv
         final = n2 * vecs[4:5, :] + vecs[5:6, :]
         out = final.astype(BF16)
-        g[1, 0, r, :] = out
+        layer_out[r, :] = out
         g[1, 1, r, :] = (final - out.astype(F32)).astype(BF16)
         dyt = work[r, :].astype(F32)
         dn = dyt * vecs[4:5, :]
@@ -507,13 +526,9 @@
         acc[r, :] = dr
         dlow[r, :] = dr.astype(BF16)
 
-    to_out = pltpu.make_async_copy(g.at[1, 0, span(0, length)], layer_out, ls.at[4])
-    to_out.start()
-    labels = lax.broadcasted_iota(jnp.int32, (TEXTS, length), 0)
-    member = jnp.where(segr[0:1, :] == labels, 1.0, 0.0)
-    counts = jnp.sum(member, axis=-1, keepdims=True)
-    member = member.astype(BF16)
-    pooled[...] = (nn(member, g[1, 0, 0:length, :]) + nn(member, g[1, 1, 0:length, :])) / counts
+    counts = jnp.sum(memb[...], axis=-1, keepdims=True)
+    member = memb[...].astype(BF16)
+    pooled[...] = (nn(member, layer_out[...]) + nn(member, g[1, 1, 0:length, :])) / counts
 
     ones = jnp.ones((8, length), BF16)
 
@@ -532,7 +547,6 @@
         grad_to(0, s, lambda r: act[tt, :, r].T, dlow)
         r1(0, s).start()
 
-    to_out.wait()
     transpose_to(h1)
 
     @pl.loop(0, n_t)
@@ -550,6 +564,7 @@
 
         @pl.when(s > 0)
         def _():
+            on_r1(1, s - 1)
             on_r2(0, s - 1)
 
         grad_to(1, s, lambda r: tr[r, :], work)
@@ -566,10 +581,10 @@
         vsum[pl.ds(8 + tt, 1), :] = nn(ones, work[...])[0:1, :]
 
     on_r2(0, far)
-
-    @pl.loop(0, length // 32)
-    def _(m):
-        r = span(m * 32, 32)
+    on_r1(1, far)
+
+    @by_tiles
+    def _(r):
         dh, nt1 = acc[r, :], n1[r, :]
         add_sum(4, dh * nt1)
         add_sum(5, dh)
@@ -585,7 +600,6 @@
 
     for s in range(n_t):
         on_r2b(0, s, s == far)
-    transpose_to(dlow)
     for k, row in ((3, 0), (4, 1), (5, 2), (0, 3), (1, 4), (2, 5)):
         vsum[row : row + 1, :] = jnp.sum(sums[k], axis=0, keepdims=True)
     vsum[6:8, :] = jnp.zeros((2, width), F32)
@@ -594,40 +608,53 @@
     @pl.loop(0, n_t)
     def _(s):
         tt = goes(s)
-        on_r1(1, s)
+        on_r2(1, s)
 
         @pl.loop(0, length // TILE)
         def _(m):
             r = span(m * TILE, TILE)
-            out = nn(dlow[r, :], w[QKVO, tt, :, 512:768])
+            out = nt(dlow[r, :], w[QKVO, tt, 512:768, :])
             dctx[r, 0:128] = (out[:, 0:128] * high32).astype(BF16)
             dctx[r, 128:256] = out[:, 128:256].astype(BF16)
 
+        @pl.when(s == 0)
+        def _():
+            on_r3(0)
+
+        attend_back(tt)
+        on_r2b(1, s, None)
+
         @pl.when(s == 1)
         def _():
-            on_r3(0)
-
-        @pl.when(s == 2)
-        def _():
             on_r4(0)
 
-        attend_back(tt)
-
         @pl.when(s > 0)
         def _():
-            on_r2(1, s - 1)
+            on_r1(2, s - 1)
+
+        @pl.when(s > 1)
+        def _():
+            on_r2(2, s - 2)
+
+        @pl.when(s == far)
+        def _():
+            on_r3(1)
 
         r1(0, s).wait_send()
-        for j in range(3):
-            r2(0, s, j).wait_send()
-
-        @pl.loop(0, rows // TILE)
-        def _(m):
-            r = span(m * TILE, TILE)
-            lt = x[:, r].T
-            g[0, s, r, 0:256] = nn(lt, work[:, 0:256]).astype(BF16)
-            g[0, s, r, 256:512] = nn(lt, work[:, 256:512]).astype(BF16)
-            g[0, s, r, 512:768] = (nn(lt, work[:, 512:768]) + nn(tr[r, :], ctx[tt])).astype(BF16)
+        for h in range(2):
+            for j in range(3):
+                r2(0, s, h, j).wait_send()
+
+        for m in range(rows // TILE):
+            r = slice(m * TILE, (m + 1) * TILE)
+            lt = work[:, r].T
+            ct = ctx[tt].T if r.start == 512 else None
+            for n in range(width // TILE):
+                c = slice(n * TILE, (n + 1) * TILE)
+                out = nn(lt, x[:, c])
+                if ct is not None:
+                    out = out + nn(ct, dlow[:, c])
+                g[0, s, r, c] = out.astype(BF16)
 
         r1(2, s).start()
 
@@ -637,41 +664,43 @@
             dm = work[r, 0:640]
             for n in range(width // TILE):
                 c = slice(n * TILE, (n + 1) * TILE)
-                acc[r, c] += nt(dm, w[QKVO, tt, c, 0:640])
+                acc[r, c] += nn(dm, w[QKVO, tt, 0:640, c])
 
         vsum[pl.ds(12 + tt, 1), :] = nn(ones, work[...])[0:1, :]
 
     v1 = remote(vsum, va, vs.at[0], vr.at[0], me.sibling())
     v1.start()
-    on_r2(1, far)
-    for s in range(n_t):
-        on_r1(2, s)
+    on_r1(2, far)
     v1.wait()
     vsum[...] = vsum[...] + va[...]
     v2 = [remote(vsum, vb.at[j], vs.at[1 + j], vr.at[1 + j], me.chip(j)) for j in range(3)]
     for c in v2:
         c.start()
-    for s in range(n_t):
-        on_r2b(1, s, s == far)
-    for s in range(n_t):
-        on_r2(2, s)
+    on_r2(2, far - 1)
+    on_r2b(2, 0, False)
+    on_r2b(2, 1, False)
+    on_r4(1)
+    on_r2(2, far)
+    on_r2b(2, 2, False)
     for c in v2:
         c.wait()
     va[...] = vsum[...] + vb[0] + vb[1] + vb[2]
     v3 = [remote(va, vd.at[s], vs.at[4 + s], vr.at[4 + s], me.z(s + 1)) for s in range(far)]
     for c in v3:
         c.start()
-    on_r3(1)
-    for s in range(n_t):
-        on_r2b(2, s, s == far)
-    on_r4(1)
+    on_r2b(2, far, True)
     on_r3(2)
     for c in v3:
         c.wait()
     total = va[...]
     for s in range(far):
         total = total + vd[s]
-    vout[...] = total
+    vsum[...] = total
+    inner = width // n_t
+    turns = lax.rem(width - me.t * inner, width)
+    vout[...] = pltpu.roll(total[0:8, :], turns, 1)
+    vout[6:7, :] = vsum[pl.ds(8 + me.t, 1), :]
+    vout[7:8, :] = vsum[pl.ds(12 + me.t, 1), :]
     on_r4(2)
     for k in range(3):
         r5(k).wait_recv()
@@ -688,15 +717,16 @@
         for s in range(n_t):
             if k > 0:
                 r1(k, s).wait_send()
-                for j in range(3):
-                    r2(k, s, j).wait_send()
+                for h in range(2):
+                    for j in range(3):
+                        r2(k, s, h, j).wait_send()
         for j in range(3):
             r4(k, j).wait_send()
         r5(k).wait_send()
 
 
-def run_layer(wl, x, dy, segc, segr, vecs, bloc, n_t):
-    groups, rows, cols = wl.shape
+def run_layer(wq, wk, wv, wo, wup, wdown, x, dy, seg, vecs, n_t):
+    groups, (rows, cols) = 3, wup.shape
     length, width = x.shape
     ch, half, far = rows // PLANE, rows // 2, n_t - 1
     dma, vmem = pltpu.SemaphoreType.DMA, pltpu.VMEM
@@ -710,10 +740,10 @@
             shape((TEXTS, width), F32),
             shape((length, width), F32),
             shape((groups, rows, cols), BF16),
-            shape((16, width), F32),
+            shape((8, width), F32),
         ),
-        in_specs=[there, here, there, here, here, here, here],
-        out_specs=[there, here, here, here, here],
+        in_specs=[there] * 6 + [here, there, here, here],
+        out_specs=[here] * 5,
         scratch_shapes=[
             vmem((groups, n_t, rows, cols), BF16),
             vmem((2, n_t, rows, cols), BF16),
@@ -733,21 +763,23 @@
             vmem((2, length, 384), BF16),
             vmem((length, width), F32),
             vmem((n_t, 8, width), F32),
+            vmem((8, width), F32),
             vmem((length, 384), F32),
+            vmem((TEXTS, length), F32),
             vmem((length, 1), F32),
             vmem((6, 8, width), F32),
             vmem((16, width), F32),
             vmem((16, width), F32),
             vmem((3, 16, width), F32),
             vmem((far, 16, width), F32),
-            dma((5,)),
+            dma((11,)),
             *pair(groups, far),
             *pair(groups, far, 2),
             *pair(groups, far, 2),
             *pair(groups, far),
             *pair(far),
             *pair(groups, n_t),
-            *pair(groups, n_t, 3),
+            *pair(groups, n_t, 2, 3),
             *pair(groups, far),
             *pair(groups, 3),
             *pair(groups),
@@ -756,7 +788,7 @@
         compiler_params=pltpu.CompilerParams(
             collective_id=1, has_side_effects=True, vmem_limit_bytes=67043328
         ),
-    )(wl, x, dy, segc, segr, vecs, bloc)
+    )(wq, wk, wv, wo, wup, wdown, x, dy, seg, vecs)
 
 
 def per_device(
@@ -765,66 +797,48 @@
     out_weight, out_bias, attn_gain, attn_shift, up_weight, up_bias, down_weight, down_bias,
     ffn_gain, ffn_shift, cotangent,
 ):
-    x = hidden_in[0]
-    width, inner = query_weight.shape
-    two = 2 * HEAD_DIM
-    t = lax.axis_index("tensor")
-    wo = out_weight.T
-    qkvo = jnp.concatenate(
+    inner, width = out_weight.shape
+    spare = jnp.zeros((width - 2 * inner,), F32)
+    vecs = jnp.concatenate(
         [
-            query_weight[:, :two], key_weight[:, :two], value_weight[:, :two],
-            query_weight[:, two:], value_weight[:, two:], key_weight[:, two:],
-            wo[:, two:], wo[:, :two],
-        ],
-        axis=1,
-    )
-    wl = jnp.stack([qkvo, up_weight, down_weight])
-    none = jnp.zeros((two,), F32)
-    scale = 1.0 / math.sqrt(HEAD_DIM)
-    bias_row = jnp.concatenate(
-        [query_bias[:two], none, value_bias[:two], query_bias[two:], value_bias[two:], none, none]
-    )
-    full = jnp.ones((HEAD_DIM,), F32)
-    down = full * scale
-    scale_row = jnp.concatenate([down, down] + [full] * 4 + [down] + [full] * 5)
-    bloc = jnp.concatenate(
-        [jnp.stack([up_bias, bias_row, scale_row]), jnp.zeros((5, width), F32)], axis=0
-    )
-    vecs = jnp.stack(
-        [out_bias, attn_gain, attn_shift, down_bias, ffn_gain, ffn_shift, out_bias, out_bias]
-    )
-    seg = lax.dynamic_slice_in_dim(segment_ids, t, 1, 0)[0]
-    segr = jnp.broadcast_to(seg[None, :], (8, seg.shape[0]))
+            out_bias, attn_gain, attn_shift, down_bias, ffn_gain, ffn_shift, up_bias,
+            query_bias, value_bias, spare,
+        ]
+    ).reshape(8, width)
     final, pooled, dx, fout, vout = run_layer(
-        wl, x, cotangent[0], seg[:, None], segr, vecs, bloc, n_t
+        query_weight.T, key_weight.T, value_weight.T, out_weight, up_weight, down_weight,
+        hidden_in[0], cotangent[0], segment_ids, vecs, n_t,
     )
     if n_b > PLANE:
         apart = [[i + PLANE * j for j in range(n_b // PLANE)] for i in range(PLANE)]
         fout, vout = lax.psum((fout.astype(F32), vout), "batch", axis_index_groups=apart)
-    gq = fout[2].astype(F32)
-    here = lax.dynamic_slice_in_dim(vout, t * inner, inner, 1)
-    dub = lax.dynamic_slice_in_dim(vout, 8 + t, 1, 0)[0]
-    dqb = lax.dynamic_slice_in_dim(vout, 12 + t, 1, 0)[0]
     h = HEAD_DIM
+
+    def rows_of(*spans):
+        return jnp.concatenate([fout[2, h * lo : h * hi] for lo, hi in spans], axis=0).astype(F32)
+
+    def lanes_of(*spans):
+        return jnp.concatenate([vout[7, h * lo : h * hi] for lo, hi in spans])
+
     return (
         final[None],
         pooled[None],
         dx[None],
-        jnp.concatenate([gq[:, :two], gq[:, 6 * h : 7 * h]], axis=1),
-        jnp.concatenate([dqb[:two], dqb[6 * h : 7 * h]]),
-        jnp.concatenate([gq[:, two : 2 * two], gq[:, 8 * h : 9 * h]], axis=1),
-        jnp.concatenate([gq[:, 2 * two : 3 * two], gq[:, 7 * h : 8 * h]], axis=1),
-        jnp.concatenate([dqb[2 * two : 3 * two], dqb[7 * h : 8 * h]]),
-        jnp.concatenate([gq[:, 10 * h :], gq[:, 9 * h : 10 * h]], axis=1).T,
-        here[0],
-        here[1],
-        here[2],
+        rows_of((0, 2), (6, 7)).T,
+        lanes_of((0, 2), (6, 7)),
+        rows_of((2, 4), (8, 9)).T,
+        rows_of((4, 6), (7, 8)).T,
+        lanes_of((4, 6), (7, 8)),
+        rows_of((10, 12), (9, 10)),
+        vout[0, :inner],
+        vout[1, :inner],
+        vout[2, :inner],
         fout[1].astype(F32),
-        dub,
+        vout[6],
         fout[0].astype(F32),
-        here[3],
-        here[4],
-        here[5],
+        vout[3, :inner],
+        vout[4, :inner],
+        vout[5, :inner],
     )
 
 

time: 240 us -> 210 us (0.88)
  local copies, waits for them, and re-layouts: 36.8 us -> 11.2 us
  other arithmetic: 8.72 us -> 5.29 us
    unnamed x24 -> x11, local copies, waits for them, and re-layouts: 13.2 us -> 2.84 us
    slice x19 -> x2, local copies, waits for them, and re-layouts: 11.4 us -> 2.84 us  [the longest x1 1.5 us: per_device(): vout[5, :inner]]
    another operation x11 -> x0, local copies, waits for them, and re-layouts: 7.04 us -> none  [the longest x7 4.78 us: per_device(): jnp.stack([out_bias, attn_gain, attn_shift, down_bias, ffn_gain, ffn_shif...]
    squeeze x0 -> x4, local copies, waits for them, and re-layouts: none -> 3.98 us  [the longest x2 2.47 us: rows_of(): fout[2, h * lo:h * hi]]
where the time goes in v3:
time: 210 us; the launch traced here: 209 us
  Pallas kernels  192 us (91%)
  local copies, waits for them, and re-layouts  11.2 us (5%)
  other arithmetic  5.29 us (3%)
    pallas_call x1, Pallas kernels, run_layer(): pl.pallas_call(functools.partial(layer_kernel, n_t), out_shape=(shape((le...  192 us

profile of v3, /device:TPU:0, one launch (start us, length us, event | category | flops | bytes accessed | tf_op | source)
XLA Modules:
  0.0 209.5 jit_solution(4016555996141936820)
XLA Ops:
  0.7 0.9 concatenate.21
  1.6 0.6 reshape.43.vecs
  2.2 192.3 %shard_map.313 = (bf16[512,768]{1,0:T(8,128)(2,1)}, f32[8,768]{1,0:T(8,128)}, f32[512,768]{1,0:T(8,128)}, bf16[3,768,768]{2,1,0:T(8,128)(2,1)}, f32[8,768]{1,0:T(8,128)}) custom-call(bf16[192,768]{1,0:T(8,128)(2,1)} %bitcast.54, bf16[192,768]{1,0:T(8,128)(2,1)} %bitcast.55, bf16[192,768]{1,0:T(8,128)(2,1)} %bitcast.56, bf16[192,768]{1,0:T(8,128)(2,1)} %wo.1, ...), custom_call_target="tpu_custom_call" | custom-call | tf_op jit(solution)/shard_map/pallas_call | solution.py:736
  194.5 0.8 slice_bitcast_fusion.8
  195.3 0.7 slice_bitcast_fusion.9
  196.0 0.6 pad_maximum_fusion
  196.6 1.3 slice_reduce_fusion
  197.9 1.5 fusion
  199.4 1.1 slice_bitcast_fusion.4
  200.5 0.0 copy-start
  200.5 1.4 slice_bitcast_fusion
  201.9 1.1 convert_bitcast_fusion.2
  203.0 1.1 convert_bitcast_fusion
  204.1 0.0 copy-done
  204.1 0.0 copy-start.2
  204.1 0.0 copy-start.3
  204.1 2.5 %bitcast_convert_fusion = (f32[768,768]{1,0:T(8,128)}, f32[768,768]{1,0:T(8,128)}) fusion(bf16[3,768,768]{2,1,0:T(8,128)(2,1)S(1)} %copy-done), kind=kLoop, calls=%fused_computation | loop fusion | flops 1179648 | bytes 7077888 | tf_op jit(solution)/shard_map/convert_element_type | solution.py:838
  206.6 0.0 copy-start.1
  206.6 0.0 copy-done.2
  206.6 0.9 copy.39
  207.5 0.0 copy-done.3
  207.5 0.6 copy.40
  208.1 0.2 copy-done.1
  208.3 1.1 copy.41
  (1 shorter events, 0.0 us)
Async XLA Ops:
  200.5 3.6 %copy-start = (bf16[3,768,768]{2,1,0:T(8,128)(2,1)S(1)}, bf16[3,768,768]{2,1,0:T(8,128)(2,1)}, u32[]{:S(2)}) copy-start(bf16[3,768,768]{2,1,0:T(8,128)(2,1)} %get-tuple-element.26) | copy-start | bytes 10616836
  204.1 2.6 %copy-start.2 = (bf16[512,768]{1,0:T(8,128)(2,1)S(1)}, bf16[512,768]{1,0:T(8,128)(2,1)}, u32[]{:S(2)}) copy-start(bf16[512,768]{1,0:T(8,128)(2,1)} %get-tuple-element.23) | copy-start | bytes 2359300
  204.1 3.4 %copy-start.3 = (f32[8,768]{1,0:T(8,128)S(1)}, f32[8,768]{1,0:T(8,128)}, u32[]{:S(2)}) copy-start(f32[8,768]{1,0:T(8,128)} %get-tuple-element.24) | copy-start | bytes 73732
  206.6 1.7 copy-start.1

commit v4 on v3

--- a/solution.py
+++ b/solution.py
@@ -47,6 +47,10 @@
     def z(self, step):
         return {"batch": self.base + self.r, "tensor": lax.rem(self.t + step, self.n_t)}
 
+    def line(self, way):
+        step = 1 if way == 0 else self.n_t - 1
+        return {"batch": self.base + self.r, "tensor": lax.rem(self.t + step, self.n_t)}
+
     def other(self, axis):
         y = self.y if axis == 0 else 1 - self.y
         x = self.x if axis == 1 else 1 - self.x
@@ -119,30 +123,58 @@
     blocks = length // LANES
     far = n_t - 1
 
+    order = [sorted((abs(i - j), j) for j in range(n_t) if j != i) for i in range(n_t)]
+
+    def pick(index, values):
+        out = values[-1]
+        for i in range(len(values) - 2, -1, -1):
+            out = jnp.where(index == i, values[i], out)
+        return out
+
+    near_first = [pick(me.t, [jnp.int32(row[e][1]) for row in order]) for e in range(far)]
+
     def came(s):
-        return lax.rem(me.t + far - s, n_t)
+        return near_first[s] if isinstance(s, int) else pick(s, near_first)
 
     def goes(s):
         return lax.rem(me.t + 1 + s, n_t)
 
-    pieces = (
-        (wq, 0, 128, 0), (wk, 0, 128, 128), (wv, 0, 128, 256), (wq, 128, 64, 384),
-        (wv, 128, 64, 448), (wk, 128, 64, 512), (wo, 128, 64, 576), (wo, 0, 128, 640),
-    )
+    inner = rows // 4
 
     def local(k):
         if k > 0:
-            return [pltpu.make_async_copy((wup, wdown)[k - 1], w.at[k, me.t], ls.at[7 + k])]
+            return [pltpu.make_async_copy((wup, wdown)[k - 1], w.at[k, me.t], ls.at[3 + k])]
         return [
-            pltpu.make_async_copy(
-                src.at[pl.ds(at, size)], w.at[0, me.t, pl.ds(to, size)], ls.at[n]
-            )
-            for n, (src, at, size, to) in enumerate(pieces)
+            pltpu.make_async_copy(src, w.at[0, me.t, pl.ds(n * inner, inner)], ls.at[n])
+            for n, src in enumerate((wq, wk, wv, wo))
         ]
 
-    def zcopy(k, s):
+    def zown(k, way):
         place = w.at[k, me.t, mine]
-        return remote(place, place, zs.at[k, s], zr.at[k, s], me.z(s + 1))
+        return remote(place, place, zs.at[k, far + way], zr.at[k, me.t], me.line(way))
+
+    def zrecv(k, s):
+        place = w.at[k, came(s), mine]
+        return remote(place, place, zs.at[k, s], zr.at[k, came(s)], me.line(0))
+
+    def zpass(k, s, act_on):
+        src = came(s)
+        place = w.at[k, src, mine]
+        for way in range(2):
+            goes_on = (src < me.t) & (me.t < far) if way == 0 else (src > me.t) & (me.t > 0)
+
+            @pl.when(goes_on)
+            def _():
+                act_on(remote(place, place, zs.at[k, s], zr.at[k, src], me.line(way)))
+
+    def zends(k, act_on):
+        @pl.when(me.t < far)
+        def _():
+            act_on(zown(k, 0))
+
+        @pl.when(me.t > 0)
+        def _():
+            act_on(zown(k, 1))
 
     def xcopy(k, s, j):
         place = w.at[k, came(s), mine]
@@ -161,7 +193,8 @@
         return remote(bloc, near.at[me.t], cs.at[s], cr.at[s], me.z(s + 1))
 
     def on_z(k, s):
-        zcopy(k, s).wait_recv()
+        zrecv(k, s).wait_recv()
+        zpass(k, s, lambda c: c.start())
         for j in range(2):
             xcopy(k, s, j).start()
 
@@ -198,12 +231,12 @@
     def r2(k, s, h, j):
         source = (me.other(h), me.other(2), me.other(1 - h))[j]
         return remote(
-            g.at[slot(k), s, sub(source, h)], b.at[slot(k), s, j, span(h * cut, cut)],
+            g.at[slot(k), s, sub(source, h)], b.at[k, s, j, span(h * cut, cut)],
             r2s.at[k, s, h, j], r2r.at[k, s, h, j], me.chip(1 - h if j == 2 else h),
         )
 
     def r3(k, s):
-        return remote(b.at[slot(k), s, 0], d.at[k, s], r3s.at[k, s], r3r.at[k, s], me.z(s + 1))
+        return remote(b.at[k, s, 0], d.at[k, s], r3s.at[k, s], r3r.at[k, s], me.z(s + 1))
 
     def r4(k, j):
         place = fout.at[k, mine]
@@ -229,15 +262,15 @@
         for h in range(2):
             rows_h = span(h * cut, cut)
             r2(k, s, h, 1).wait_recv()
-            g[slot(k), s, sub(me.other(1 - h), h)] += b[slot(k), s, 1, rows_h]
+            g[slot(k), s, sub(me.other(1 - h), h)] += b[k, s, 1, rows_h]
             r2(k, s, h, 2).start()
             r2(k, s, h, 0).wait_recv()
-            g[slot(k), s, sub(me.q, h)] += b[slot(k), s, 0, rows_h]
+            g[slot(k), s, sub(me.q, h)] += b[k, s, 0, rows_h]
 
     def on_r2b(k, s, last):
         for h in range(2):
             r2(k, s, h, 2).wait_recv()
-        b[slot(k), s, 0] = g[slot(k), s, quarter(me.q)] + b[slot(k), s, 2]
+        b[k, s, 0] = g[slot(k), s, quarter(me.q)] + b[k, s, 2]
         if last is None:
 
             @pl.when(s < far)
@@ -248,7 +281,7 @@
             r3(k, s).start()
 
     def on_r3(k):
-        total = b[slot(k), far, 0].astype(F32)
+        total = b[k, far, 0].astype(F32)
         for s in range(far):
             r3(k, s).wait_recv()
             total = total + d[k, s].astype(F32)
@@ -263,6 +296,36 @@
             r4(k, j).wait_recv()
         r5(k).start()
 
+    def pair_sum(n):
+        return remote(vsum.at[n], va.at[n], vs.at[n, 0], vr.at[n, 0], me.sibling())
+
+    def plane_sum(n, j):
+        return remote(vsum.at[n], vb.at[n, j], vs.at[n, 1 + j], vr.at[n, 1 + j], me.chip(j))
+
+    def line_sum(n, s):
+        return remote(va.at[n], vd.at[n, s], vs.at[n, 4 + s], vr.at[n, 4 + s], me.z(s + 1))
+
+    def on_pair(n):
+        pair_sum(n).wait()
+        vsum[n] += va[n]
+        for j in range(3):
+            plane_sum(n, j).start()
+
+    def on_plane(n):
+        for j in range(3):
+            plane_sum(n, j).wait()
+        va[n] = vsum[n] + vb[n, 0] + vb[n, 1] + vb[n, 2]
+        for s in range(far):
+            line_sum(n, s).start()
+
+    def on_line(n):
+        for s in range(far):
+            line_sum(n, s).wait()
+        total = va[n]
+        for s in range(far):
+            total = total + vd[n, s]
+        return total
+
     low_lanes = lax.broadcasted_iota(jnp.int32, (1, LANES), 1) < HEAD_DIM
     low = jnp.where(low_lanes, 1.0, 0.0).astype(BF16)
     high = jnp.where(low_lanes, 0.0, 1.0).astype(BF16)
@@ -273,13 +336,21 @@
         lo = max(0, i * LANES - TEXT_MOST)
         return lo, min(length, (i + 1) * LANES + TEXT_MOST)
 
+    q01, k01, v01, o01 = (0, 128), (192, 320), (384, 512), (576, 704)
+    q2, k2, v2, o2 = (128, 192), (320, 384), (512, 576), (704, 768)
+
+    def picked(tt, spans, cols=slice(None)):
+        return jnp.concatenate([w[QKVO, tt, lo:hi, cols] for lo, hi in spans], axis=0)
+
     def project(tt):
         @pl.loop(0, length // TILE)
         def _(m):
             r = span(m * TILE, TILE)
             xm = x[r, :]
-            for lo, hi in ((0, 256), (256, 512), (512, 640)):
-                piece = nt(xm, w[QKVO, tt, lo:hi, :])
+            for lo, hi, spans in (
+                (0, 256, (q01, k01)), (256, 512, (v01, q2, v2)), (512, 640, (k2, o2)),
+            ):
+                piece = nt(xm, picked(tt, spans))
                 qkv[tt, r, lo:hi] = (
                     (piece + near[tt, 1:2, lo:hi]) * scales[:, lo:hi]
                 ).astype(BF16)
@@ -293,13 +364,17 @@
                 (qkv[tt, r, 0:128] * high, 128, 256),
                 (qkv[tt, r, 384:512] * low, 512, 384),
             )
-            outs = []
-            for h, (q, kc, vc) in enumerate(heads_in):
-                s = nt(q, qkv[tt, lo:hi, kc : kc + LANES]) + bias[r, 0 : hi - lo]
-                e = jnp.exp(s - jnp.max(s, axis=-1, keepdims=True))
-                p = (e * (1.0 / jnp.sum(e, axis=-1, keepdims=True))).astype(BF16)
+            sc = [
+                nt(q, qkv[tt, lo:hi, kc : kc + LANES]) + bias[r, 0 : hi - lo]
+                for q, kc, _ in heads_in
+            ]
+            ex = [jnp.exp(z - jnp.max(z, axis=-1, keepdims=True)) for z in sc]
+            ps = [(e * (1.0 / jnp.sum(e, axis=-1, keepdims=True))).astype(BF16) for e in ex]
+            for h, p in enumerate(ps):
                 prob[tt, h, r, 0 : hi - lo] = p
-                outs.append(nn(p, qkv[tt, lo:hi, vc : vc + LANES]))
+            outs = [
+                nn(p, qkv[tt, lo:hi, vc : vc + LANES]) for p, (_, _, vc) in zip(ps, heads_in)
+            ]
             ctx[tt, r, 0:128] = (outs[2] * high32).astype(BF16)
             ctx[tt, r, 128:256] = (outs[0] * low32 + outs[1] * high32).astype(BF16)
 
@@ -355,8 +430,7 @@
     def by_tiles(body):
         @pl.loop(0, length // 64)
         def _(m):
-            for part in range(4):
-                body(span(m * 64 + part * 16, 16))
+            body(span(m * 64, 64))
 
     def transpose_to(src):
         @pl.loop(0, rows // TILE)
@@ -367,7 +441,7 @@
     for k in range(3):
         for copy in local(k):
             copy.start()
-    dy_in = pltpu.make_async_copy(dy, work, ls.at[10])
+    dy_in = pltpu.make_async_copy(dy, work, ls.at[6])
     dy_in.start()
     own = vecs[7:8, :]
     mid, end = own[:, 128:256], own[:, 256:384]
@@ -379,14 +453,12 @@
     bloc[1:2, 384:512] = jnp.where(low_lanes, mid, end)
     near[me.t] = bloc[...]
     me.greet()
+    for s in range(far):
+        bcopy(s).start()
     for k in range(3):
         for copy in local(k):
             copy.wait()
-        for s in range(far):
-            zcopy(k, s).start()
-        if k == 0:
-            for s in range(far):
-                bcopy(s).start()
+        zends(k, lambda c: c.start())
     lane = lax.broadcasted_iota(jnp.int32, (1, 640), 1)
     is_query = (lane < 128) | ((lane >= 384) & (lane < 448))
     scales = jnp.where(is_query, 1.0 / math.sqrt(HEAD_DIM), 1.0)
@@ -434,7 +506,7 @@
             c = slice(n * TILE, (n + 1) * TILE)
             out = x[r, c].astype(F32) + vecs[0:1, c]
             for t in range(n_t):
-                out = out + nn(ctx[t, r, :], w[QKVO, t, 512:768, c])
+                out = out + nn(ctx[t, r, :], picked(t, (k2, o2, o01), c))
             acc[r, c] = out
 
     on_relay(UP, 0)
@@ -504,27 +576,26 @@
 
     @by_tiles
     def _(r):
+        dyt = work[r, :].astype(F32)
         center = acc[r, :] + vecs[3:4, :] + (n1[r, :] * vecs[1:2, :] + vecs[2:3, :])
         center = center - jnp.mean(center, axis=-1, keepdims=True)
         inv = lax.rsqrt(jnp.mean(center * center, axis=-1, keepdims=True) + 1e-12)
         n2 = center * inv
         final = n2 * vecs[4:5, :] + vecs[5:6, :]
         out = final.astype(BF16)
-        layer_out[r, :] = out
-        g[1, 1, r, :] = (final - out.astype(F32)).astype(BF16)
-        dyt = work[r, :].astype(F32)
         dn = dyt * vecs[4:5, :]
-        dyn = dyt * n2
-        add_sum(1, dyn)
-        add_sum(2, dyt)
         dr = inv * (
             dn
             - jnp.mean(dn, axis=-1, keepdims=True)
             - n2 * jnp.mean(dn * n2, axis=-1, keepdims=True)
         )
-        add_sum(0, dr)
+        layer_out[r, :] = out
+        g[1, 1, r, :] = (final - out.astype(F32)).astype(BF16)
         acc[r, :] = dr
         dlow[r, :] = dr.astype(BF16)
+        add_sum(0, dr)
+        add_sum(1, dyt * n2)
+        add_sum(2, dyt)
 
     counts = jnp.sum(memb[...], axis=-1, keepdims=True)
     member = memb[...].astype(BF16)
@@ -547,12 +618,16 @@
         grad_to(0, s, lambda r: act[tt, :, r].T, dlow)
         r1(0, s).start()
 
+        @pl.when(s > 0)
+        def _():
+            on_r1(0, s - 1)
+
     transpose_to(h1)
+    on_r1(0, far)
 
     @pl.loop(0, n_t)
     def _(s):
         tt = goes(s)
-        on_r1(0, s)
 
         @pl.loop(0, length // TILE)
         def _(m):
@@ -565,7 +640,6 @@
         @pl.when(s > 0)
         def _():
             on_r1(1, s - 1)
-            on_r2(0, s - 1)
 
         grad_to(1, s, lambda r: tr[r, :], work)
         r1(1, s).start()
@@ -578,67 +652,70 @@
                 c = slice(n * TILE, (n + 1) * TILE)
                 acc[r, c] += nt(dm, w[UP, tt, c, :])
 
-        vsum[pl.ds(8 + tt, 1), :] = nn(ones, work[...])[0:1, :]
-
-    on_r2(0, far)
+        vsum[1, pl.ds(tt, 1), :] = nn(ones, work[...])[0:1, :]
+        on_r2(0, s)
+
     on_r1(1, far)
 
     @by_tiles
     def _(r):
         dh, nt1 = acc[r, :], n1[r, :]
-        add_sum(4, dh * nt1)
-        add_sum(5, dh)
         dn = dh * vecs[1:2, :]
         dr = rstd[r, :] * (
             dn
             - jnp.mean(dn, axis=-1, keepdims=True)
             - nt1 * jnp.mean(dn * nt1, axis=-1, keepdims=True)
         )
-        add_sum(3, dr)
         acc[r, :] = dr
         dlow[r, :] = dr.astype(BF16)
-
-    for s in range(n_t):
-        on_r2b(0, s, s == far)
+        add_sum(3, dr)
+        add_sum(4, dh * nt1)
+        add_sum(5, dh)
+
+    on_r2b(0, 0, False)
+    on_r2b(0, 1, False)
+    vsum[0] = jnp.zeros((8, width), F32)
     for k, row in ((3, 0), (4, 1), (5, 2), (0, 3), (1, 4), (2, 5)):
-        vsum[row : row + 1, :] = jnp.sum(sums[k], axis=0, keepdims=True)
-    vsum[6:8, :] = jnp.zeros((2, width), F32)
+        vsum[0, row : row + 1, :] = jnp.sum(sums[k], axis=0, keepdims=True)
+    pair_sum(0).start()
     work[:, 640:768] = jnp.zeros((length, LANES), BF16)
 
     @pl.loop(0, n_t)
     def _(s):
         tt = goes(s)
-        on_r2(1, s)
 
         @pl.loop(0, length // TILE)
         def _(m):
             r = span(m * TILE, TILE)
-            out = nt(dlow[r, :], w[QKVO, tt, 512:768, :])
+            out = nt(dlow[r, :], picked(tt, (k2, o2, o01)))
             dctx[r, 0:128] = (out[:, 0:128] * high32).astype(BF16)
             dctx[r, 128:256] = out[:, 128:256].astype(BF16)
 
+        attend_back(tt)
+
         @pl.when(s == 0)
         def _():
+            on_pair(0)
+            on_r2b(0, 2, False)
+            on_r2(1, 0)
+            on_r2(1, 1)
+
+        @pl.when(s == 1)
+        def _():
+            on_r2b(0, 3, True)
+            on_r2(1, 2)
+            on_r2(1, 3)
+
+        @pl.when(s == 2)
+        def _():
             on_r3(0)
-
-        attend_back(tt)
-        on_r2b(1, s, None)
-
-        @pl.when(s == 1)
-        def _():
-            on_r4(0)
-
-        @pl.when(s > 0)
-        def _():
-            on_r1(2, s - 1)
-
-        @pl.when(s > 1)
-        def _():
-            on_r2(2, s - 2)
-
-        @pl.when(s == far)
-        def _():
-            on_r3(1)
+            on_plane(0)
+            on_r2b(1, 0, False)
+
+        @pl.when(s == 3)
+        def _():
+            on_r2b(1, 1, False)
+            on_r2b(1, 2, False)
 
         r1(0, s).wait_send()
         for h in range(2):
@@ -654,7 +731,11 @@
                 out = nn(lt, x[:, c])
                 if ct is not None:
                     out = out + nn(ct, dlow[:, c])
-                g[0, s, r, c] = out.astype(BF16)
+                out = out.astype(BF16)
+                at = 0
+                for lo, hi in ((q01, k01), (v01, q2, v2), (k2, o2, o01))[m]:
+                    g[0, s, lo:hi, c] = out[at : at + hi - lo, :]
+                    at += hi - lo
 
         r1(2, s).start()
 
@@ -664,43 +745,41 @@
             dm = work[r, 0:640]
             for n in range(width // TILE):
                 c = slice(n * TILE, (n + 1) * TILE)
-                acc[r, c] += nn(dm, w[QKVO, tt, 0:640, c])
-
-        vsum[pl.ds(12 + tt, 1), :] = nn(ones, work[...])[0:1, :]
-
-    v1 = remote(vsum, va, vs.at[0], vr.at[0], me.sibling())
-    v1.start()
+                acc[r, c] += nn(dm, picked(tt, (q01, k01, v01, q2, v2, k2, o2), c))
+
+        vsum[1, pl.ds(4 + tt, 1), :] = nn(ones, work[...])[0:1, :]
+
+        @pl.when(s > 0)
+        def _():
+            on_r1(2, s - 1)
+
+    pair_sum(1).start()
     on_r1(2, far)
-    v1.wait()
-    vsum[...] = vsum[...] + va[...]
-    v2 = [remote(vsum, vb.at[j], vs.at[1 + j], vr.at[1 + j], me.chip(j)) for j in range(3)]
-    for c in v2:
-        c.start()
-    on_r2(2, far - 1)
+    on_r2b(1, far, True)
+    on_pair(1)
+    on_r4(0)
+    on_r2(2, 0)
+    on_r2(2, 1)
+    on_r2(2, 2)
+    on_plane(1)
     on_r2b(2, 0, False)
+    on_r2(2, far)
+    on_r3(1)
+    turns = lax.rem(width - me.t * (width // n_t), width)
+    vout[0:8, :] = pltpu.roll(on_line(0), turns, 1)
+    vout[8:16, :] = jnp.zeros((8, width), F32)
     on_r2b(2, 1, False)
-    on_r4(1)
-    on_r2(2, far)
     on_r2b(2, 2, False)
-    for c in v2:
-        c.wait()
-    va[...] = vsum[...] + vb[0] + vb[1] + vb[2]
-    v3 = [remote(va, vd.at[s], vs.at[4 + s], vr.at[4 + s], me.z(s + 1)) for s in range(far)]
-    for c in v3:
-        c.start()
+    vsum[1] = on_line(1)
+    mine_row = vsum[1, pl.ds(4 + me.t, 1), :]
+    vout[6:7, 0:128] = mine_row[:, 0:128]
+    vout[6:7, 128:256] = mine_row[:, 384:512]
+    vout[7:8, 0:128] = mine_row[:, 256:384]
+    vout[7:8, 128:256] = pltpu.roll(mine_row[:, 384:512], HEAD_DIM, 1)
+    vout[8:9, :] = vsum[1, pl.ds(me.t, 1), :]
     on_r2b(2, far, True)
     on_r3(2)
-    for c in v3:
-        c.wait()
-    total = va[...]
-    for s in range(far):
-        total = total + vd[s]
-    vsum[...] = total
-    inner = width // n_t
-    turns = lax.rem(width - me.t * inner, width)
-    vout[...] = pltpu.roll(total[0:8, :], turns, 1)
-    vout[6:7, :] = vsum[pl.ds(8 + me.t, 1), :]
-    vout[7:8, :] = vsum[pl.ds(12 + me.t, 1), :]
+    on_r4(1)
     on_r4(2)
     for k in range(3):
         r5(k).wait_recv()
@@ -708,8 +787,9 @@
     for s in range(far):
         bcopy(s).wait_send()
     for k in range(3):
+        zends(k, lambda c: c.wait_send())
         for s in range(far):
-            zcopy(k, s).wait_send()
+            zpass(k, s, lambda c: c.wait_send())
             scopy(k, s).wait_send()
             for j in range(2):
                 xcopy(k, s, j).wait_send()
@@ -740,7 +820,7 @@
             shape((TEXTS, width), F32),
             shape((length, width), F32),
             shape((groups, rows, cols), BF16),
-            shape((8, width), F32),
+            shape((16, width), F32),
         ),
         in_specs=[there] * 6 + [here, there, here, here],
         out_specs=[here] * 5,
@@ -748,7 +828,7 @@
             vmem((groups, n_t, rows, cols), BF16),
             vmem((2, n_t, rows, cols), BF16),
             vmem((2, n_t, half, cols), BF16),
-            vmem((2, n_t, 3, ch, cols), BF16),
+            vmem((groups, n_t, 3, ch, cols), BF16),
             vmem((groups, far, ch, cols), BF16),
             vmem((n_t, length, 640), BF16),
             vmem((n_t, length, 256), BF16),
@@ -768,12 +848,13 @@
             vmem((TEXTS, length), F32),
             vmem((length, 1), F32),
             vmem((6, 8, width), F32),
-            vmem((16, width), F32),
-            vmem((16, width), F32),
-            vmem((3, 16, width), F32),
-            vmem((far, 16, width), F32),
-            dma((11,)),
-            *pair(groups, far),
+            vmem((2, 8, width), F32),
+            vmem((2, 8, width), F32),
+            vmem((2, 3, 8, width), F32),
+            vmem((2, far, 8, width), F32),
+            dma((7,)),
+            dma((groups, far + 2)),
+            dma((groups, n_t)),
             *pair(groups, far, 2),
             *pair(groups, far, 2),
             *pair(groups, far),
@@ -783,7 +864,7 @@
             *pair(groups, far),
             *pair(groups, 3),
             *pair(groups),
-            *pair(4 + far),
+            *pair(2, 4 + far),
         ],
         compiler_params=pltpu.CompilerParams(
             collective_id=1, has_side_effects=True, vmem_limit_bytes=67043328
@@ -812,29 +893,22 @@
     if n_b > PLANE:
         apart = [[i + PLANE * j for j in range(n_b // PLANE)] for i in range(PLANE)]
         fout, vout = lax.psum((fout.astype(F32), vout), "batch", axis_index_groups=apart)
-    h = HEAD_DIM
-
-    def rows_of(*spans):
-        return jnp.concatenate([fout[2, h * lo : h * hi] for lo, hi in spans], axis=0).astype(F32)
-
-    def lanes_of(*spans):
-        return jnp.concatenate([vout[7, h * lo : h * hi] for lo, hi in spans])
-
+    own = fout[2].astype(F32)
     return (
         final[None],
         pooled[None],
         dx[None],
-        rows_of((0, 2), (6, 7)).T,
-        lanes_of((0, 2), (6, 7)),
-        rows_of((2, 4), (8, 9)).T,
-        rows_of((4, 6), (7, 8)).T,
-        lanes_of((4, 6), (7, 8)),
-        rows_of((10, 12), (9, 10)),
+        own[:inner].T,
+        vout[6, :inner],
+        own[inner : 2 * inner].T,
+        own[2 * inner : 3 * inner].T,
+        vout[7, :inner],
+        own[3 * inner :],
         vout[0, :inner],
         vout[1, :inner],
         vout[2, :inner],
         fout[1].astype(F32),
-        vout[6],
+        vout[8],
         fout[0].astype(F32),
         vout[3, :inner],
         vout[4, :inner],

time: 210 us -> 179 us (0.85)
  Pallas kernels: 192 us -> 164 us
  local copies, waits for them, and re-layouts: 11.2 us -> 8.62 us
    pallas_call x1, Pallas kernels: 192 us -> 164 us  [run_layer(): pl.pallas_call(functools.partial(layer_kernel, n_t), out_shape=(shape((le...]
    squeeze x4 -> x0, local copies, waits for them, and re-layouts: 3.98 us -> none  [the longest x2 2.47 us: rows_of(): fout[2, h * lo:h * hi]]
    transpose x2 -> x0, other arithmetic: 2.18 us -> none  [the longest x1 1.09 us: per_device(): rows_of((0, 2), (6, 7))]
where the time goes in v4:
time: 179 us; the launch traced here: 178 us
  Pallas kernels  164 us (92%)
  local copies, waits for them, and re-layouts  8.62 us (5%)
  other arithmetic  4.62 us (3%)
    pallas_call x1, Pallas kernels, run_layer(): pl.pallas_call(functools.partial(layer_kernel, n_t), out_shape=(shape((le...  164 us
    convert_element_type x1, other arithmetic, per_device(): fout[0].astype(F32)  4.62 us

profile of v4, /device:TPU:0, one launch (start us, length us, event | category | flops | bytes accessed | tf_op | source)
XLA Modules:
  0.0 178.1 jit_solution(3518873855679684829)
XLA Ops:
  0.7 0.9 concatenate.3
  1.6 0.6 reshape.48.vecs
  2.2 164.2 %shard_map.313 = (bf16[512,768]{1,0:T(8,128)(2,1)}, f32[8,768]{1,0:T(8,128)}, f32[512,768]{1,0:T(8,128)}, bf16[3,768,768]{2,1,0:T(8,128)(2,1)}, f32[16,768]{1,0:T(8,128)}) custom-call(bf16[192,768]{1,0:T(8,128)(2,1)} %bitcast.40, bf16[192,768]{1,0:T(8,128)(2,1)} %bitcast.41, bf16[192,768]{1,0:T(8,128)(2,1)} %bitcast.42, bf16[192,768]{1,0:T(8,128)(2,1)} %wo.1, ...), custom_call_target="tpu_custom_call" | custom-call | tf_op jit(solution)/shard_map/pallas_call | solution.py:816
  166.3 1.3 slice_reduce_fusion
  167.7 1.6 fusion
  169.3 4.6 %bitcast_convert_fusion = (f32[768,768]{1,0:T(8,128)}, f32[768,768]{1,0:T(8,128)}, f32[1,768,768]{2,1,0:T(8,128)S(1)}) fusion(bf16[3,768,768]{2,1,0:T(8,128)(2,1)} %get-tuple-element.26), kind=kLoop, calls=%fused_computation | loop fusion | flops 1769472 | bytes 10616832 | tf_op jit(solution)/shard_map/convert_element_type | solution.py:912
  173.9 0.0 copy-start.1
  173.9 0.0 copy-start.2
  173.9 0.0 copy-start
  173.9 1.4 slice_bitcast_fusion
  175.3 0.1 copy-done.1
  175.5 0.9 copy.39
  176.3 0.0 copy-done.2
  176.3 0.6 copy.40
  176.9 0.0 copy-done
  176.9 1.1 copy.41
  (1 shorter events, 0.0 us)
Async XLA Ops:
  173.9 1.6 copy-start.1
  173.9 2.4 %copy-start.2 = (f32[8,768]{1,0:T(8,128)S(1)}, f32[8,768]{1,0:T(8,128)}, u32[]{:S(2)}) copy-start(f32[8,768]{1,0:T(8,128)} %get-tuple-element.24) | copy-start | bytes 73732
  173.9 3.0 %copy-start = (f32[512,768]{1,0:T(8,128)S(1)}, f32[512,768]{1,0:T(8,128)}, u32[]{:S(2)}) copy-start(f32[512,768]{1,0:T(8,128)} %get-tuple-element.25) | copy-start | bytes 4718596

commit v5 on v4

--- a/solution.py
+++ b/solution.py
@@ -68,7 +68,7 @@
         peers += [self.chip(j) for j in range(3)] + [self.sibling()]
         for peer in peers:
             pl.semaphore_signal(barrier, inc=1, device_id=peer, device_id_type=MESH)
-        pl.semaphore_wait(barrier, len(peers))
+        return lambda: pl.semaphore_wait(barrier, len(peers))
 
 
 def remote(src, dst, send, recv, dev):
@@ -79,6 +79,10 @@
 
 def span(start, size):
     return pl.ds(start if isinstance(start, int) else pl.multiple_of(start, size), size)
+
+
+def rows_at(start, size):
+    return pl.ds(pl.multiple_of(start, 16), size)
 
 
 def nn(left, right):
@@ -111,7 +115,7 @@
     w, g, a, b, d, qkv, ctx, dctx, prob, act, dg, h1, dlow, work, tr, dsc, n1, near, bloc, bias,
     memb, rstd, sums, vsum, va, vb, vd,
     ls, zs, zr, xs, xr, rs, rr, ss, sr, cs, cr,
-    r1s, r1r, r2s, r2r, r3s, r3r, r4s, r4r, r5s, r5r, vs, vr,
+    r1s, r1r, r2s, r2r, r3s, r3r, r4s, r4r, r5s, r5r, r6s, r6r, vs, vr,
 ):
     me = Place(n_t)
     length, width = x.shape
@@ -149,40 +153,57 @@
             for n, src in enumerate((wq, wk, wv, wo))
         ]
 
-    def zown(k, way):
+    def chunk(q, lo=0, hi=None):
+        hi = ch if hi is None else hi
+        return rows_at(me.c * half + q * ch + lo, hi - lo)
+
+    def zown(way):
+        place = w.at[QKVO, me.t, mine]
+        return remote(
+            place, place, zs.at[QKVO, far + way], zr.at[QKVO, me.t], me.line(way)
+        )
+
+    def zfar(k, s):
         place = w.at[k, me.t, mine]
-        return remote(place, place, zs.at[k, far + way], zr.at[k, me.t], me.line(way))
+        return remote(place, place, zs.at[k, s], zr.at[k, me.t], me.z(s + 1))
 
     def zrecv(k, s):
         place = w.at[k, came(s), mine]
         return remote(place, place, zs.at[k, s], zr.at[k, came(s)], me.line(0))
 
-    def zpass(k, s, act_on):
+    def zpass(s, act_on):
         src = came(s)
-        place = w.at[k, src, mine]
+        place = w.at[QKVO, src, mine]
         for way in range(2):
             goes_on = (src < me.t) & (me.t < far) if way == 0 else (src > me.t) & (me.t > 0)
 
             @pl.when(goes_on)
             def _():
-                act_on(remote(place, place, zs.at[k, s], zr.at[k, src], me.line(way)))
-
-    def zends(k, act_on):
-        @pl.when(me.t < far)
-        def _():
-            act_on(zown(k, 0))
-
-        @pl.when(me.t > 0)
-        def _():
-            act_on(zown(k, 1))
+                act_on(remote(place, place, zs.at[QKVO, s], zr.at[QKVO, src], me.line(way)))
+
+    def zends(act_on):
+        for way, there in ((0, me.t < far), (1, me.t > 0)):
+
+            @pl.when(there)
+            def _():
+                act_on(zown(way))
+
+    def zstart(k):
+        for s in (0, far - 1, *range(1, far - 1)):
+            zfar(k, s).start()
 
     def xcopy(k, s, j):
-        place = w.at[k, came(s), mine]
+        place = w.at[k, came(s), chunk(me.q)]
         return remote(place, place, xs.at[k, s, j], xr.at[k, s, j], me.chip(j))
 
     def relay(k, s, j):
-        start = (me.c * CHIPS + me.other(j)) * ch + j * (ch // 2)
-        place = w.at[k, came(s), span(start, ch // 2)]
+        part = (0, ch // 2) if j == 0 else (ch // 2, None)
+        place = w.at[k, came(s), chunk(me.other(j), *part)]
+        return remote(place, place, rs.at[k, s, j], rr.at[k, s, j], me.chip(1 - j))
+
+    def relayed(k, s, j):
+        part = (0, ch // 2) if j == 0 else (ch // 2, None)
+        place = w.at[k, came(s), chunk(me.other(2), *part)]
         return remote(place, place, rs.at[k, s, j], rr.at[k, s, j], me.chip(1 - j))
 
     def scopy(k, s):
@@ -194,7 +215,8 @@
 
     def on_z(k, s):
         zrecv(k, s).wait_recv()
-        zpass(k, s, lambda c: c.start())
+        if k == QKVO:
+            zpass(s, lambda c: c.start())
         for j in range(2):
             xcopy(k, s, j).start()
 
@@ -205,7 +227,7 @@
 
     def on_relay(k, s):
         for j in range(2):
-            relay(k, s, j).wait_recv()
+            relayed(k, s, j).wait_recv()
         scopy(k, s).start()
 
     def slot(k):
@@ -241,6 +263,10 @@
     def r4(k, j):
         place = fout.at[k, mine]
         return remote(place, place, r4s.at[k, j], r4r.at[k, j], me.chip(j))
+
+    def r4b(k, j, q):
+        place = fout.at[k, span((me.c * CHIPS + q) * ch + j * (ch // 2), ch // 2)]
+        return remote(place, place, r6s.at[k, j], r6r.at[k, j], me.chip(1 - j))
 
     def r5(k):
         place = fout.at[k, my_half]
@@ -288,12 +314,17 @@
         for s in range(far):
             r3(k, s).wait_send()
         fout[k, mine] = total.astype(BF16)
-        for j in range(3):
+        for j in range(2):
             r4(k, j).start()
 
     def on_r4(k):
-        for j in range(3):
+        for j in range(2):
             r4(k, j).wait_recv()
+            r4b(k, j, me.other(j)).start()
+
+    def on_r4b(k):
+        for j in range(2):
+            r4b(k, j, me.other(2)).wait_recv()
         r5(k).start()
 
     def pair_sum(n):
@@ -443,6 +474,7 @@
             copy.start()
     dy_in = pltpu.make_async_copy(dy, work, ls.at[6])
     dy_in.start()
+    all_here = me.greet()
     own = vecs[7:8, :]
     mid, end = own[:, 128:256], own[:, 256:384]
     turned = jnp.where(low_lanes, pltpu.roll(mid, HEAD_DIM, 1), pltpu.roll(end, HEAD_DIM, 1))
@@ -452,13 +484,6 @@
     bloc[1:2, 256:384] = turned
     bloc[1:2, 384:512] = jnp.where(low_lanes, mid, end)
     near[me.t] = bloc[...]
-    me.greet()
-    for s in range(far):
-        bcopy(s).start()
-    for k in range(3):
-        for copy in local(k):
-            copy.wait()
-        zends(k, lambda c: c.start())
     lane = lax.broadcasted_iota(jnp.int32, (1, 640), 1)
     is_query = (lane < 128) | ((lane >= 384) & (lane < 448))
     scales = jnp.where(is_query, 1.0 / math.sqrt(HEAD_DIM), 1.0)
@@ -469,17 +494,27 @@
         lo, hi = band(i)
         r = slice(i * LANES, (i + 1) * LANES)
         bias[r, 0 : hi - lo] = (tn(memb[:, r], memb[:, lo:hi]) - 1.0) * 1000000000.0
+    for copy in local(QKVO):
+        copy.wait()
+    all_here()
+    zends(lambda c: c.start())
+    for s in range(far):
+        bcopy(s).start()
+    for k in (UP, DOWN):
+        for copy in local(k):
+            copy.wait()
     project(me.t)
     on_z(QKVO, 0)
+    on_z(QKVO, 1)
     attend(me.t, (0, 1))
-    on_z(QKVO, 1)
+    on_z(QKVO, 2)
+    zstart(UP)
+    attend(me.t, (2, 3))
     on_xy(QKVO, 0)
-    attend(me.t, (2, 3))
-    on_z(QKVO, 2)
+    for s in range(far):
+        bcopy(s).wait_recv()
     on_xy(QKVO, 1)
     on_relay(QKVO, 0)
-    for s in range(far):
-        bcopy(s).wait_recv()
     on_xy(QKVO, 2)
 
     @pl.loop(0, far)
@@ -494,6 +529,10 @@
 
         attend(tt)
         on_z(UP, s)
+
+        @pl.when(s == 1)
+        def _():
+            zstart(DOWN)
 
         @pl.when(s > 0)
         def _():
@@ -759,6 +798,7 @@
     on_pair(1)
     on_r4(0)
     on_r2(2, 0)
+    on_r4b(0)
     on_r2(2, 1)
     on_r2(2, 2)
     on_plane(1)
@@ -781,15 +821,21 @@
     on_r3(2)
     on_r4(1)
     on_r4(2)
+    on_r4b(1)
+    on_r4b(2)
     for k in range(3):
         r5(k).wait_recv()
 
     for s in range(far):
         bcopy(s).wait_send()
     for k in range(3):
-        zends(k, lambda c: c.wait_send())
+        if k == QKVO:
+            zends(lambda c: c.wait_send())
         for s in range(far):
-            zpass(k, s, lambda c: c.wait_send())
+            if k == QKVO:
+                zpass(s, lambda c: c.wait_send())
+            else:
+                zfar(k, s).wait_send()
             scopy(k, s).wait_send()
             for j in range(2):
                 xcopy(k, s, j).wait_send()
@@ -800,8 +846,9 @@
                 for h in range(2):
                     for j in range(3):
                         r2(k, s, h, j).wait_send()
-        for j in range(3):
+        for j in range(2):
             r4(k, j).wait_send()
+            r4b(k, j, me.other(j)).wait_send()
         r5(k).wait_send()
 
 
@@ -862,8 +909,9 @@
             *pair(groups, n_t),
             *pair(groups, n_t, 2, 3),
             *pair(groups, far),
-            *pair(groups, 3),
+            *pair(groups, 2),
             *pair(groups),
+            *pair(groups, 2),
             *pair(2, 4 + far),
         ],
         compiler_params=pltpu.CompilerParams(

time: 179 us -> 175 us (0.978)
  Pallas kernels: 164 us -> 160 us
    pallas_call x1, Pallas kernels: 164 us -> 160 us  [run_layer(): pl.pallas_call(functools.partial(layer_kernel, n_t), out_shape=(shape((le...]
where the time goes in v5:
time: 175 us; the launch traced here: 174 us
  Pallas kernels  160 us (91%)
  local copies, waits for them, and re-layouts  8.62 us (5%)
  other arithmetic  4.62 us (3%)
    pallas_call x1, Pallas kernels, run_layer(): pl.pallas_call(functools.partial(layer_kernel, n_t), out_shape=(shape((le...  160 us
    convert_element_type x1, other arithmetic, per_device(): fout[0].astype(F32)  4.62 us

profile of v5, /device:TPU:0, one launch (start us, length us, event | category | flops | bytes accessed | tf_op | source)
XLA Modules:
  0.0 174.4 jit_solution(9725762900346219502)
XLA Ops:
  0.7 0.9 concatenate.3
  1.6 0.6 reshape.48.vecs
  2.2 160.5 %shard_map.313 = (bf16[512,768]{1,0:T(8,128)(2,1)}, f32[8,768]{1,0:T(8,128)}, f32[512,768]{1,0:T(8,128)}, bf16[3,768,768]{2,1,0:T(8,128)(2,1)}, f32[16,768]{1,0:T(8,128)}) custom-call(bf16[192,768]{1,0:T(8,128)(2,1)} %bitcast.40, bf16[192,768]{1,0:T(8,128)(2,1)} %bitcast.41, bf16[192,768]{1,0:T(8,128)(2,1)} %bitcast.42, bf16[192,768]{1,0:T(8,128)(2,1)} %wo.1, ...), custom_call_target="tpu_custom_call" | custom-call | tf_op jit(solution)/shard_map/pallas_call | solution.py:863
  162.6 1.3 slice_reduce_fusion
  164.0 1.6 fusion
  165.6 4.6 %bitcast_convert_fusion = (f32[768,768]{1,0:T(8,128)}, f32[768,768]{1,0:T(8,128)}, f32[1,768,768]{2,1,0:T(8,128)S(1)}) fusion(bf16[3,768,768]{2,1,0:T(8,128)(2,1)} %get-tuple-element.26), kind=kLoop, calls=%fused_computation | loop fusion | flops 1769472 | bytes 10616832 | tf_op jit(solution)/shard_map/convert_element_type | solution.py:960
  170.2 0.0 copy-start.1
  170.2 0.0 copy-start.2
  170.2 0.0 copy-start
  170.2 1.4 slice_bitcast_fusion
  171.6 0.1 copy-done.1
  171.8 0.9 copy.39
  172.6 0.0 copy-done.2
  172.6 0.6 copy.40
  173.2 0.0 copy-done
  173.2 1.1 copy.41
  (1 shorter events, 0.0 us)
Async XLA Ops:
  170.2 1.6 copy-start.1
  170.2 2.4 %copy-start.2 = (f32[8,768]{1,0:T(8,128)S(1)}, f32[8,768]{1,0:T(8,128)}, u32[]{:S(2)}) copy-start(f32[8,768]{1,0:T(8,128)} %get-tuple-element.24) | copy-start | bytes 73732
  170.2 3.0 %copy-start = (f32[512,768]{1,0:T(8,128)S(1)}, f32[512,768]{1,0:T(8,128)}, u32[]{:S(2)}) copy-start(f32[512,768]{1,0:T(8,128)} %get-tuple-element.25) | copy-start | bytes 4718596

commit v6 on v5

--- a/solution.py
+++ b/solution.py
@@ -19,6 +19,8 @@
 F32 = jnp.float32
 BF16 = jnp.bfloat16
 QKVO, UP, DOWN = 0, 1, 2
+PARTS = ((0, 48), (48, 80))
+PLANE_ROWS, Z_ROWS = 80, 16
 ERFC_STEP = 0.43
 ERFC_POLY = (
     0.24251981500369507,
@@ -112,10 +114,10 @@
     n_t,
     wq, wk, wv, wo, wup, wdown, x, dy, seg, vecs,
     layer_out, pooled, acc, fout, vout,
-    w, g, a, b, d, qkv, ctx, dctx, prob, act, dg, h1, dlow, work, tr, dsc, n1, near, bloc, bias,
+    w, g, a, b, d, e, hz, bz, qkv, ctx, dctx, prob, act, dg, h1, dlow, work, tr, dsc, n1, near, bloc, bias,
     memb, rstd, sums, vsum, va, vb, vd,
     ls, zs, zr, xs, xr, rs, rr, ss, sr, cs, cr,
-    r1s, r1r, r2s, r2r, r3s, r3r, r4s, r4r, r5s, r5r, r6s, r6r, vs, vr,
+    r1s, r1r, r2s, r2r, r3s, r3r, r4s, r4r, r5s, r5r, r6s, r6r, rzs, rzr, zps, zpr, vs, vr,
 ):
     me = Place(n_t)
     length, width = x.shape
@@ -243,30 +245,60 @@
         )
 
     def quarter(q):
-        return span(me.c * half + q * ch, ch)
-
-    cut = ch // 2
+        return rows_at(me.c * half + q * PLANE_ROWS, PLANE_ROWS)
 
     def sub(q, h):
-        return span(me.c * half + q * ch + h * cut, cut)
+        lo, hi = PARTS[h]
+        return rows_at(me.c * half + q * PLANE_ROWS + lo, hi - lo)
+
+    def axis(k, h):
+        return (h + k) % 2
 
     def r2(k, s, h, j):
-        source = (me.other(h), me.other(2), me.other(1 - h))[j]
+        ax, (lo, hi) = axis(k, h), PARTS[h]
+        source = (me.other(ax), me.other(2), me.other(1 - ax))[j]
         return remote(
-            g.at[slot(k), s, sub(source, h)], b.at[k, s, j, span(h * cut, cut)],
-            r2s.at[k, s, h, j], r2r.at[k, s, h, j], me.chip(1 - h if j == 2 else h),
+            g.at[slot(k), s, sub(source, h)], b.at[k, s, j, pl.ds(lo, hi - lo)],
+            r2s.at[k, s, h, j], r2r.at[k, s, h, j], me.chip(1 - ax if j == 2 else ax),
         )
 
     def r3(k, s):
         return remote(b.at[k, s, 0], d.at[k, s], r3s.at[k, s], r3r.at[k, s], me.z(s + 1))
 
-    def r4(k, j):
-        place = fout.at[k, mine]
-        return remote(place, place, r4s.at[k, j], r4r.at[k, j], me.chip(j))
+    zfirst = rows_at(me.c * half + CHIPS * PLANE_ROWS, CHIPS * Z_ROWS)
+
+    def rz(k, s):
+        return remote(
+            g.at[slot(k), s, zfirst], e.at[k, s], rzs.at[k, s], rzr.at[k, s], me.z(s + 1)
+        )
+
+    def piece(q):
+        return rows_at(q * Z_ROWS, Z_ROWS)
+
+    def r2z(k, j):
+        ax = axis(k, 1)
+        source = (me.other(ax), me.other(2), me.other(1 - ax))[j]
+        return remote(
+            hz.at[k, piece(source)], bz.at[k, j], zps.at[k, j], zpr.at[k, j],
+            me.chip(1 - ax if j == 2 else ax),
+        )
+
+    def final_rows(q, i, lo=0, hi=PLANE_ROWS):
+        if i == 0:
+            return rows_at(me.c * half + q * PLANE_ROWS + lo, hi - lo)
+        return rows_at(me.c * half + CHIPS * PLANE_ROWS + q * Z_ROWS, Z_ROWS)
+
+    def r4(k, j, i):
+        place = fout.at[k, final_rows(me.q, i)]
+        return remote(place, place, r4s.at[k, j, i], r4r.at[k, j, i], me.chip(j))
 
     def r4b(k, j, q):
-        place = fout.at[k, span((me.c * CHIPS + q) * ch + j * (ch // 2), ch // 2)]
+        place = fout.at[k, final_rows(q, 0, *PARTS[j])]
         return remote(place, place, r6s.at[k, j], r6r.at[k, j], me.chip(1 - j))
+
+    def r4c(k, q):
+        place = fout.at[k, final_rows(q, 1)]
+        return remote(place, place, r6s.at[k, 2], r6r.at[k, 2], me.chip(1))
 
     def r5(k):
         place = fout.at[k, my_half]
@@ -283,27 +315,23 @@
         for h in range(2):
             for j in range(2):
                 r2(k, s, h, j).start()
+        if not isinstance(s, int) or s < far:
+            rz(k, s).start()
 
     def on_r2(k, s):
-        for h in range(2):
-            rows_h = span(h * cut, cut)
+        for h, (lo, hi) in enumerate(PARTS):
+            got = slice(lo, hi)
             r2(k, s, h, 1).wait_recv()
-            g[slot(k), s, sub(me.other(1 - h), h)] += b[k, s, 1, rows_h]
+            g[slot(k), s, sub(me.other(1 - axis(k, h)), h)] += b[k, s, 1, got]
             r2(k, s, h, 2).start()
             r2(k, s, h, 0).wait_recv()
-            g[slot(k), s, sub(me.q, h)] += b[k, s, 0, rows_h]
+            g[slot(k), s, sub(me.q, h)] += b[k, s, 0, got]
 
     def on_r2b(k, s, last):
         for h in range(2):
             r2(k, s, h, 2).wait_recv()
         b[k, s, 0] = g[slot(k), s, quarter(me.q)] + b[k, s, 2]
-        if last is None:
-
-            @pl.when(s < far)
-            def _():
-                r3(k, s).start()
-
-        elif not last:
+        if not last:
             r3(k, s).start()
 
     def on_r3(k):
@@ -313,18 +341,44 @@
             total = total + d[k, s].astype(F32)
         for s in range(far):
             r3(k, s).wait_send()
-        fout[k, mine] = total.astype(BF16)
+        fout[k, final_rows(me.q, 0)] = total.astype(BF16)
         for j in range(2):
-            r4(k, j).start()
+            r4(k, j, 0).start()
+
+    def on_rz(k):
+        total = g[slot(k), far, zfirst].astype(F32)
+        for s in range(far):
+            rz(k, s).wait_recv()
+            total = total + e[k, s].astype(F32)
+        hz[k] = total.astype(BF16)
+        for j in range(2):
+            r2z(k, j).start()
+
+    def on_r2z(k):
+        r2z(k, 1).wait_recv()
+        hz[k, piece(me.other(1 - axis(k, 1)))] += bz[k, 1]
+        r2z(k, 2).start()
+        r2z(k, 0).wait_recv()
+        hz[k, piece(me.q)] += bz[k, 0]
+
+    def on_r2zb(k):
+        r2z(k, 2).wait_recv()
+        fout[k, final_rows(me.q, 1)] = hz[k, piece(me.q)] + bz[k, 2]
+        for j in range(2):
+            r4(k, j, 1).start()
 
     def on_r4(k):
         for j in range(2):
-            r4(k, j).wait_recv()
+            r4(k, j, 0).wait_recv()
             r4b(k, j, me.other(j)).start()
+        for j in range(2):
+            r4(k, j, 1).wait_recv()
+        r4c(k, me.other(0)).start()
 
     def on_r4b(k):
         for j in range(2):
             r4b(k, j, me.other(2)).wait_recv()
+        r4c(k, me.other(2)).wait_recv()
         r5(k).start()
 
     def pair_sum(n):
@@ -712,6 +766,7 @@
         add_sum(5, dh)
 
     on_r2b(0, 0, False)
+    on_rz(0)
     on_r2b(0, 1, False)
     vsum[0] = jnp.zeros((8, width), F32)
     for k, row in ((3, 0), (4, 1), (5, 2), (0, 3), (1, 4), (2, 5)):
@@ -742,11 +797,14 @@
         @pl.when(s == 1)
         def _():
             on_r2b(0, 3, True)
+            on_rz(1)
+            on_r2z(0)
             on_r2(1, 2)
             on_r2(1, 3)
 
         @pl.when(s == 2)
         def _():
+            on_r2zb(0)
             on_r3(0)
             on_plane(0)
             on_r2b(1, 0, False)
@@ -754,12 +812,18 @@
         @pl.when(s == 3)
         def _():
             on_r2b(1, 1, False)
+            on_r2z(1)
             on_r2b(1, 2, False)
+            on_r2(2, 0)
 
         r1(0, s).wait_send()
         for h in range(2):
             for j in range(3):
                 r2(0, s, h, j).wait_send()
+
+        @pl.when(s < far)
+        def _():
+            rz(0, s).wait_send()
 
         for m in range(rows // TILE):
             r = slice(m * TILE, (m + 1) * TILE)
@@ -794,22 +858,30 @@
 
     pair_sum(1).start()
     on_r1(2, far)
+    on_r2(2, 1)
     on_r2b(1, far, True)
     on_pair(1)
+    on_r2(2, 2)
     on_r4(0)
-    on_r2(2, 0)
-    on_r4b(0)
-    on_r2(2, 1)
-    on_r2(2, 2)
-    on_plane(1)
     on_r2b(2, 0, False)
     on_r2(2, far)
+    on_r2b(2, 1, False)
+    on_r2b(2, 2, False)
+    on_rz(2)
+    on_plane(1)
+    on_r2zb(1)
     on_r3(1)
     turns = lax.rem(width - me.t * (width // n_t), width)
     vout[0:8, :] = pltpu.roll(on_line(0), turns, 1)
     vout[8:16, :] = jnp.zeros((8, width), F32)
-    on_r2b(2, 1, False)
-    on_r2b(2, 2, False)
+    on_r2b(2, far, True)
+    on_r2z(2)
+    on_r4b(0)
+    on_r3(2)
+    on_r2zb(2)
+    on_r4(1)
+    on_r4(2)
+    on_r4b(1)
     vsum[1] = on_line(1)
     mine_row = vsum[1, pl.ds(4 + me.t, 1), :]
     vout[6:7, 0:128] = mine_row[:, 0:128]
@@ -817,11 +889,6 @@
     vout[7:8, 0:128] = mine_row[:, 256:384]
     vout[7:8, 128:256] = pltpu.roll(mine_row[:, 384:512], HEAD_DIM, 1)
     vout[8:9, :] = vsum[1, pl.ds(me.t, 1), :]
-    on_r2b(2, far, True)
-    on_r3(2)
-    on_r4(1)
-    on_r4(2)
-    on_r4b(1)
     on_r4b(2)
     for k in range(3):
         r5(k).wait_recv()
@@ -847,8 +914,15 @@
                     for j in range(3):
                         r2(k, s, h, j).wait_send()
         for j in range(2):
-            r4(k, j).wait_send()
+            r4(k, j, 0).wait_send()
+            r4(k, j, 1).wait_send()
             r4b(k, j, me.other(j)).wait_send()
+        r4c(k, me.other(0)).wait_send()
+        for j in range(3):
+            r2z(k, j).wait_send()
+        if k > 0:
+            for s in range(far):
+                rz(k, s).wait_send()
         r5(k).wait_send()
 
 
@@ -875,8 +949,11 @@
             vmem((groups, n_t, rows, cols), BF16),
             vmem((2, n_t, rows, cols), BF16),
             vmem((2, n_t, half, cols), BF16),
-            vmem((groups, n_t, 3, ch, cols), BF16),
-            vmem((groups, far, ch, cols), BF16),
+            vmem((groups, n_t, 3, PLANE_ROWS, cols), BF16),
+            vmem((groups, far, PLANE_ROWS, cols), BF16),
+            vmem((groups, far, CHIPS * Z_ROWS, cols), BF16),
+            vmem((groups, CHIPS * Z_ROWS, cols), BF16),
+            vmem((groups, 3, Z_ROWS, cols), BF16),
             vmem((n_t, length, 640), BF16),
             vmem((n_t, length, 256), BF16),
             vmem((length, 256), BF16),
@@ -909,9 +986,11 @@
             *pair(groups, n_t),
             *pair(groups, n_t, 2, 3),
             *pair(groups, far),
-            *pair(groups, 2),
+            *pair(groups, 2, 2),
             *pair(groups),
-            *pair(groups, 2),
+            *pair(groups, 3),
+            *pair(groups, far),
+            *pair(groups, 3),
             *pair(2, 4 + far),
         ],
         compiler_params=pltpu.CompilerParams(

time: 175 us -> 172 us (0.983)
  Pallas kernels: 160 us -> 157 us
    pallas_call x1, Pallas kernels: 160 us -> 157 us  [run_layer(): pl.pallas_call(functools.partial(layer_kernel, n_t), out_shape=(shape((le...]
where the time goes in v6:
time: 172 us; the launch traced here: 171 us
  Pallas kernels  157 us (91%)
  local copies, waits for them, and re-layouts  8.62 us (5%)
  other arithmetic  4.62 us (3%)
    pallas_call x1, Pallas kernels, run_layer(): pl.pallas_call(functools.partial(layer_kernel, n_t), out_shape=(shape((le...  157 us
    convert_element_type x1, other arithmetic, per_device(): fout[0].astype(F32)  4.62 us

profile of v6, /device:TPU:0, one launch (start us, length us, event | category | flops | bytes accessed | tf_op | source)
XLA Modules:
  0.0 170.9 jit_solution(2589956570398470146)
XLA Ops:
  0.7 0.9 concatenate.3
  1.6 0.6 reshape.48.vecs
  2.2 157.0 %shard_map.313 = (bf16[512,768]{1,0:T(8,128)(2,1)}, f32[8,768]{1,0:T(8,128)}, f32[512,768]{1,0:T(8,128)}, bf16[3,768,768]{2,1,0:T(8,128)(2,1)}, f32[16,768]{1,0:T(8,128)}) custom-call(bf16[192,768]{1,0:T(8,128)(2,1)} %bitcast.40, bf16[192,768]{1,0:T(8,128)(2,1)} %bitcast.41, bf16[192,768]{1,0:T(8,128)(2,1)} %bitcast.42, bf16[192,768]{1,0:T(8,128)(2,1)} %wo.1, ...), custom_call_target="tpu_custom_call" | custom-call | tf_op jit(solution)/shard_map/pallas_call | solution.py:937
  159.2 1.3 slice_reduce_fusion
  160.5 1.6 fusion
  162.1 4.6 %bitcast_convert_fusion = (f32[768,768]{1,0:T(8,128)}, f32[768,768]{1,0:T(8,128)}, f32[1,768,768]{2,1,0:T(8,128)S(1)}) fusion(bf16[3,768,768]{2,1,0:T(8,128)(2,1)} %get-tuple-element.26), kind=kLoop, calls=%fused_computation | loop fusion | flops 1769472 | bytes 10616832 | tf_op jit(solution)/shard_map/convert_element_type | solution.py:1039
  166.7 0.0 copy-start.1
  166.7 0.0 copy-start.2
  166.7 0.0 copy-start
  166.7 1.4 slice_bitcast_fusion
  168.2 0.1 copy-done.1
  168.3 0.9 copy.39
  169.2 0.0 copy-done.2
  169.2 0.6 copy.40
  169.8 0.0 copy-done
  169.8 1.1 copy.41
  (1 shorter events, 0.0 us)
Async XLA Ops:
  166.7 1.6 copy-start.1
  166.7 2.4 %copy-start.2 = (f32[8,768]{1,0:T(8,128)S(1)}, f32[8,768]{1,0:T(8,128)}, u32[]{:S(2)}) copy-start(f32[8,768]{1,0:T(8,128)} %get-tuple-element.24) | copy-start | bytes 73732
  166.7 3.0 %copy-start = (f32[512,768]{1,0:T(8,128)S(1)}, f32[512,768]{1,0:T(8,128)}, u32[]{:S(2)}) copy-start(f32[512,768]{1,0:T(8,128)} %get-tuple-element.25) | copy-start | bytes 4718596
